TPU v7x, 256 devices: a whole 4x4x8 slice. The times are simulated.
256 devices in a mesh: gx: 8 (over z), gy: 8 (over x, core), gz: 4 (over y).
Axes of the slice: x: 4, y: 4, z: 8, core: 2. Of those that a mesh axis runs over, the one named last changes fastest.
Arguments:
- displacement: float32 [3, 64, 128, 512], P(None, 'gx', 'gy', 'gz'), may hold values from -100 to 100
- density: float32 [64, 128, 512], P('gx', 'gy', 'gz'), may hold values from 0.1 to 1
Outputs:
- aggregate: float32 [], replicated
- adjoint: float32 [3, 64, 128, 512], P(None, 'gx', 'gy', 'gz')
- sensitivity: float32 [64, 128, 512], P('gx', 'gy', 'gz')
All inputs are finite; a program needn't handle non-finite values.
Results may differ from a plain program's by a relative error of at most 0.0003.
Values sent between devices are 32-bit elements; how exact they have to be, the bound alone decides.
No kernel may reach another device: no remote copies, remote signals or barrier semaphores. Data moves between devices by JAX's collectives and lax.ppermute only.
A program may use at most 64 MiB of HBM per device.

v0:
```python
import functools
import math

import jax
import jax.numpy as jnp
from jax import lax
from jax.sharding import Mesh
from jax.sharding import PartitionSpec as P

ITERS = 6
GY = ("gy_0", "gy_1")
GX_GY_GZ = ("gx", "gy_0", "gy_1", "gz")


lame_first = 0.3 / (1.3 * 0.4)
shear_modulus = 1.0 / 2.6
power_scale = 3.0
damping = 0.6
shift_term = 0.1
diag_factor = (lame_first + 3.0 * shear_modulus) / 16.0
CORNERS = [(first, second, third) for first in (0, 1) for second in (0, 1) for third in (0, 1)]
OFFSETS = [
    ((first, second, third), 2.5 - math.sqrt(first * first + second * second + third * third))
    for first in range(-2, 3)
    for second in range(-2, 3)
    for third in range(-2, 3)
    if first * first + second * second + third * third <= 4
]


def passed_along(block, axis, distance):
    devices = range(lax.axis_size(axis))
    route = [(i - distance, i) for i in devices if i - distance in devices]
    return lax.ppermute(block, axis, route)


def extended(array, sides, width):
    for axis, dim in sides:
        count, length = (lax.axis_size(axis), array.shape[dim])
        up = [(i, (i + 1) % count) for i in range(count - 1)]
        down = [(j, i) for i, j in up]
        last = lax.slice_in_dim(array, length - width, length, axis=dim)
        leading = lax.slice_in_dim(array, 0, width, axis=dim)
        before = lax.ppermute(last, axis, up)
        after = lax.ppermute(leading, axis, down)
        array = jnp.concatenate([before, array, after], axis=dim)
    return array


def over_axes(array, axes):
    return functools.reduce(lax.pmax, axes, array)


def over_axes_2(array, axes):
    return functools.reduce(lax.psum, axes, array)


def window(array, anchor, extent):
    return array[
        :,
        anchor[0] : anchor[0] + extent[0],
        anchor[1] : anchor[1] + extent[1],
        anchor[2] : anchor[2] + extent[2],
    ]


def window_cells(array, anchor, extent):
    return array[
        anchor[0] : anchor[0] + extent[0],
        anchor[1] : anchor[1] + extent[1],
        anchor[2] : anchor[2] + extent[2],
    ]


def gradients(padded, offset, extent):
    totals = [0.0, 0.0, 0.0]
    for corner in CORNERS:
        piece = window(padded, (offset + corner[0], offset + corner[1], offset + corner[2]), extent)
        for direction in range(3):
            totals[direction] = totals[direction] + (2 * corner[direction] - 1) * piece
    return 0.25 * jnp.concatenate(totals, axis=0)


def strains(grad_all):
    return [
        grad_all[0],
        grad_all[4],
        grad_all[8],
        grad_all[3] + grad_all[1],
        grad_all[7] + grad_all[5],
        grad_all[2] + grad_all[6],
    ]


def stiffen(values):
    trace = values[0] + values[1] + values[2]
    return [
        lame_first * trace + 2.0 * shear_modulus * values[0],
        lame_first * trace + 2.0 * shear_modulus * values[1],
        lame_first * trace + 2.0 * shear_modulus * values[2],
        shear_modulus * values[3],
        shear_modulus * values[4],
        shear_modulus * values[5],
    ]


def spread(terms):
    return jnp.stack(
        [terms[0], terms[3], terms[5], terms[3], terms[1], terms[4], terms[5], terms[4], terms[2]],
        axis=0,
    )


def assemble(padded, extent):
    result = 0.0
    for corner in CORNERS:
        anchor = (1 - corner[0], 1 - corner[1], 1 - corner[2])
        for direction in range(3):
            piece = window(padded[3 * direction : 3 * direction + 3], anchor, extent)
            result = result + 0.25 * (2 * corner[direction] - 1) * piece
    return result


def mises(sigma):
    return (
        sigma[0] * sigma[0]
        + sigma[1] * sigma[1]
        + sigma[2] * sigma[2]
        - sigma[0] * sigma[1]
        - sigma[1] * sigma[2]
        - sigma[2] * sigma[0]
        + 3.0 * (sigma[3] * sigma[3] + sigma[4] * sigma[4] + sigma[5] * sigma[5])
    )


def mises_slope(sigma):
    return [
        2.0 * sigma[0] - sigma[1] - sigma[2],
        2.0 * sigma[1] - sigma[2] - sigma[0],
        2.0 * sigma[2] - sigma[0] - sigma[1],
        6.0 * sigma[3],
        6.0 * sigma[4],
        6.0 * sigma[5],
    ]


def nodes_above(field):
    received = passed_along(field[:, :1], "gx", -1)
    field = jnp.concatenate([field, received], axis=1)
    received = passed_along(field[:, :, :1], GY, -1)
    field = jnp.concatenate([field, received], axis=2)
    received = passed_along(field[:, :, :, :1], "gz", -1)
    return jnp.concatenate([field, received], axis=3)


def terms_below(terms):
    received = passed_along(terms[:, -1:], "gx", 1)
    terms = jnp.concatenate([received, terms], axis=1)
    received = passed_along(terms[:, :, -1:], GY, 1)
    terms = jnp.concatenate([received, terms], axis=2)
    received = passed_along(terms[:, :, :, -1:], "gz", 1)
    return jnp.concatenate([received, terms], axis=3)


def dens_below(values):
    received = passed_along(values[-1:], "gx", 1)
    values = jnp.concatenate([received, values], axis=0)
    received = passed_along(values[:, -1:], GY, 1)
    values = jnp.concatenate([received, values], axis=1)
    received = passed_along(values[:, :, -1:], "gz", 1)
    return jnp.concatenate([received, values], axis=2)


def node_rim_deep(field):
    return extended(field, (("gx", 1), (GY, 2), ("gz", 3)), 1)


def inside_line(position, count, length, lower, upper):
    cell_index = position * length + jnp.arange(-lower, length + upper, dtype=jnp.int32)
    limit = count * length
    return ((cell_index >= 0) & (cell_index < limit)).astype(jnp.float32)


def inside_block(extent, lower, upper):
    counts = (lax.axis_size("gx"), lax.axis_size(GY), lax.axis_size("gz"))
    first = inside_line(lax.axis_index("gx"), counts[0], extent[0], lower, upper)
    second = inside_line(lax.axis_index(GY), counts[1], extent[1], lower, upper)
    third = inside_line(lax.axis_index("gz"), counts[2], extent[2], lower, upper)
    return first[:, None, None] * second[None, :, None] * third[None, None, :]


def on_device(displacement, density):
    extent = density.shape
    widened = (extent[0] + 1, extent[1] + 1, extent[2] + 1)
    elements = (
        extent[0]
        * extent[1]
        * extent[2]
        * lax.axis_size("gx")
        * lax.axis_size(GY)
        * lax.axis_size("gz")
    )
    inside_low = inside_block(extent, 1, 0)
    inside = inside_block(extent, 2, 2)
    lowered = dens_below(density)
    stiff_low = (0.01 + 0.99 * lowered**3) * inside_low
    base = stiffen(strains(gradients(nodes_above(displacement), 0, extent)))
    rooted = jnp.sqrt(density)
    sigma = [rooted * value for value in base]
    stress = jnp.sqrt(mises(sigma) + 1.0)
    score = power_scale * stress
    local_top = jnp.max(score)
    top = over_axes(local_top, GX_GY_GZ)
    total = over_axes_2(jnp.sum(jnp.exp(score - top)), GX_GY_GZ)
    aggregate = (top + jnp.log(total)) / power_scale
    weight = jnp.exp(score - top) / total * float(elements)
    factor = weight / (2.0 * stress)
    slope = [factor * value for value in mises_slope(sigma)]
    load = assemble(terms_below(spread(stiffen([rooted * value for value in slope]))), extent)
    summed = 0.0
    for corner in CORNERS:
        summed = summed + window_cells(
            stiff_low, (1 - corner[0], 1 - corner[1], 1 - corner[2]), extent
        )
    diag = diag_factor * summed + shift_term

    def operate(field):
        values = stiffen(strains(gradients(node_rim_deep(field), 0, widened)))
        forces = assemble(spread([stiff_low * value for value in values]), extent)
        return forces + shift_term * field

    adjoint = damping * load / diag
    for sweep in range(1, ITERS):
        adjoint = adjoint + damping * (load - operate(adjoint)) / diag
    other = strains(gradients(nodes_above(adjoint), 0, extent))
    explicit = sum((slope[index] * base[index] for index in range(6))) / (2.0 * rooted)
    worked = sum((base[index] * other[index] for index in range(6)))
    raw = explicit - 2.97 * density * density * worked
    hsum = 0.0
    for offset, factor_w in OFFSETS:
        hsum = hsum + factor_w * window_cells(
            inside, (2 + offset[0], 2 + offset[1], 2 + offset[2]), extent
        )
    scaled = extended(raw / hsum, (("gx", 0), (GY, 1), ("gz", 2)), 2)
    sensitivity = 0.0
    for offset, factor_w in OFFSETS:
        sensitivity = sensitivity + factor_w * window_cells(
            scaled, (2 + offset[0], 2 + offset[1], 2 + offset[2]), extent
        )
    return (aggregate, adjoint, sensitivity)


def solution(mesh):
    finer = Mesh(
        mesh.devices.reshape(mesh.shape["gx"], 4, 2, mesh.shape["gz"]), ("gx", "gy_0", "gy_1", "gz")
    )
    placed = (P(None, "gx", GY, "gz"), P("gx", GY, "gz"))
    return jax.shard_map(
        on_device,
        mesh=finer,
        in_specs=placed,
        out_specs=(P(), P(None, "gx", GY, "gz"), P("gx", GY, "gz")),
        check_vma=False,
    )
```

profile of v0, /device:TPU:1, one launch (start us, length us, event | category | flops | bytes accessed | tf_op | source)
XLA Modules:
  0.0 381.7 jit_solution(1116717883717319299)
XLA Ops:
  3.4 5.0 %collective-permute-start.6 = (f32[1,16,128]{2,1,0:T(8,128)S(1)}, f32[1,16,128]{2,1,0:T(8,128)S(1)}, u32[]{:S(2)}, u32[]{:S(2)}) collective-permute-start(f32[1,16,128]{2,1,0:T(8,128)S(1)} %slice.1477), channel_id=1, source_target_pairs={{0,32},{32,64},{64,96},{96,128},{128,160},{160,192},{192,224},{1,3... | collective-permute-start | bytes 24584 | tf_op jit(solution)/shard_map/ppermute | solution.py:34
  9.4 4.7 %collective-permute-start.1 = (f32[3,9,1,128]{3,2,1,0:T(1,128)S(1)}, f32[3,9,1,128]{3,2,1,0:T(1,128)S(1)}, u32[]{:S(2)}, u32[]{:S(2)}) collective-permute-start(f32[3,9,1,128]{3,2,1,0:T(1,128)S(1)} %slice.1813), channel_id=1, source_target_pairs={{4,0},{8,4},{12,8},{16,12},{20,16},{24,20},{28,24},{5,1},{9,5},{13... | collective-permute-start | bytes 41480 | tf_op jit(solution)/shard_map/ppermute | solution.py:34
  16.3 9.6 %collective-permute-done.2 = f32[3,9,17,1]{3,2,1,0:T(8,128)S(1)} collective-permute-done((f32[3,9,17,1]{3,2,1,0:T(8,128)S(1)}, f32[3,9,17,1]{3,2,1,0:T(8,128)S(1)}, u32[]{:S(2)}, u32[]{:S(2)}) %collective-permute-start.2) | collective-permute-done | bytes 1868 | tf_op jit(solution)/shard_map/ppermute | solution.py:34
  27.5 15.4 %pmax.28 = f32[]{:T(128)} all-reduce(f32[]{:T(128)} %get-tuple-element.34), channel_id=1, replica_groups=mesh['gx'=8,'gy_0'=4,'gy_1'=2,'gz'=4] {'gx'}, use_global_device_ids=true, to_apply=%region_1.0 | all-reduce | flops 1 | bytes 8 | tf_op jit(solution)/shard_map/pmax | solution.py:51
  42.9 8.2 %pmax.29 = f32[]{:T(128)} all-reduce(f32[]{:T(128)} %pmax.28), channel_id=1, replica_groups=mesh['gx'=8,'gy_0'=4,'gy_1'=2,'gz'=4] {'gy_0'}, use_global_device_ids=true, to_apply=%region_2.0 | all-reduce | flops 1 | bytes 8 | tf_op jit(solution)/shard_map/pmax | solution.py:51
  51.1 9.1 %pmax.30 = f32[]{:T(128)} all-reduce(f32[]{:T(128)} %pmax.29), channel_id=1, replica_groups=mesh['gx'=8,'gy_0'=4,'gy_1'=2,'gz'=4] {'gy_1'}, use_global_device_ids=true, to_apply=%region_3.0 | all-reduce | flops 1 | bytes 8 | tf_op jit(solution)/shard_map/pmax | solution.py:51
  60.3 7.9 %pmax.31 = f32[]{:T(128)} all-reduce(f32[]{:T(128)} %pmax.30), channel_id=1, replica_groups=mesh['gx'=8,'gy_0'=4,'gy_1'=2,'gz'=4] {'gz'}, use_global_device_ids=true, to_apply=%region_4.0 | all-reduce | flops 1 | bytes 8 | tf_op jit(solution)/shard_map/pmax | solution.py:51
  69.5 12.0 %psum.28 = f32[]{:T(128)} all-reduce(f32[]{:T(128)} %fusion.291), channel_id=1, replica_groups=mesh['gx'=8,'gy_0'=4,'gy_1'=2,'gz'=4] {'gx'}, use_global_device_ids=true, to_apply=%region_6.0 | all-reduce | flops 1 | bytes 8 | tf_op jit(solution)/shard_map/psum | solution.py:55
  81.5 6.8 %psum.29 = f32[]{:T(128)} all-reduce(f32[]{:T(128)} %psum.28), channel_id=1, replica_groups=mesh['gx'=8,'gy_0'=4,'gy_1'=2,'gz'=4] {'gy_0'}, use_global_device_ids=true, to_apply=%region_7.0 | all-reduce | flops 1 | bytes 8 | tf_op jit(solution)/shard_map/psum | solution.py:55
  88.3 10.8 %psum.30 = f32[]{:T(128)} all-reduce(f32[]{:T(128)} %psum.29), channel_id=1, replica_groups=mesh['gx'=8,'gy_0'=4,'gy_1'=2,'gz'=4] {'gy_1'}, use_global_device_ids=true, to_apply=%region_8.0 | all-reduce | flops 1 | bytes 8 | tf_op jit(solution)/shard_map/psum | solution.py:55
  99.1 7.4 %psum.31 = f32[]{:T(128)} all-reduce(f32[]{:T(128)} %psum.30), channel_id=1, replica_groups=mesh['gx'=8,'gy_0'=4,'gy_1'=2,'gz'=4] {'gz'}, use_global_device_ids=true, to_apply=%region_9.0 | all-reduce | flops 1 | bytes 8 | tf_op jit(solution)/shard_map/psum | solution.py:55
  106.4 2.0 constant_dynamic-update-slice_fusion.10
  113.3 5.5 %collective-permute-start.7 = (f32[9,1,128]{2,1,0:T(1,128)S(1)}, f32[9,1,128]{2,1,0:T(1,128)S(1)}, u32[]{:S(2)}, u32[]{:S(2)}) collective-permute-start(f32[9,1,128]{2,1,0:T(1,128)S(1)} %slice.1852), channel_id=1, source_target_pairs={{0,4},{4,8},{8,12},{12,16},{16,20},{20,24},{24,28},{1,5},{5,9},{9,... | collective-permute-start | bytes 13832 | tf_op jit(solution)/shard_map/ppermute | solution.py:34
  119.5 2.6 collective-permute-start.3
  122.3 2.7 collective-permute-start.8
  125.1 2.5 collective-permute-start.4
  129.7 2.8 collective-permute-start.5
  138.3 4.0 %collective-permute-start.9 = (f32[3,1,16,128]{3,2,1,0:T(8,128)S(1)}, f32[3,1,16,128]{3,2,1,0:T(8,128)S(1)}, u32[]{:S(2)}, u32[]{:S(2)}) collective-permute-start(f32[3,1,16,128]{3,2,1,0:T(8,128)S(1)} %get-tuple-element.246), channel_id=1, source_target_pairs={{0,32},{32,64},{64,96},{96,128},{128,160},{160,192},{192,224},{1,3... | collective-permute-start | bytes 73736 | tf_op jit(solution)/shard_map/ppermute | solution.py:44
  143.3 4.8 %collective-permute-start.11 = (f32[3,10,1,128]{3,2,1,0:T(1,128)S(1)}, f32[3,10,1,128]{3,2,1,0:T(1,128)S(1)}, u32[]{:S(2)}, u32[]{:S(2)}) collective-permute-start(f32[3,10,1,128]{3,2,1,0:T(1,128)S(1)} %get-tuple-element.236), channel_id=1, source_target_pairs={{0,4},{4,8},{8,12},{12,16},{16,20},{20,24},{24,28},{1,5},{5,9},{9,... | collective-permute-start | bytes 46088 | tf_op jit(solution)/shard_map/ppermute | solution.py:44
  148.1 1.9 collective-permute-start.12
  150.0 3.1 collective-permute-done.12
  153.4 4.0 %collective-permute-start.13 = (f32[3,10,18,1]{3,2,1,0:T(8,128)S(1)}, f32[3,10,18,1]{3,2,1,0:T(8,128)S(1)}, u32[]{:S(2)}, u32[]{:S(2)}) collective-permute-start(f32[3,10,18,1]{3,2,1,0:T(8,128)S(1)} %get-tuple-element.216), channel_id=1, source_target_pairs={{0,1},{1,2},{2,3},{4,5},{5,6},{6,7},{8,9},{9,10},{10,11},{12,13},{... | collective-permute-start | bytes 6488 | tf_op jit(solution)/shard_map/ppermute | solution.py:44
  159.4 4.9 %collective-permute-done.13 = f32[3,10,18,1]{3,2,1,0:T(8,128)S(1)} collective-permute-done((f32[3,10,18,1]{3,2,1,0:T(8,128)S(1)}, f32[3,10,18,1]{3,2,1,0:T(8,128)S(1)}, u32[]{:S(2)}, u32[]{:S(2)}) %collective-permute-start.13) | collective-permute-done | bytes 2192 | tf_op jit(solution)/shard_map/ppermute | solution.py:44
  164.2 4.1 %collective-permute-done.14 = f32[3,10,18,1]{3,2,1,0:T(8,128)S(1)} collective-permute-done((f32[3,10,18,1]{3,2,1,0:T(8,128)S(1)}, f32[3,10,18,1]{3,2,1,0:T(8,128)S(1)}, u32[]{:S(2)}, u32[]{:S(2)}) %collective-permute-start.14) | collective-permute-done | bytes 2192 | tf_op jit(solution)/shard_map/ppermute | solution.py:45
  176.2 3.9 %collective-permute-start.15 = (f32[3,1,16,128]{3,2,1,0:T(8,128)S(1)}, f32[3,1,16,128]{3,2,1,0:T(8,128)S(1)}, u32[]{:S(2)}, u32[]{:S(2)}) collective-permute-start(f32[3,1,16,128]{3,2,1,0:T(8,128)S(1)} %get-tuple-element.244), channel_id=1, source_target_pairs={{0,32},{32,64},{64,96},{96,128},{128,160},{160,192},{192,224},{1,3... | collective-permute-start | bytes 73736 | tf_op jit(solution)/shard_map/ppermute | solution.py:44
  181.4 4.0 %collective-permute-done.16 = f32[3,1,16,128]{3,2,1,0:T(8,128)S(1)} collective-permute-done((f32[3,1,16,128]{3,2,1,0:T(8,128)S(1)}, f32[3,1,16,128]{3,2,1,0:T(8,128)S(1)}, u32[]{:S(2)}, u32[]{:S(2)}) %collective-permute-start.16) | collective-permute-done | bytes 24608 | tf_op jit(solution)/shard_map/ppermute | solution.py:45
  185.4 3.8 collective-permute-start.17
  189.2 1.9 collective-permute-start.18
  191.1 3.1 collective-permute-done.18
  194.4 2.3 collective-permute-start.19
  198.3 5.3 %collective-permute-done.19 = f32[3,10,18,1]{3,2,1,0:T(8,128)S(1)} collective-permute-done((f32[3,10,18,1]{3,2,1,0:T(8,128)S(1)}, f32[3,10,18,1]{3,2,1,0:T(8,128)S(1)}, u32[]{:S(2)}, u32[]{:S(2)}) %collective-permute-start.19) | collective-permute-done | bytes 2192 | tf_op jit(solution)/shard_map/ppermute | solution.py:44
  203.7 4.1 %collective-permute-done.20 = f32[3,10,18,1]{3,2,1,0:T(8,128)S(1)} collective-permute-done((f32[3,10,18,1]{3,2,1,0:T(8,128)S(1)}, f32[3,10,18,1]{3,2,1,0:T(8,128)S(1)}, u32[]{:S(2)}, u32[]{:S(2)}) %collective-permute-start.20) | collective-permute-done | bytes 2192 | tf_op jit(solution)/shard_map/ppermute | solution.py:45
  215.3 2.8 collective-permute-start.21
  219.3 5.5 %collective-permute-done.22 = f32[3,1,16,128]{3,2,1,0:T(8,128)S(1)} collective-permute-done((f32[3,1,16,128]{3,2,1,0:T(8,128)S(1)}, f32[3,1,16,128]{3,2,1,0:T(8,128)S(1)}, u32[]{:S(2)}, u32[]{:S(2)}) %collective-permute-start.22) | collective-permute-done | bytes 24608 | tf_op jit(solution)/shard_map/ppermute | solution.py:45
  224.8 4.4 %collective-permute-start.23 = (f32[3,10,1,128]{3,2,1,0:T(1,128)S(1)}, f32[3,10,1,128]{3,2,1,0:T(1,128)S(1)}, u32[]{:S(2)}, u32[]{:S(2)}) collective-permute-start(f32[3,10,1,128]{3,2,1,0:T(1,128)S(1)} %get-tuple-element.232), channel_id=1, source_target_pairs={{0,4},{4,8},{8,12},{12,16},{16,20},{20,24},{24,28},{1,5},{5,9},{9,... | collective-permute-start | bytes 46088 | tf_op jit(solution)/shard_map/ppermute | solution.py:44
  229.3 1.9 collective-permute-start.24
  231.2 3.1 collective-permute-done.24
  234.6 2.5 collective-permute-start.25
  238.9 5.1 %collective-permute-done.25 = f32[3,10,18,1]{3,2,1,0:T(8,128)S(1)} collective-permute-done((f32[3,10,18,1]{3,2,1,0:T(8,128)S(1)}, f32[3,10,18,1]{3,2,1,0:T(8,128)S(1)}, u32[]{:S(2)}, u32[]{:S(2)}) %collective-permute-start.25) | collective-permute-done | bytes 2192 | tf_op jit(solution)/shard_map/ppermute | solution.py:44
  244.0 4.1 %collective-permute-done.26 = f32[3,10,18,1]{3,2,1,0:T(8,128)S(1)} collective-permute-done((f32[3,10,18,1]{3,2,1,0:T(8,128)S(1)}, f32[3,10,18,1]{3,2,1,0:T(8,128)S(1)}, u32[]{:S(2)}, u32[]{:S(2)}) %collective-permute-start.26) | collective-permute-done | bytes 2192 | tf_op jit(solution)/shard_map/ppermute | solution.py:45
  255.6 4.8 %collective-permute-start.27 = (f32[3,1,16,128]{3,2,1,0:T(8,128)S(1)}, f32[3,1,16,128]{3,2,1,0:T(8,128)S(1)}, u32[]{:S(2)}, u32[]{:S(2)}) collective-permute-start(f32[3,1,16,128]{3,2,1,0:T(8,128)S(1)} %get-tuple-element.240), channel_id=1, source_target_pairs={{0,32},{32,64},{64,96},{96,128},{128,160},{160,192},{192,224},{1,3... | collective-permute-start | bytes 73736 | tf_op jit(solution)/shard_map/ppermute | solution.py:44
  261.7 4.0 %collective-permute-done.28 = f32[3,1,16,128]{3,2,1,0:T(8,128)S(1)} collective-permute-done((f32[3,1,16,128]{3,2,1,0:T(8,128)S(1)}, f32[3,1,16,128]{3,2,1,0:T(8,128)S(1)}, u32[]{:S(2)}, u32[]{:S(2)}) %collective-permute-start.28) | collective-permute-done | bytes 24608 | tf_op jit(solution)/shard_map/ppermute | solution.py:45
  265.7 3.7 collective-permute-start.29
  269.4 1.9 collective-permute-start.30
  271.3 3.1 collective-permute-done.30
  278.1 5.4 %collective-permute-done.31 = f32[3,10,18,1]{3,2,1,0:T(8,128)S(1)} collective-permute-done((f32[3,10,18,1]{3,2,1,0:T(8,128)S(1)}, f32[3,10,18,1]{3,2,1,0:T(8,128)S(1)}, u32[]{:S(2)}, u32[]{:S(2)}) %collective-permute-start.31) | collective-permute-done | bytes 2192 | tf_op jit(solution)/shard_map/ppermute | solution.py:44
  283.5 4.1 %collective-permute-done.32 = f32[3,10,18,1]{3,2,1,0:T(8,128)S(1)} collective-permute-done((f32[3,10,18,1]{3,2,1,0:T(8,128)S(1)}, f32[3,10,18,1]{3,2,1,0:T(8,128)S(1)}, u32[]{:S(2)}, u32[]{:S(2)}) %collective-permute-start.32) | collective-permute-done | bytes 2192 | tf_op jit(solution)/shard_map/ppermute | solution.py:45
  295.1 3.6 collective-permute-start.33
  300.0 3.6 collective-permute-done.34
  303.7 2.6 collective-permute-start.35
  306.3 1.9 collective-permute-start.36
  308.2 3.1 collective-permute-done.36
  315.0 5.3 %collective-permute-done.37 = f32[3,10,18,1]{3,2,1,0:T(8,128)S(1)} collective-permute-done((f32[3,10,18,1]{3,2,1,0:T(8,128)S(1)}, f32[3,10,18,1]{3,2,1,0:T(8,128)S(1)}, u32[]{:S(2)}, u32[]{:S(2)}) %collective-permute-start.37) | collective-permute-done | bytes 2192 | tf_op jit(solution)/shard_map/ppermute | solution.py:44
  320.3 4.1 %collective-permute-done.38 = f32[3,10,18,1]{3,2,1,0:T(8,128)S(1)} collective-permute-done((f32[3,10,18,1]{3,2,1,0:T(8,128)S(1)}, f32[3,10,18,1]{3,2,1,0:T(8,128)S(1)}, u32[]{:S(2)}, u32[]{:S(2)}) %collective-permute-start.38) | collective-permute-done | bytes 2192 | tf_op jit(solution)/shard_map/ppermute | solution.py:45
  333.3 3.6 collective-permute-done.39
  336.9 2.3 collective-permute-start.40
  339.2 2.7 collective-permute-done.40
  343.4 8.9 %collective-permute-done.41 = f32[3,9,17,1]{3,2,1,0:T(8,128)S(1)} collective-permute-done((f32[3,9,17,1]{3,2,1,0:T(8,128)S(1)}, f32[3,9,17,1]{3,2,1,0:T(8,128)S(1)}, u32[]{:S(2)}, u32[]{:S(2)}) %collective-permute-start.41) | collective-permute-done | bytes 1868 | tf_op jit(solution)/shard_map/ppermute | solution.py:34
  353.3 1.9 fusion.221
  355.2 2.9 collective-permute-start.42
  359.4 3.2 collective-permute-done.43
  362.6 3.2 collective-permute-start.44
  365.8 1.9 collective-permute-start.45
  375.0 4.1 %collective-permute-done.47 = f32[12,20,2]{2,1,0:T(8,128)S(1)} collective-permute-done((f32[12,20,2]{2,1,0:T(8,128)S(1)}, f32[12,20,2]{2,1,0:T(8,128)S(1)}, u32[]{:S(2)}, u32[]{:S(2)}) %collective-permute-start.47) | collective-permute-done | bytes 1952 | tf_op jit(solution)/shard_map/ppermute | solution.py:45
  (237 shorter events, 91.1 us)
Async XLA Ops:
  0.6 25.3 %copy-start.3 = (f32[3,8,16,128]{3,2,1,0:T(8,128)S(1)}, f32[3,8,16,128]{3,2,1,0:T(8,128)}, u32[]{:S(2)}) copy-start(f32[3,8,16,128]{3,2,1,0:T(8,128)} %param.2) | copy-start | bytes 589828
  1.4 7.9 %collective-permute-start = (f32[3,1,16,128]{3,2,1,0:T(8,128)S(1)}, f32[3,1,16,128]{3,2,1,0:T(8,128)S(1)}, u32[]{:S(2)}, u32[]{:S(2)}) collective-permute-start(f32[3,1,16,128]{3,2,1,0:T(8,128)S(1)} %slice.1434), channel_id=1, source_target_pairs={{32,0},{64,32},{96,64},{128,96},{160,128},{192,160},{224,192},{33,... | collective-permute-start | bytes 73736 | tf_op jit(solution)/shard_map/ppermute | solution.py:34
  3.4 12.8 %collective-permute-start.6 = (f32[1,16,128]{2,1,0:T(8,128)S(1)}, f32[1,16,128]{2,1,0:T(8,128)S(1)}, u32[]{:S(2)}, u32[]{:S(2)}) collective-permute-start(f32[1,16,128]{2,1,0:T(8,128)S(1)} %slice.1477), channel_id=1, source_target_pairs={{0,32},{32,64},{64,96},{96,128},{128,160},{160,192},{192,224},{1,3... | collective-permute-start | bytes 24584 | tf_op jit(solution)/shard_map/ppermute | solution.py:34
  9.4 5.5 %collective-permute-start.1 = (f32[3,9,1,128]{3,2,1,0:T(1,128)S(1)}, f32[3,9,1,128]{3,2,1,0:T(1,128)S(1)}, u32[]{:S(2)}, u32[]{:S(2)}) collective-permute-start(f32[3,9,1,128]{3,2,1,0:T(1,128)S(1)} %slice.1813), channel_id=1, source_target_pairs={{4,0},{8,4},{12,8},{16,12},{20,16},{24,20},{28,24},{5,1},{9,5},{13... | collective-permute-start | bytes 41480 | tf_op jit(solution)/shard_map/ppermute | solution.py:34
  14.9 10.9 %collective-permute-start.2 = (f32[3,9,17,1]{3,2,1,0:T(8,128)S(1)}, f32[3,9,17,1]{3,2,1,0:T(8,128)S(1)}, u32[]{:S(2)}, u32[]{:S(2)}) collective-permute-start(f32[3,9,17,1]{3,2,1,0:T(8,128)S(1)} %fusion), channel_id=1, source_target_pairs={{1,0},{2,1},{3,2},{5,4},{6,5},{7,6},{9,8},{10,9},{11,10},{13,12},{... | collective-permute-start | bytes 5516 | tf_op jit(solution)/shard_map/ppermute | solution.py:34
  27.5 81.0 %copy-start.13 = (f32[1,8,16,128]{3,2,1,0:T(8,128)}, f32[1,8,16,128]{3,2,1,0:T(8,128)S(1)}, u32[]{:S(2)}) copy-start(f32[1,8,16,128]{3,2,1,0:T(8,128)S(1)} %get-tuple-element.36) | copy-start | bytes 196612
  27.5 82.4 %copy-start.15 = (f32[1,8,16,128]{3,2,1,0:T(8,128)}, f32[1,8,16,128]{3,2,1,0:T(8,128)S(1)}, u32[]{:S(2)}) copy-start(f32[1,8,16,128]{3,2,1,0:T(8,128)S(1)} %get-tuple-element.37) | copy-start | bytes 196612
  27.5 84.4 %copy-start.17 = (f32[1,8,16,128]{3,2,1,0:T(8,128)}, f32[1,8,16,128]{3,2,1,0:T(8,128)S(1)}, u32[]{:S(2)}) copy-start(f32[1,8,16,128]{3,2,1,0:T(8,128)S(1)} %get-tuple-element.38) | copy-start | bytes 196612
  27.5 100.1 %copy-start.5 = (f32[9,16,128]{2,1,0:T(8,128)}, f32[9,16,128]{2,1,0:T(8,128)S(1)}, u32[]{:S(2)}) copy-start(f32[9,16,128]{2,1,0:T(8,128)S(1)} %get-tuple-element.273) | copy-start | bytes 221188
  109.9 18.8 %copy-start.7 = (f32[1,8,16,128]{3,2,1,0:T(8,128)}, f32[1,8,16,128]{3,2,1,0:T(8,128)S(1)}, u32[]{:S(2)}) copy-start(f32[1,8,16,128]{3,2,1,0:T(8,128)S(1)} %get-tuple-element.28) | copy-start | bytes 196612
  111.2 17.4 %copy-start.9 = (f32[1,8,16,128]{3,2,1,0:T(8,128)}, f32[1,8,16,128]{3,2,1,0:T(8,128)S(1)}, u32[]{:S(2)}) copy-start(f32[1,8,16,128]{3,2,1,0:T(8,128)S(1)} %get-tuple-element.26) | copy-start | bytes 196612
  113.3 15.3 %copy-start.11 = (f32[1,8,16,128]{3,2,1,0:T(8,128)}, f32[1,8,16,128]{3,2,1,0:T(8,128)S(1)}, u32[]{:S(2)}) copy-start(f32[1,8,16,128]{3,2,1,0:T(8,128)S(1)} %get-tuple-element.22) | copy-start | bytes 196612
  113.3 8.8 %collective-permute-start.7 = (f32[9,1,128]{2,1,0:T(1,128)S(1)}, f32[9,1,128]{2,1,0:T(1,128)S(1)}, u32[]{:S(2)}, u32[]{:S(2)}) collective-permute-start(f32[9,1,128]{2,1,0:T(1,128)S(1)} %slice.1852), channel_id=1, source_target_pairs={{0,4},{4,8},{8,12},{12,16},{16,20},{20,24},{24,28},{1,5},{5,9},{9,... | collective-permute-start | bytes 13832 | tf_op jit(solution)/shard_map/ppermute | solution.py:34
  119.5 5.4 %collective-permute-start.3 = (f32[9,1,16,128]{3,2,1,0:T(8,128)S(1)}, f32[9,1,16,128]{3,2,1,0:T(8,128)S(1)}, u32[]{:S(2)}, u32[]{:S(2)}) collective-permute-start(f32[9,1,16,128]{3,2,1,0:T(8,128)S(1)} %slice.1832), channel_id=1, source_target_pairs={{0,32},{32,64},{64,96},{96,128},{128,160},{160,192},{192,224},{1,3... | collective-permute-start | bytes 221192 | tf_op jit(solution)/shard_map/ppermute | solution.py:34
  122.2 6.5 %copy-start.24 = (f32[9,1,128]{2,1,0:T(1,128)}, f32[9,1,128]{2,1,0:T(1,128)S(1)}, u32[]{:S(2)}) copy-start(f32[9,1,128]{2,1,0:T(1,128)S(1)} %collective-permute-done.7) | copy-start | bytes 13828
  122.3 5.2 %collective-permute-start.8 = (f32[9,17,1]{2,1,0:T(8,128)S(1)}, f32[9,17,1]{2,1,0:T(8,128)S(1)}, u32[]{:S(2)}, u32[]{:S(2)}) collective-permute-start(f32[9,17,1]{2,1,0:T(8,128)S(1)} %fusion.185), channel_id=1, source_target_pairs={{0,1},{1,2},{2,3},{4,5},{5,6},{6,7},{8,9},{9,10},{10,11},{12,13},{... | collective-permute-start | bytes 1844 | tf_op jit(solution)/shard_map/ppermute | solution.py:34
  125.0 10.5 %copy-start.4 = (f32[9,1,16,128]{3,2,1,0:T(8,128)}, f32[9,1,16,128]{3,2,1,0:T(8,128)S(1)}, u32[]{:S(2)}) copy-start(f32[9,1,16,128]{3,2,1,0:T(8,128)S(1)} %collective-permute-done.3) | copy-start | bytes 221188
  125.1 3.6 collective-permute-start.4
  127.6 1.1 copy-start.19
  129.7 4.4 %collective-permute-start.5 = (f32[9,9,17,1]{2,3,1,0:T(1,128)S(1)}, f32[9,9,17,1]{2,3,1,0:T(1,128)S(1)}, u32[]{:S(2)}, u32[]{:S(2)}) collective-permute-start(f32[9,9,17,1]{2,3,1,0:T(1,128)S(1)} %copy.434), channel_id=1, source_target_pairs={{0,1},{1,2},{2,3},{4,5},{5,6},{6,7},{8,9},{9,10},{10,11},{12,13},{... | collective-permute-start | bytes 16532 | tf_op jit(solution)/shard_map/ppermute | solution.py:34
  134.7 1.0 copy-start.23
  136.8 22.0 %copy-start.6 = (f32[9,16,128]{2,1,0:T(8,128)S(1)}, f32[9,16,128]{2,1,0:T(8,128)}, u32[]{:S(2)}) copy-start(f32[9,16,128]{2,1,0:T(8,128)} %copy-done.5) | copy-start | bytes 221188
  136.9 22.0 %copy-start.25 = (f32[9,1,128]{2,1,0:T(1,128)S(1)}, f32[9,1,128]{2,1,0:T(1,128)}, u32[]{:S(2)}) copy-start(f32[9,1,128]{2,1,0:T(1,128)} %copy-done.24) | copy-start | bytes 13828
  136.9 22.1 %copy-start.20 = (f32[9,17,1]{2,1,0:T(8,128)S(1)}, f32[9,17,1]{2,1,0:T(8,128)}, u32[]{:S(2)}) copy-start(f32[9,17,1]{2,1,0:T(8,128)} %copy-done.19) | copy-start | bytes 1840
  136.9 5.4 %collective-permute-start.10 = (f32[3,1,16,128]{3,2,1,0:T(8,128)S(1)}, f32[3,1,16,128]{3,2,1,0:T(8,128)S(1)}, u32[]{:S(2)}, u32[]{:S(2)}) collective-permute-start(f32[3,1,16,128]{3,2,1,0:T(8,128)S(1)} %get-tuple-element.247), channel_id=1, source_target_pairs={{32,0},{64,32},{96,64},{128,96},{160,128},{192,160},{224,192},{33,... | collective-permute-start | bytes 73736 | tf_op jit(solution)/shard_map/ppermute | solution.py:45
  138.3 4.9 %collective-permute-start.9 = (f32[3,1,16,128]{3,2,1,0:T(8,128)S(1)}, f32[3,1,16,128]{3,2,1,0:T(8,128)S(1)}, u32[]{:S(2)}, u32[]{:S(2)}) collective-permute-start(f32[3,1,16,128]{3,2,1,0:T(8,128)S(1)} %get-tuple-element.246), channel_id=1, source_target_pairs={{0,32},{32,64},{64,96},{96,128},{128,160},{160,192},{192,224},{1,3... | collective-permute-start | bytes 73736 | tf_op jit(solution)/shard_map/ppermute | solution.py:44
  143.3 6.8 %collective-permute-start.11 = (f32[3,10,1,128]{3,2,1,0:T(1,128)S(1)}, f32[3,10,1,128]{3,2,1,0:T(1,128)S(1)}, u32[]{:S(2)}, u32[]{:S(2)}) collective-permute-start(f32[3,10,1,128]{3,2,1,0:T(1,128)S(1)} %get-tuple-element.236), channel_id=1, source_target_pairs={{0,4},{4,8},{8,12},{12,16},{16,20},{20,24},{24,28},{1,5},{5,9},{9,... | collective-permute-start | bytes 46088 | tf_op jit(solution)/shard_map/ppermute | solution.py:44
  148.1 5.0 %collective-permute-start.12 = (f32[3,10,1,128]{3,2,1,0:T(1,128)S(1)}, f32[3,10,1,128]{3,2,1,0:T(1,128)S(1)}, u32[]{:S(2)}, u32[]{:S(2)}) collective-permute-start(f32[3,10,1,128]{3,2,1,0:T(1,128)S(1)} %get-tuple-element.237), channel_id=1, source_target_pairs={{4,0},{8,4},{12,8},{16,12},{20,16},{24,20},{28,24},{5,1},{9,5},{13... | collective-permute-start | bytes 46088 | tf_op jit(solution)/shard_map/ppermute | solution.py:45
  153.4 10.9 %collective-permute-start.13 = (f32[3,10,18,1]{3,2,1,0:T(8,128)S(1)}, f32[3,10,18,1]{3,2,1,0:T(8,128)S(1)}, u32[]{:S(2)}, u32[]{:S(2)}) collective-permute-start(f32[3,10,18,1]{3,2,1,0:T(8,128)S(1)} %get-tuple-element.216), channel_id=1, source_target_pairs={{0,1},{1,2},{2,3},{4,5},{5,6},{6,7},{8,9},{9,10},{10,11},{12,13},{... | collective-permute-start | bytes 6488 | tf_op jit(solution)/shard_map/ppermute | solution.py:44
  157.4 11.0 %collective-permute-start.14 = (f32[3,10,18,1]{3,2,1,0:T(8,128)S(1)}, f32[3,10,18,1]{3,2,1,0:T(8,128)S(1)}, u32[]{:S(2)}, u32[]{:S(2)}) collective-permute-start(f32[3,10,18,1]{3,2,1,0:T(8,128)S(1)} %get-tuple-element.217), channel_id=1, source_target_pairs={{1,0},{2,1},{3,2},{5,4},{6,5},{7,6},{9,8},{10,9},{11,10},{13,12},{... | collective-permute-start | bytes 6488 | tf_op jit(solution)/shard_map/ppermute | solution.py:45
  176.2 5.2 %collective-permute-start.15 = (f32[3,1,16,128]{3,2,1,0:T(8,128)S(1)}, f32[3,1,16,128]{3,2,1,0:T(8,128)S(1)}, u32[]{:S(2)}, u32[]{:S(2)}) collective-permute-start(f32[3,1,16,128]{3,2,1,0:T(8,128)S(1)} %get-tuple-element.244), channel_id=1, source_target_pairs={{0,32},{32,64},{64,96},{96,128},{128,160},{160,192},{192,224},{1,3... | collective-permute-start | bytes 73736 | tf_op jit(solution)/shard_map/ppermute | solution.py:44
  180.1 5.3 %collective-permute-start.16 = (f32[3,1,16,128]{3,2,1,0:T(8,128)S(1)}, f32[3,1,16,128]{3,2,1,0:T(8,128)S(1)}, u32[]{:S(2)}, u32[]{:S(2)}) collective-permute-start(f32[3,1,16,128]{3,2,1,0:T(8,128)S(1)} %get-tuple-element.245), channel_id=1, source_target_pairs={{32,0},{64,32},{96,64},{128,96},{160,128},{192,160},{224,192},{33,... | collective-permute-start | bytes 73736 | tf_op jit(solution)/shard_map/ppermute | solution.py:45
  185.4 5.7 %collective-permute-start.17 = (f32[3,10,1,128]{3,2,1,0:T(1,128)S(1)}, f32[3,10,1,128]{3,2,1,0:T(1,128)S(1)}, u32[]{:S(2)}, u32[]{:S(2)}) collective-permute-start(f32[3,10,1,128]{3,2,1,0:T(1,128)S(1)} %get-tuple-element.234), channel_id=1, source_target_pairs={{0,4},{4,8},{8,12},{12,16},{16,20},{20,24},{24,28},{1,5},{5,9},{9,... | collective-permute-start | bytes 46088 | tf_op jit(solution)/shard_map/ppermute | solution.py:44
  189.2 5.0 %collective-permute-start.18 = (f32[3,10,1,128]{3,2,1,0:T(1,128)S(1)}, f32[3,10,1,128]{3,2,1,0:T(1,128)S(1)}, u32[]{:S(2)}, u32[]{:S(2)}) collective-permute-start(f32[3,10,1,128]{3,2,1,0:T(1,128)S(1)} %get-tuple-element.235), channel_id=1, source_target_pairs={{4,0},{8,4},{12,8},{16,12},{20,16},{24,20},{28,24},{5,1},{9,5},{13... | collective-permute-start | bytes 46088 | tf_op jit(solution)/shard_map/ppermute | solution.py:45
  194.4 9.2 %collective-permute-start.19 = (f32[3,10,18,1]{3,2,1,0:T(8,128)S(1)}, f32[3,10,18,1]{3,2,1,0:T(8,128)S(1)}, u32[]{:S(2)}, u32[]{:S(2)}) collective-permute-start(f32[3,10,18,1]{3,2,1,0:T(8,128)S(1)} %get-tuple-element.214), channel_id=1, source_target_pairs={{0,1},{1,2},{2,3},{4,5},{5,6},{6,7},{8,9},{9,10},{10,11},{12,13},{... | collective-permute-start | bytes 6488 | tf_op jit(solution)/shard_map/ppermute | solution.py:44
  196.8 11.0 %collective-permute-start.20 = (f32[3,10,18,1]{3,2,1,0:T(8,128)S(1)}, f32[3,10,18,1]{3,2,1,0:T(8,128)S(1)}, u32[]{:S(2)}, u32[]{:S(2)}) collective-permute-start(f32[3,10,18,1]{3,2,1,0:T(8,128)S(1)} %get-tuple-element.215), channel_id=1, source_target_pairs={{1,0},{2,1},{3,2},{5,4},{6,5},{7,6},{9,8},{10,9},{11,10},{13,12},{... | collective-permute-start | bytes 6488 | tf_op jit(solution)/shard_map/ppermute | solution.py:45
  215.3 4.1 %collective-permute-start.21 = (f32[3,1,16,128]{3,2,1,0:T(8,128)S(1)}, f32[3,1,16,128]{3,2,1,0:T(8,128)S(1)}, u32[]{:S(2)}, u32[]{:S(2)}) collective-permute-start(f32[3,1,16,128]{3,2,1,0:T(8,128)S(1)} %get-tuple-element.242), channel_id=1, source_target_pairs={{0,32},{32,64},{64,96},{96,128},{128,160},{160,192},{192,224},{1,3... | collective-permute-start | bytes 73736 | tf_op jit(solution)/shard_map/ppermute | solution.py:44
  218.0 6.8 %collective-permute-start.22 = (f32[3,1,16,128]{3,2,1,0:T(8,128)S(1)}, f32[3,1,16,128]{3,2,1,0:T(8,128)S(1)}, u32[]{:S(2)}, u32[]{:S(2)}) collective-permute-start(f32[3,1,16,128]{3,2,1,0:T(8,128)S(1)} %get-tuple-element.243), channel_id=1, source_target_pairs={{32,0},{64,32},{96,64},{128,96},{160,128},{192,160},{224,192},{33,... | collective-permute-start | bytes 73736 | tf_op jit(solution)/shard_map/ppermute | solution.py:45
  224.8 6.4 %collective-permute-start.23 = (f32[3,10,1,128]{3,2,1,0:T(1,128)S(1)}, f32[3,10,1,128]{3,2,1,0:T(1,128)S(1)}, u32[]{:S(2)}, u32[]{:S(2)}) collective-permute-start(f32[3,10,1,128]{3,2,1,0:T(1,128)S(1)} %get-tuple-element.232), channel_id=1, source_target_pairs={{0,4},{4,8},{8,12},{12,16},{16,20},{20,24},{24,28},{1,5},{5,9},{9,... | collective-permute-start | bytes 46088 | tf_op jit(solution)/shard_map/ppermute | solution.py:44
  229.3 5.0 %collective-permute-start.24 = (f32[3,10,1,128]{3,2,1,0:T(1,128)S(1)}, f32[3,10,1,128]{3,2,1,0:T(1,128)S(1)}, u32[]{:S(2)}, u32[]{:S(2)}) collective-permute-start(f32[3,10,1,128]{3,2,1,0:T(1,128)S(1)} %get-tuple-element.233), channel_id=1, source_target_pairs={{4,0},{8,4},{12,8},{16,12},{20,16},{24,20},{28,24},{5,1},{9,5},{13... | collective-permute-start | bytes 46088 | tf_op jit(solution)/shard_map/ppermute | solution.py:45
  234.6 9.4 %collective-permute-start.25 = (f32[3,10,18,1]{3,2,1,0:T(8,128)S(1)}, f32[3,10,18,1]{3,2,1,0:T(8,128)S(1)}, u32[]{:S(2)}, u32[]{:S(2)}) collective-permute-start(f32[3,10,18,1]{3,2,1,0:T(8,128)S(1)} %get-tuple-element.212), channel_id=1, source_target_pairs={{0,1},{1,2},{2,3},{4,5},{5,6},{6,7},{8,9},{9,10},{10,11},{12,13},{... | collective-permute-start | bytes 6488 | tf_op jit(solution)/shard_map/ppermute | solution.py:44
  237.1 11.0 %collective-permute-start.26 = (f32[3,10,18,1]{3,2,1,0:T(8,128)S(1)}, f32[3,10,18,1]{3,2,1,0:T(8,128)S(1)}, u32[]{:S(2)}, u32[]{:S(2)}) collective-permute-start(f32[3,10,18,1]{3,2,1,0:T(8,128)S(1)} %get-tuple-element.213), channel_id=1, source_target_pairs={{1,0},{2,1},{3,2},{5,4},{6,5},{7,6},{9,8},{10,9},{11,10},{13,12},{... | collective-permute-start | bytes 6488 | tf_op jit(solution)/shard_map/ppermute | solution.py:45
  255.6 6.2 %collective-permute-start.27 = (f32[3,1,16,128]{3,2,1,0:T(8,128)S(1)}, f32[3,1,16,128]{3,2,1,0:T(8,128)S(1)}, u32[]{:S(2)}, u32[]{:S(2)}) collective-permute-start(f32[3,1,16,128]{3,2,1,0:T(8,128)S(1)} %get-tuple-element.240), channel_id=1, source_target_pairs={{0,32},{32,64},{64,96},{96,128},{128,160},{160,192},{192,224},{1,3... | collective-permute-start | bytes 73736 | tf_op jit(solution)/shard_map/ppermute | solution.py:44
  260.4 5.3 %collective-permute-start.28 = (f32[3,1,16,128]{3,2,1,0:T(8,128)S(1)}, f32[3,1,16,128]{3,2,1,0:T(8,128)S(1)}, u32[]{:S(2)}, u32[]{:S(2)}) collective-permute-start(f32[3,1,16,128]{3,2,1,0:T(8,128)S(1)} %get-tuple-element.241), channel_id=1, source_target_pairs={{32,0},{64,32},{96,64},{128,96},{160,128},{192,160},{224,192},{33,... | collective-permute-start | bytes 73736 | tf_op jit(solution)/shard_map/ppermute | solution.py:45
  265.7 5.6 %collective-permute-start.29 = (f32[3,10,1,128]{3,2,1,0:T(1,128)S(1)}, f32[3,10,1,128]{3,2,1,0:T(1,128)S(1)}, u32[]{:S(2)}, u32[]{:S(2)}) collective-permute-start(f32[3,10,1,128]{3,2,1,0:T(1,128)S(1)} %get-tuple-element.230), channel_id=1, source_target_pairs={{0,4},{4,8},{8,12},{12,16},{16,20},{20,24},{24,28},{1,5},{5,9},{9,... | collective-permute-start | bytes 46088 | tf_op jit(solution)/shard_map/ppermute | solution.py:44
  269.4 5.0 %collective-permute-start.30 = (f32[3,10,1,128]{3,2,1,0:T(1,128)S(1)}, f32[3,10,1,128]{3,2,1,0:T(1,128)S(1)}, u32[]{:S(2)}, u32[]{:S(2)}) collective-permute-start(f32[3,10,1,128]{3,2,1,0:T(1,128)S(1)} %get-tuple-element.231), channel_id=1, source_target_pairs={{4,0},{8,4},{12,8},{16,12},{20,16},{24,20},{28,24},{5,1},{9,5},{13... | collective-permute-start | bytes 46088 | tf_op jit(solution)/shard_map/ppermute | solution.py:45
  274.7 8.8 %collective-permute-start.31 = (f32[3,10,18,1]{3,2,1,0:T(8,128)S(1)}, f32[3,10,18,1]{3,2,1,0:T(8,128)S(1)}, u32[]{:S(2)}, u32[]{:S(2)}) collective-permute-start(f32[3,10,18,1]{3,2,1,0:T(8,128)S(1)} %get-tuple-element.210), channel_id=1, source_target_pairs={{0,1},{1,2},{2,3},{4,5},{5,6},{6,7},{8,9},{9,10},{10,11},{12,13},{... | collective-permute-start | bytes 6488 | tf_op jit(solution)/shard_map/ppermute | solution.py:44
  276.6 11.0 %collective-permute-start.32 = (f32[3,10,18,1]{3,2,1,0:T(8,128)S(1)}, f32[3,10,18,1]{3,2,1,0:T(8,128)S(1)}, u32[]{:S(2)}, u32[]{:S(2)}) collective-permute-start(f32[3,10,18,1]{3,2,1,0:T(8,128)S(1)} %get-tuple-element.211), channel_id=1, source_target_pairs={{1,0},{2,1},{3,2},{5,4},{6,5},{7,6},{9,8},{10,9},{11,10},{13,12},{... | collective-permute-start | bytes 6488 | tf_op jit(solution)/shard_map/ppermute | solution.py:45
  295.1 4.9 %collective-permute-start.33 = (f32[3,1,16,128]{3,2,1,0:T(8,128)S(1)}, f32[3,1,16,128]{3,2,1,0:T(8,128)S(1)}, u32[]{:S(2)}, u32[]{:S(2)}) collective-permute-start(f32[3,1,16,128]{3,2,1,0:T(8,128)S(1)} %get-tuple-element.238), channel_id=1, source_target_pairs={{0,32},{32,64},{64,96},{96,128},{128,160},{160,192},{192,224},{1,3... | collective-permute-start | bytes 73736 | tf_op jit(solution)/shard_map/ppermute | solution.py:44
  298.7 4.9 %collective-permute-start.34 = (f32[3,1,16,128]{3,2,1,0:T(8,128)S(1)}, f32[3,1,16,128]{3,2,1,0:T(8,128)S(1)}, u32[]{:S(2)}, u32[]{:S(2)}) collective-permute-start(f32[3,1,16,128]{3,2,1,0:T(8,128)S(1)} %get-tuple-element.239), channel_id=1, source_target_pairs={{32,0},{64,32},{96,64},{128,96},{160,128},{192,160},{224,192},{33,... | collective-permute-start | bytes 73736 | tf_op jit(solution)/shard_map/ppermute | solution.py:45
  303.7 4.5 %collective-permute-start.35 = (f32[3,10,1,128]{3,2,1,0:T(1,128)S(1)}, f32[3,10,1,128]{3,2,1,0:T(1,128)S(1)}, u32[]{:S(2)}, u32[]{:S(2)}) collective-permute-start(f32[3,10,1,128]{3,2,1,0:T(1,128)S(1)} %get-tuple-element.228), channel_id=1, source_target_pairs={{0,4},{4,8},{8,12},{12,16},{16,20},{20,24},{24,28},{1,5},{5,9},{9,... | collective-permute-start | bytes 46088 | tf_op jit(solution)/shard_map/ppermute | solution.py:44
  306.3 5.0 %collective-permute-start.36 = (f32[3,10,1,128]{3,2,1,0:T(1,128)S(1)}, f32[3,10,1,128]{3,2,1,0:T(1,128)S(1)}, u32[]{:S(2)}, u32[]{:S(2)}) collective-permute-start(f32[3,10,1,128]{3,2,1,0:T(1,128)S(1)} %get-tuple-element.229), channel_id=1, source_target_pairs={{4,0},{8,4},{12,8},{16,12},{20,16},{24,20},{28,24},{5,1},{9,5},{13... | collective-permute-start | bytes 46088 | tf_op jit(solution)/shard_map/ppermute | solution.py:45
  311.5 8.8 %collective-permute-start.37 = (f32[3,10,18,1]{3,2,1,0:T(8,128)S(1)}, f32[3,10,18,1]{3,2,1,0:T(8,128)S(1)}, u32[]{:S(2)}, u32[]{:S(2)}) collective-permute-start(f32[3,10,18,1]{3,2,1,0:T(8,128)S(1)} %get-tuple-element.208), channel_id=1, source_target_pairs={{0,1},{1,2},{2,3},{4,5},{5,6},{6,7},{8,9},{9,10},{10,11},{12,13},{... | collective-permute-start | bytes 6488 | tf_op jit(solution)/shard_map/ppermute | solution.py:44
  313.5 11.0 %collective-permute-start.38 = (f32[3,10,18,1]{3,2,1,0:T(8,128)S(1)}, f32[3,10,18,1]{3,2,1,0:T(8,128)S(1)}, u32[]{:S(2)}, u32[]{:S(2)}) collective-permute-start(f32[3,10,18,1]{3,2,1,0:T(8,128)S(1)} %get-tuple-element.209), channel_id=1, source_target_pairs={{1,0},{2,1},{3,2},{5,4},{6,5},{7,6},{9,8},{10,9},{11,10},{13,12},{... | collective-permute-start | bytes 6488 | tf_op jit(solution)/shard_map/ppermute | solution.py:45
  331.9 20.8 %copy-start = (f32[3,8,16,128]{3,2,1,0:T(8,128)}, f32[3,8,16,128]{3,2,1,0:T(8,128)S(1)}, u32[]{:S(2)}) copy-start(f32[3,8,16,128]{3,2,1,0:T(8,128)S(1)} %fusion.32) | copy-start | bytes 589828
  331.9 5.0 %collective-permute-start.39 = (f32[3,1,16,128]{3,2,1,0:T(8,128)S(1)}, f32[3,1,16,128]{3,2,1,0:T(8,128)S(1)}, u32[]{:S(2)}, u32[]{:S(2)}) collective-permute-start(f32[3,1,16,128]{3,2,1,0:T(8,128)S(1)} %slice.2088), channel_id=1, source_target_pairs={{32,0},{64,32},{96,64},{128,96},{160,128},{192,160},{224,192},{33,... | collective-permute-start | bytes 73736 | tf_op jit(solution)/shard_map/ppermute | solution.py:34
  336.9 5.0 %collective-permute-start.40 = (f32[3,9,1,128]{3,2,1,0:T(1,128)S(1)}, f32[3,9,1,128]{3,2,1,0:T(1,128)S(1)}, u32[]{:S(2)}, u32[]{:S(2)}) collective-permute-start(f32[3,9,1,128]{3,2,1,0:T(1,128)S(1)} %pad_maximum_fusion.58), channel_id=1, source_target_pairs={{4,0},{8,4},{12,8},{16,12},{20,16},{24,20},{28,24},{5,1},{9,5},{13... | collective-permute-start | bytes 41480 | tf_op jit(solution)/shard_map/ppermute | solution.py:34
  342.0 10.3 %collective-permute-start.41 = (f32[3,9,17,1]{3,2,1,0:T(8,128)S(1)}, f32[3,9,17,1]{3,2,1,0:T(8,128)S(1)}, u32[]{:S(2)}, u32[]{:S(2)}) collective-permute-start(f32[3,9,17,1]{3,2,1,0:T(8,128)S(1)} %bitcast.173), channel_id=1, source_target_pairs={{1,0},{2,1},{3,2},{5,4},{6,5},{7,6},{9,8},{10,9},{11,10},{13,12},{... | collective-permute-start | bytes 5516 | tf_op jit(solution)/shard_map/ppermute | solution.py:34
  355.2 4.2 %collective-permute-start.42 = (f32[2,16,128]{2,1,0:T(8,128)S(1)}, f32[2,16,128]{2,1,0:T(8,128)S(1)}, u32[]{:S(2)}, u32[]{:S(2)}) collective-permute-start(f32[2,16,128]{2,1,0:T(8,128)S(1)} %get-tuple-element.271), channel_id=1, source_target_pairs={{0,32},{32,64},{64,96},{96,128},{128,160},{160,192},{192,224},{1,3... | collective-permute-start | bytes 49160 | tf_op jit(solution)/shard_map/ppermute | solution.py:44
  358.1 4.5 %collective-permute-start.43 = (f32[2,16,128]{2,1,0:T(8,128)S(1)}, f32[2,16,128]{2,1,0:T(8,128)S(1)}, u32[]{:S(2)}, u32[]{:S(2)}) collective-permute-start(f32[2,16,128]{2,1,0:T(8,128)S(1)} %get-tuple-element.272), channel_id=1, source_target_pairs={{32,0},{64,32},{96,64},{128,96},{160,128},{192,160},{224,192},{33,... | collective-permute-start | bytes 49160 | tf_op jit(solution)/shard_map/ppermute | solution.py:45
  362.6 6.5 %collective-permute-start.44 = (f32[12,2,128]{2,1,0:T(2,128)S(1)}, f32[12,2,128]{2,1,0:T(2,128)S(1)}, u32[]{:S(2)}, u32[]{:S(2)}) collective-permute-start(f32[12,2,128]{2,1,0:T(2,128)S(1)} %get-tuple-element.269), channel_id=1, source_target_pairs={{0,4},{4,8},{8,12},{12,16},{16,20},{20,24},{24,28},{1,5},{5,9},{9,... | collective-permute-start | bytes 36872 | tf_op jit(solution)/shard_map/ppermute | solution.py:44
  365.8 5.0 %collective-permute-start.45 = (f32[12,2,128]{2,1,0:T(2,128)S(1)}, f32[12,2,128]{2,1,0:T(2,128)S(1)}, u32[]{:S(2)}, u32[]{:S(2)}) collective-permute-start(f32[12,2,128]{2,1,0:T(2,128)S(1)} %get-tuple-element.270), channel_id=1, source_target_pairs={{4,0},{8,4},{12,8},{16,12},{20,16},{24,20},{28,24},{5,1},{9,5},{13... | collective-permute-start | bytes 36872 | tf_op jit(solution)/shard_map/ppermute | solution.py:45
  370.9 4.1 %collective-permute-start.46 = (f32[12,20,2]{2,1,0:T(8,128)S(1)}, f32[12,20,2]{2,1,0:T(8,128)S(1)}, u32[]{:S(2)}, u32[]{:S(2)}) collective-permute-start(f32[12,20,2]{2,1,0:T(8,128)S(1)} %get-tuple-element.263), channel_id=1, source_target_pairs={{0,1},{1,2},{2,3},{4,5},{5,6},{6,7},{8,9},{9,10},{10,11},{12,13},{... | collective-permute-start | bytes 5768 | tf_op jit(solution)/shard_map/ppermute | solution.py:44
  372.8 6.3 %collective-permute-start.47 = (f32[12,20,2]{2,1,0:T(8,128)S(1)}, f32[12,20,2]{2,1,0:T(8,128)S(1)}, u32[]{:S(2)}, u32[]{:S(2)}) collective-permute-start(f32[12,20,2]{2,1,0:T(8,128)S(1)} %get-tuple-element.264), channel_id=1, source_target_pairs={{1,0},{2,1},{3,2},{5,4},{6,5},{7,6},{9,8},{10,9},{11,10},{13,12},{... | collective-permute-start | bytes 5768 | tf_op jit(solution)/shard_map/ppermute | solution.py:45
  (10 other events, 8.8 us)
where the time goes:
time: 389 us; the launch traced here: 382 us
  starting transfers between devices  121 us (31%)
  waiting for transfers between devices  116 us (30%)
  blocking collectives  77.6 us (20%)
  other arithmetic  46.3 us (12%)
  local copies, waits for them, and re-layouts  16.5 us (4%)
  between operations  4.89 us (1%)
    ppermute x18, waiting for transfers between devices, extended(): after = lax.ppermute(leading, axis, down)  62.1 us
    ppermute x18, starting transfers between devices, extended(): before = lax.ppermute(last, axis, up)  59.1 us
    pmax x4, blocking collectives, over_axes(): return functools.reduce(lax.pmax, axes, array)  40.6 us
    psum x4, blocking collectives, over_axes_2(): return functools.reduce(lax.psum, axes, array)  36.9 us
    ppermute x12, starting transfers between devices, passed_along(): return lax.ppermute(block, axis, route)  33.2 us
    ppermute x18, starting transfers between devices, extended(): after = lax.ppermute(leading, axis, down)  28.5 us
    ppermute x18, waiting for transfers between devices, extended(): before = lax.ppermute(last, axis, up)  27.8 us
    ppermute x12, waiting for transfers between devices, passed_along(): return lax.ppermute(block, axis, route)  25.8 us
  transfers between devices with their start and end apart: 48, of which 30 were waited for; matrix products, arithmetic and copies ran while one was open for 1% of the time, Pallas kernels for 0%

commit v1 on v0

v1 whole, which is shorter than its diff:
```python
import functools
import math

import jax
import jax.numpy as jnp
from jax import lax
from jax.experimental import pallas as pl
from jax.experimental.pallas import tpu as pltpu
from jax.sharding import PartitionSpec as P

ITERS = 6
lame_first = 0.3 / (1.3 * 0.4)
shear_modulus = 1.0 / 2.6
lame_ratio = lame_first / shear_modulus
power_scale = 3.0
damping = 0.6
shift_term = 0.1
diag_factor = (lame_first + 3.0 * shear_modulus) / 16.0
W1, W2, W3 = (2.5 - math.sqrt(n) for n in (1, 2, 3))
W4 = 0.5
AXES = ("gx", "gy", "gz")

BX, BY, BZ = 8, 16, 128
NODES, CELLS = 25, 24
ROWS = 40
F32 = jnp.float32
VM = 24 * 1024 * 1024


def tile(value):
    return jax.ShapeDtypeStruct(value, F32)


def kernel_call(body, outs, name, scratch=(), flops=1_000_000, aliases=None):
    spec = pl.BlockSpec(memory_space=pltpu.VMEM)

    def run(*args):
        return pl.pallas_call(
            body,
            out_shape=[tile(shape) for shape in outs],
            in_specs=[spec] * len(args),
            out_specs=[spec] * len(outs),
            scratch_shapes=list(scratch),
            input_output_aliases=aliases or {},
            name=name,
            compiler_params=pltpu.CompilerParams(vmem_limit_bytes=VM),
            cost_estimate=pl.CostEstimate(flops=flops, bytes_accessed=1_000_000, transcendentals=0),
        )(*args)

    return run


def rolled(value, shift, axis):
    shift = shift % value.shape[axis]
    return value if shift == 0 else pltpu.roll(value, shift, axis)


def lanes():
    return lax.broadcasted_iota(jnp.int32, (8, 128), 1)


def rows():
    return lax.broadcasted_iota(jnp.int32, (8, 128), 0)


def split(value):
    return [value[8 * g : 8 * g + 8] for g in range(4)], value[32:40]


def join(main, strip):
    return jnp.concatenate([*main, strip], axis=0)


def z_next(value):
    main, strip = split(value)
    lane = lanes()
    moved = [rolled(m, -1, 1) for m in main]
    out = [jnp.where(lane == 127, rolled(strip, 127 - 32 * g, 1), moved[g]) for g in range(4)]
    tail = rolled(strip, -1, 1)
    for g in range(4):
        tail = jnp.where(lane == 32 * g + 31, rolled(moved[g], 32 * g + 32, 1), tail)
    return join(out, tail)


def z_prev(value):
    main, strip = split(value)
    lane = lanes()
    moved = [rolled(m, 1, 1) for m in main]
    out = [jnp.where(lane == 0, rolled(strip, 97 - 32 * g, 1), moved[g]) for g in range(4)]
    tail = rolled(strip, 1, 1)
    for g in range(4):
        tail = jnp.where(lane == 32 * g, rolled(moved[g], 32 * g, 1), tail)
    return join(out, tail)


def y_next(value, beyond=None):
    main, strip = split(value)
    row = rows()
    turned = [rolled(m, -1, 0) for m in main]
    follow = [turned[1], turned[2], turned[3], turned[3] if beyond is None else beyond[0]]
    out = [jnp.where(row == 7, follow[g], turned[g]) for g in range(4)]
    tail = rolled(strip, -1, 0)
    after = rolled(tail, -32, 1)
    if beyond is not None:
        after = jnp.where(lanes() >= 96, beyond[1], after)
    return join(out, jnp.where(row == 7, after, tail))


def y_prev(value):
    main, strip = split(value)
    row = rows()
    turned = [rolled(m, 1, 0) for m in main]
    before = [turned[0], turned[0], turned[1], turned[2]]
    out = [jnp.where(row == 0, before[g], turned[g]) for g in range(4)]
    tail = rolled(strip, 1, 0)
    return join(out, jnp.where(row == 0, rolled(tail, 32, 1), tail))


def pack_z(disp, dens, up, down):
    lane = lanes()
    for c in range(4):
        for k in range(4):
            top = bottom = jnp.zeros((8, 128), F32)
            for q in range(4):
                x, t = k + 4 * (q // 2), 8 * (q % 2)
                value = disp[c, x, t : t + 8, :] if c < 3 else dens[x, t : t + 8, :]
                mine = (lane >= 32 * q) & (lane < 32 * q + 32)
                top = jnp.where(mine & (lane >= 32 * q + 24), rolled(value, 32 * q + 32, 1), top)
                bottom = jnp.where(mine & (lane < 32 * q + 9), rolled(value, 32 * q, 1), bottom)
            up[4 * c + k] = top
            down[4 * c + k] = bottom


def pack_y(mid, low, high, far, up, down):
    lane = lanes()
    odd = (lane // 32) % 2 == 1
    sources = (low, mid, high)
    for s, src in enumerate(sources):
        for i in range(32):
            up[32 * s + i] = src[2 * i + 1]
            down[32 * s + i] = src[2 * i]
        for c in range(4):
            for k in range(2):
                first, second = src[64 + 4 * c + k], src[64 + 4 * c + k + 2]
                up[99 + 8 * s + 2 * c + k] = jnp.where(odd, first, rolled(second, -32, 1))
                down[99 + 8 * s + 2 * c + k] = jnp.where(odd, rolled(second, 32, 1), first)
        for i in range(24):
            r = 24 * s + i
            down[126 + r // 8, r % 8 : r % 8 + 1, :] = src[2 * i + 1, 0:1, :]
        for i in range(12):
            r = 12 * s + i
            down[136 + r // 8, r % 8 : r % 8 + 1, :] = src[64 + i, 0:1, :]
    for c in range(3):
        up[96 + c] = far[2 * c + 1]
        down[96 + c] = far[2 * c]
        up[123 + c] = far[6 + c]
        down[123 + c] = far[6 + c]
        r = 72 + c
        down[126 + r // 8, r % 8 : r % 8 + 1, :] = far[2 * c + 1, 0:1, :]
        r = 36 + c
        down[136 + r // 8, r % 8 : r % 8 + 1, :] = far[6 + c, 0:1, :]


def unpacked(c, p, sources, far, below, above):
    lane = lanes()
    group = lane // 32
    if p < 24:
        s, x = divmod(p, 8)
        src, i, k = sources[s], 8 * c + x, x % 4
        own = rolled(src[64 + 4 * c + k], 32 if x < 4 else -32, 1)
        slot = 99 + 8 * s + 2 * c + x % 2
        under = rolled(below[slot], {0: -32, 1: -96, 2: 0, 3: -64}[(1 if x >= 4 else 0) + (2 if k >= 2 else 0)], 1)
        over = rolled(above[slot], {0: 96, 1: 32, 2: 64, 3: 0}[(1 if x >= 4 else 0) + (2 if k >= 2 else 0)], 1)
        main = [below[32 * s + i], src[2 * i], src[2 * i + 1], above[32 * s + i]]
        r, q = 24 * s + i, 12 * s + 4 * c + k
        turn = 64 if x < 4 else 0
    else:
        own = rolled(far[6 + c], 32, 1)
        under = rolled(below[123 + c], -32, 1)
        over = rolled(above[123 + c], 96, 1)
        main = [below[96 + c], far[2 * c], far[2 * c + 1], above[96 + c]]
        r, q, turn = 72 + c, 36 + c, 64
    strip = jnp.where(group == 0, under, jnp.where(group == 3, over, own))
    if c == 3:
        return join(main, strip), None
    line = jnp.broadcast_to(above[126 + r // 8, r % 8 : r % 8 + 1, :], (8, 128))
    edge = jnp.broadcast_to(above[136 + q // 8, q % 8 : q % 8 + 1, :], (8, 128))
    return join(main, strip), (line, rolled(edge, turn, 1))


def corner_sums(value, beyond=None):
    if beyond is not None:
        following = y_next(value, beyond)
        both, change = following + value, following - value
        first, second = z_next(both), z_next(change)
        return first + both, second + change, first - both
    following = z_next(value)
    both, change = following + value, following - value
    after = y_next(both)
    return after + both, after - both, y_next(change) + change


def strain_of(new, old):
    grad = [[new[c][0] - old[c][0] for c in range(3)]]
    grad.append([new[c][1] + old[c][1] for c in range(3)])
    grad.append([new[c][2] + old[c][2] for c in range(3)])
    return [
        grad[0][0],
        grad[1][1],
        grad[2][2],
        grad[0][1] + grad[1][0],
        grad[1][2] + grad[2][1],
        grad[2][0] + grad[0][2],
    ]


def scaled_stress(values, factor):
    trace = lame_ratio * (values[0] + values[1] + values[2])
    return [factor * (trace + 2.0 * v) for v in values[:3]] + [factor * v for v in values[3:]]


def forces(prev, here):
    add = [prev[i] + here[i] for i in range(6)]
    sub = {i: prev[i] - here[i] for i in (0, 3, 5)}
    out = []
    for along_x, along_y, along_z in ((0, 3, 5), (3, 1, 4), (5, 4, 2)):
        a, b, w = sub[along_x], add[along_y], add[along_z]
        first = y_prev(a + b) + (a - b)
        second = y_prev(w) + w
        out.append(z_prev(first + second) + (first - second))
    return out


def get3(ref, p):
    return [ref[c, p] for c in range(3)]


def put_corners(ref, values):
    for c in range(3):
        for i in range(3):
            ref[3 * c + i] = values[c][i]


def get_corners(ref):
    return [[ref[3 * c + i] for i in range(3)] for c in range(3)]


def mises(v):
    return (
        v[0] * v[0] + v[1] * v[1] + v[2] * v[2] - v[0] * v[1] - v[1] * v[2] - v[2] * v[0]
        + 3.0 * (v[3] * v[3] + v[4] * v[4] + v[5] * v[5])
    )


def mises_slope(v):
    return [
        2.0 * v[0] - v[1] - v[2],
        2.0 * v[1] - v[2] - v[0],
        2.0 * v[2] - v[0] - v[1],
        6.0 * v[3],
        6.0 * v[4],
        6.0 * v[5],
    ]


def stress_kernel(mid, low, high, far, below, above, base, cells, stress, stats, disp, line, edge, corners):
    sources = (low, mid, high)
    for p in range(NODES):
        for c in range(4 if p < CELLS else 3):
            value, beyond = unpacked(c, p, sources, far, below, above)
            if c == 3:
                cells[p] = value
            else:
                disp[c, p] = value
                line[c, p] = beyond[0]
                edge[c, p] = beyond[1]

    def planes(p):
        return [corner_sums(disp[c, p], (line[c, p], edge[c, p])) for c in range(3)]

    put_corners(corners, planes(0))

    def step(p, most):
        new = planes(p + 1)
        values = scaled_stress(strain_of(new, get_corners(corners)), 0.25 * shear_modulus)
        put_corners(corners, new)
        dens = cells[p]
        for i in range(6):
            base[i, p] = values[i]
        local = jnp.sqrt(dens * mises(values) + 1.0)
        stress[p] = local
        return jnp.maximum(most, jnp.where(dens > 0.0, local, 0.0))

    most = lax.fori_loop(0, CELLS, step, jnp.zeros((ROWS, 128), F32))
    top = power_scale * jnp.max(most, axis=(0, 1), keepdims=True)

    def add(p, total):
        return total + jnp.exp(power_scale * stress[p, 8:24, :] - top)

    total = lax.fori_loop(8, 16, add, jnp.zeros((BY, 128), F32))
    total = jnp.sum(total, axis=(0, 1), keepdims=True)
    stats[0] = jnp.broadcast_to(top, (8, 128))
    stats[1] = jnp.broadcast_to(total, (8, 128))


def load_kernel(base, cells, stress, stats, rhs, stiff, weight, explicit, field, held, kept):
    top = stats[0, 0:1, 0:1]

    def element(p):
        dens = cells[p]
        values = [base[i, p] for i in range(6)]
        local = stress[p]
        factor = jnp.where(dens > 0.0, jnp.exp(power_scale * local - top), 0.0) / (2.0 * local)
        explicit[p] = factor * mises(values)
        part = scaled_stress(mises_slope(values), (0.25 * shear_modulus) * dens * factor)
        rigid = jnp.where(dens > 0.0, 0.01 + 0.99 * (dens * dens * dens), 0.0)
        stiff[p] = (shear_modulus / 16.0) * rigid
        return part, rigid

    part, rigid = element(0)
    for i in range(6):
        held[i] = part[i]
    kept[...] = rigid

    def step(p, carry):
        part, rigid = element(p)
        load = forces([held[i] for i in range(6)], part)
        for i in range(6):
            held[i] = part[i]
        total = kept[...] + rigid
        kept[...] = rigid
        total = total + y_prev(total)
        total = total + z_prev(total)
        own = jnp.where(cells[p] > 0.0, damping / (diag_factor * total + shift_term), 0.0)
        weight[p] = own
        for c in range(3):
            value = own * load[c]
            rhs[c, p] = value
            field[c, p] = value
        return carry

    lax.fori_loop(1, CELLS, step, 0)


def sweep_into(field, rhs, stiff, weight, held, corners, lo, hi):
    def planes(p):
        return [corner_sums(v) for v in get3(field, p)]

    def element(new, old, p):
        return scaled_stress(strain_of(new, old), stiff[p])

    first, second = planes(lo - 1), planes(lo)
    part = element(second, first, lo - 1)
    for i in range(6):
        held[i] = part[i]
    put_corners(corners, second)

    def step(p, carry):
        new = planes(p + 1)
        part = element(new, get_corners(corners), p)
        put_corners(corners, new)
        force = forces([held[i] for i in range(6)], part)
        for i in range(6):
            held[i] = part[i]
        own = weight[p]
        keep = 1.0 - shift_term * own
        for c in range(3):
            field[c, p] = keep * field[c, p] + rhs[c, p] - own * force[c]
        return carry

    lax.fori_loop(lo, hi + 1, step, 0)


def positions(axis, length, cell):
    whole = lax.axis_size(axis) * length
    place = lax.axis_index(axis) * length + cell
    return lambda o: ((place + o >= 0) & (place + o < whole)).astype(F32)


def sweeps_kernel(rhs, stiff, weight, explicit, base, cells, start, adjoint, sens, field, held, corners, near, side, out):
    for c in range(3):
        for p in range(1, CELLS):
            field[c, p] = start[c, p]
    for k in range(1, ITERS):
        sweep_into(field, rhs, stiff, weight, held, corners, 1 + k, 23 - k)
    final_part(field, explicit, base, cells, adjoint, sens, corners, near, side, out)


def final_part(field, explicit, base, cells, adjoint, sens, corners, near, side, out):
    for c in range(3):
        adjoint[c] = field[c, 8:16, 8:24, :]

    row = lax.broadcasted_iota(jnp.int32, (ROWS, 128), 0)
    lane = lax.broadcasted_iota(jnp.int32, (ROWS, 128), 1)
    group, place = lane // 32, lane % 32
    main = row < 32
    y_cell = jnp.where(main, row - 8, 8 * group + row - 40)
    z_cell = jnp.where(main, lane, jnp.where(place < 16, 128 + place, place - 32))
    in_y, in_z = positions("gy", BY, y_cell), positions("gz", BZ, z_cell)
    ys, zs = {o: in_y(o) for o in range(-2, 3)}, {o: in_z(o) for o in range(-2, 3)}
    beside = ys[-1] + ys[1]
    across = zs[-1] + zs[1]
    ones = beside * zs[0] + ys[0] * across
    diagonal = beside * across
    twos = (ys[-2] + ys[2]) * zs[0] + ys[0] * (zs[-2] + zs[2])
    centre = ys[0] * zs[0]
    near_0 = 2.5 * centre + W1 * ones + W2 * diagonal + W4 * twos
    near_1 = W1 * centre + W2 * ones + W3 * diagonal
    near_2 = W4 * centre

    def planes(p):
        return [corner_sums(v) for v in get3(field, p)]

    put_corners(corners, planes(6))

    def step(p, carry):
        new = planes(p + 1)
        strain = strain_of(new, get_corners(corners))
        put_corners(corners, new)
        dens = cells[p]
        worked = base[0, p] * strain[0]
        for i in range(1, 6):
            worked = worked + base[i, p] * strain[i]
        raw = explicit[p] - (0.25 * 2.97) * dens * dens * worked
        in_x = positions("gx", BX, p - 8)
        hsum = near_0 + near_1 * (in_x(-1) + in_x(1)) + near_2 * (in_x(-2) + in_x(2))
        value = jnp.where(dens > 0.0, raw / jnp.where(dens > 0.0, hsum, 1.0), 0.0)
        above, under = z_next(value), z_prev(value)
        left, right = y_next(value), y_prev(value)
        row_pair = above + under
        unit = row_pair + (left + right)
        corner = y_next(row_pair) + y_prev(row_pair)
        two = z_next(above) + z_prev(under) + y_next(left) + y_prev(right)
        near[p - 6] = (2.5 * value + W1 * unit + W2 * corner + W4 * two)[8:24]
        side[p - 6] = (W1 * value + W2 * unit + W3 * corner)[8:24]
        out[p - 6] = (W4 * value)[8:24]
        return carry

    lax.fori_loop(6, 18, step, 0)
    for p in range(8):
        q = p + 2
        sens[p] = near[q] + (side[q - 1] + side[q + 1]) + (out[q - 2] + out[q + 2])


def passed(block, axis, distance):
    count = lax.axis_size(axis)
    return lax.ppermute(block, axis, [(i, i + distance) for i in range(count) if 0 <= i + distance < count])


def merged(mine, other):
    larger = jnp.maximum(mine[0], other[0])
    gap = jnp.exp(jnp.minimum(mine[0], other[0]) - larger)
    first = mine[0] >= other[0]
    total = jnp.where(first, mine[1], other[1]) + jnp.where(first, other[1], mine[1]) * gap
    return jnp.stack([larger, total])


def on_device(displacement, density):
    plane = (ROWS, 128)
    up, down = kernel_call(pack_z, [(16, 8, 128)] * 2, "pack_z")(displacement, density)
    below_z, above_z = passed(up, "gz", 1), passed(down, "gz", -1)
    mid = jnp.concatenate(
        [displacement.reshape(48, 8, 128), density.reshape(16, 8, 128), below_z + above_z], axis=0
    )
    far = jnp.concatenate([mid[t : t + n] for t, n in ((0, 2), (16, 2), (32, 2), (64, 1), (68, 1), (72, 1))], axis=0)
    low, high, far = passed(mid, "gx", 1), passed(mid, "gx", -1), passed(far, "gx", -2)
    up, down = kernel_call(pack_y, [(126, 8, 128), (141, 8, 128)], "pack_y")(mid, low, high, far)
    below, above = passed(up, "gy", 1), passed(down, "gy", -1)
    base, cells, stress, stats = kernel_call(
        stress_kernel,
        [(6, CELLS, *plane), (CELLS, *plane), (CELLS, *plane), (2, 8, 128)],
        "stress",
        [
            pltpu.VMEM((3, NODES, *plane), F32),
            pltpu.VMEM((3, NODES, 8, 128), F32),
            pltpu.VMEM((3, NODES, 8, 128), F32),
            pltpu.VMEM((9, *plane), F32),
        ],
    )(mid, low, high, far, below, above)
    own_top = stats[0, 0, 0]
    everyone = stats
    for axis in AXES:
        count, hop = lax.axis_size(axis), 1
        while hop < count:
            other = lax.ppermute(everyone, axis, [(i, i ^ hop) for i in range(count)])
            everyone = merged(everyone, other)
            hop *= 2
    rhs, stiff, weight, explicit, field = kernel_call(
        load_kernel,
        [(3, CELLS, *plane), (CELLS, *plane), (CELLS, *plane), (CELLS, *plane), (3, CELLS, *plane)],
        "load",
        [pltpu.VMEM((6, *plane), F32), pltpu.VMEM(plane, F32)],
    )(base, cells, stress, stats)
    adjoint, sens = kernel_call(
        sweeps_kernel,
        [(3, BX, BY, BZ), (BX, BY, BZ)],
        "sweeps",
        [
            pltpu.VMEM((3, CELLS, *plane), F32),
            pltpu.VMEM((6, *plane), F32),
            pltpu.VMEM((9, *plane), F32),
            pltpu.VMEM((12, BY, 128), F32),
            pltpu.VMEM((12, BY, 128), F32),
            pltpu.VMEM((12, BY, 128), F32),
        ],
    )(rhs, stiff, weight, explicit, base, cells, field)
    top, total = everyone[0, 0, 0], everyone[1, 0, 0]
    elements = BX * BY * BZ * lax.axis_size("gx") * lax.axis_size("gy") * lax.axis_size("gz")
    scale = jnp.exp(own_top - top) / total * float(elements)
    aggregate = (top + jnp.log(total)) / power_scale
    return aggregate, scale * adjoint, scale * sens


def solution(mesh):
    placed = (P(None, "gx", "gy", "gz"), P("gx", "gy", "gz"))
    return jax.shard_map(
        on_device,
        mesh=mesh,
        in_specs=placed,
        out_specs=(P(), P(None, "gx", "gy", "gz"), P("gx", "gy", "gz")),
        check_vma=False,
    )
```

time: 389 us -> 132 us (0.34)
  the two profiles are of different devices: /device:TPU:1 before, /device:TPU:2 now
where the time goes in v1:
time: 132 us; the launch traced here: 131 us
  Pallas kernels  50.8 us (38%)
  starting transfers between devices  35.4 us (27%)
  waiting for transfers between devices  35.2 us (27%)
  between operations  5.33 us (4%)
  local copies, waits for them, and re-layouts  3.31 us (3%)
  other arithmetic  1.47 us (1%)
    pallas_call x5, Pallas kernels, run(): pl.pallas_call(body, out_shape=[tile(shape) for shape in outs], in_specs=...  50.8 us
    ppermute x8, starting transfers between devices, on_device(): other = lax.ppermute(everyone, axis, [(i, i ^ hop) for i in range(count)])  19.1 us
    ppermute x7, waiting for transfers between devices, passed(): lax.ppermute(block, axis, [(i, i + distance) for i in range(count) if 0 <...  19 us
    ppermute x7, starting transfers between devices, passed(): lax.ppermute(block, axis, [(i, i + distance) for i in range(count) if 0 <...  16.3 us
    ppermute x8, waiting for transfers between devices, on_device(): other = lax.ppermute(everyone, axis, [(i, i ^ hop) for i in range(count)])  16.2 us
  transfers between devices with their start and end apart: 15, of which 11 were waited for; matrix products, arithmetic and copies ran while one was open for 0% of the time, Pallas kernels for 34%

profile of v1, /device:TPU:2, one launch (start us, length us, event | category | flops | bytes accessed | tf_op | source)
XLA Modules:
  0.0 131.5 jit_solution(8410421218000405506)
XLA Ops:
  0.6 0.0 copy-start
  0.6 0.9 copy-done
  1.6 0.0 copy-start.1
  1.6 0.8 copy-done.1
  2.4 0.2 pack_z.1
  2.6 3.5 %collective-permute-start = (f32[16,8,128]{2,1,0:T(8,128)S(1)}, f32[16,8,128]{2,1,0:T(8,128)S(1)}, u32[]{:S(2)}, u32[]{:S(2)}) collective-permute-start(f32[16,8,128]{2,1,0:T(8,128)S(1)} %get-tuple-element.18), channel_id=1, source_target_pairs={{0,1},{1,2},{2,3},{4,5},{5,6},{6,7},{8,9},{9,10},{10,11},{12,13},{... | collective-permute-start | bytes 196616 | tf_op jit(solution)/shard_map/ppermute | solution.py:447
  6.1 1.3 collective-permute-start.1
  7.4 0.6 collective-permute-done
  7.9 4.3 %collective-permute-done.1 = f32[16,8,128]{2,1,0:T(8,128)S(1)} collective-permute-done((f32[16,8,128]{2,1,0:T(8,128)S(1)}, f32[16,8,128]{2,1,0:T(8,128)S(1)}, u32[]{:S(2)}, u32[]{:S(2)}) %collective-permute-start.1) | collective-permute-done | bytes 65568 | tf_op jit(solution)/shard_map/ppermute | solution.py:447
  12.3 1.3 collective-permute-start.3
  13.6 4.6 %collective-permute-start.2 = (f32[80,8,128]{2,1,0:T(8,128)S(1)}, f32[80,8,128]{2,1,0:T(8,128)S(1)}, u32[]{:S(2)}, u32[]{:S(2)}) collective-permute-start(f32[80,8,128]{2,1,0:T(8,128)S(1)} %pad_maximum_fusion.mid), channel_id=1, source_target_pairs={{0,32},{32,64},{64,96},{96,128},{128,160},{160,192},{192,224},{1,3... | collective-permute-start | bytes 983048 | tf_op jit(solution)/shard_map/ppermute | solution.py:447
  18.2 1.3 collective-permute-start.4
  19.5 6.1 %collective-permute-done.4.far = f32[9,8,128]{2,1,0:T(8,128)S(1)} collective-permute-done((f32[9,8,128]{2,1,0:T(8,128)S(1)}, f32[9,8,128]{2,1,0:T(8,128)S(1)}, u32[]{:S(2)}, u32[]{:S(2)}) %collective-permute-start.4) | collective-permute-done | bytes 36896 | tf_op jit(solution)/shard_map/ppermute | solution.py:447
  25.6 0.0 collective-permute-done.3.high
  25.6 0.0 collective-permute-done.2.low
  25.6 0.2 pack_y.1
  25.8 1.9 %collective-permute-start.6 = (f32[141,8,128]{2,1,0:T(8,128)S(1)}, f32[141,8,128]{2,1,0:T(8,128)S(1)}, u32[]{:S(2)}, u32[]{:S(2)}) collective-permute-start(f32[141,8,128]{2,1,0:T(8,128)S(1)} %get-tuple-element.21), channel_id=1, source_target_pairs={{4,0},{8,4},{12,8},{16,12},{20,16},{24,20},{28,24},{5,1},{9,5},{13... | collective-permute-start | bytes 1732616 | tf_op jit(solution)/shard_map/ppermute | solution.py:447
  27.7 2.4 %collective-permute-start.5 = (f32[126,8,128]{2,1,0:T(8,128)S(1)}, f32[126,8,128]{2,1,0:T(8,128)S(1)}, u32[]{:S(2)}, u32[]{:S(2)}) collective-permute-start(f32[126,8,128]{2,1,0:T(8,128)S(1)} %get-tuple-element.20), channel_id=1, source_target_pairs={{0,4},{4,8},{8,12},{12,16},{16,20},{20,24},{24,28},{1,5},{5,9},{9,... | collective-permute-start | bytes 1548296 | tf_op jit(solution)/shard_map/ppermute | solution.py:447
  30.1 8.0 %collective-permute-done.5.below = f32[126,8,128]{2,1,0:T(8,128)S(1)} collective-permute-done((f32[126,8,128]{2,1,0:T(8,128)S(1)}, f32[126,8,128]{2,1,0:T(8,128)S(1)}, u32[]{:S(2)}, u32[]{:S(2)}) %collective-permute-start.5) | collective-permute-done | bytes 516128 | tf_op jit(solution)/shard_map/ppermute | solution.py:447
  38.1 0.0 collective-permute-done.6.above
  38.1 6.3 %stress.1 = (f32[6,24,40,128]{3,2,1,0:T(8,128)S(1)}, f32[24,40,128]{2,1,0:T(8,128)S(1)}, f32[24,40,128]{2,1,0:T(8,128)S(1)}, f32[2,8,128]{2,1,0:T(8,128)S(1)}) custom-call(f32[80,8,128]{2,1,0:T(8,128)S(1)} %pad_maximum_fusion.mid, f32[80,8,128]{2,1,0:T(8,128)S(1)} %collective-permute-done.2.low, f32[80,8,128]{2,1,0:T(8,128)S(1)} %collective-permute-done.3.high, ...), custom_call_target="tpu_custom_call" | custom-call | flops 1000000 | bytes 1000000 | tf_op jit(solution)/shard_map/stress/pallas_call | solution.py:38
  44.4 2.9 %collective-permute-start.7 = (f32[2,8,128]{2,1,0:T(8,128)S(1)}, f32[2,8,128]{2,1,0:T(8,128)S(1)}, u32[]{:S(2)}, u32[]{:S(2)}) collective-permute-start(f32[2,8,128]{2,1,0:T(8,128)S(1)} %get-tuple-element.22.stats), channel_id=1, source_target_pairs={{0,32},{32,0},{64,96},{96,64},{128,160},{160,128},{192,224},{224,1... | collective-permute-start | bytes 24584 | tf_op jit(solution)/shard_map/ppermute | solution.py:485
  47.3 1.6 %collective-permute-done.7 = f32[2,8,128]{2,1,0:T(8,128)S(1)} collective-permute-done((f32[2,8,128]{2,1,0:T(8,128)S(1)}, f32[2,8,128]{2,1,0:T(8,128)S(1)}, u32[]{:S(2)}, u32[]{:S(2)}) %collective-permute-start.7) | collective-permute-done | bytes 8224 | tf_op jit(solution)/shard_map/ppermute | solution.py:485
  48.9 4.6 %collective-permute-start.8 = (f32[2,8,128]{2,1,0:T(8,128)S(1)}, f32[2,8,128]{2,1,0:T(8,128)S(1)}, u32[]{:S(2)}, u32[]{:S(2)}) collective-permute-start(f32[2,8,128]{2,1,0:T(8,128)S(1)} %pad_maximum_fusion.1), channel_id=1, source_target_pairs={{0,64},{32,96},{64,0},{96,32},{128,192},{160,224},{192,128},{224,1... | collective-permute-start | bytes 24584 | tf_op jit(solution)/shard_map/ppermute | solution.py:485
  53.5 1.6 %collective-permute-done.8 = f32[2,8,128]{2,1,0:T(8,128)S(1)} collective-permute-done((f32[2,8,128]{2,1,0:T(8,128)S(1)}, f32[2,8,128]{2,1,0:T(8,128)S(1)}, u32[]{:S(2)}, u32[]{:S(2)}) %collective-permute-start.8) | collective-permute-done | bytes 8224 | tf_op jit(solution)/shard_map/ppermute | solution.py:485
  55.2 4.6 %collective-permute-start.9 = (f32[2,8,128]{2,1,0:T(8,128)S(1)}, f32[2,8,128]{2,1,0:T(8,128)S(1)}, u32[]{:S(2)}, u32[]{:S(2)}) collective-permute-start(f32[2,8,128]{2,1,0:T(8,128)S(1)} %pad_maximum_fusion.2), channel_id=1, source_target_pairs={{0,128},{32,160},{64,192},{96,224},{128,0},{160,32},{192,64},{224,... | collective-permute-start | bytes 24584 | tf_op jit(solution)/shard_map/ppermute | solution.py:485
  59.8 3.0 %collective-permute-done.9 = f32[2,8,128]{2,1,0:T(8,128)S(1)} collective-permute-done((f32[2,8,128]{2,1,0:T(8,128)S(1)}, f32[2,8,128]{2,1,0:T(8,128)S(1)}, u32[]{:S(2)}, u32[]{:S(2)}) %collective-permute-start.9) | collective-permute-done | bytes 8224 | tf_op jit(solution)/shard_map/ppermute | solution.py:485
  62.8 0.1 collective-permute-start.10
  62.9 1.2 collective-permute-done.10
  64.1 0.1 collective-permute-start.11
  64.2 3.6 %collective-permute-done.11 = f32[2,8,128]{2,1,0:T(8,128)S(1)} collective-permute-done((f32[2,8,128]{2,1,0:T(8,128)S(1)}, f32[2,8,128]{2,1,0:T(8,128)S(1)}, u32[]{:S(2)}, u32[]{:S(2)}) %collective-permute-start.11) | collective-permute-done | bytes 8224 | tf_op jit(solution)/shard_map/ppermute | solution.py:485
  67.9 2.2 %collective-permute-start.12 = (f32[2,8,128]{2,1,0:T(8,128)S(1)}, f32[2,8,128]{2,1,0:T(8,128)S(1)}, u32[]{:S(2)}, u32[]{:S(2)}) collective-permute-start(f32[2,8,128]{2,1,0:T(8,128)S(1)} %pad_maximum_fusion.5), channel_id=1, source_target_pairs={{0,16},{4,20},{8,24},{12,28},{16,0},{20,4},{24,8},{28,12},{1,17},{... | collective-permute-start | bytes 24584 | tf_op jit(solution)/shard_map/ppermute | solution.py:485
  70.1 3.0 %collective-permute-done.12 = f32[2,8,128]{2,1,0:T(8,128)S(1)} collective-permute-done((f32[2,8,128]{2,1,0:T(8,128)S(1)}, f32[2,8,128]{2,1,0:T(8,128)S(1)}, u32[]{:S(2)}, u32[]{:S(2)}) %collective-permute-start.12) | collective-permute-done | bytes 8224 | tf_op jit(solution)/shard_map/ppermute | solution.py:485
  73.1 1.7 %collective-permute-start.13 = (f32[2,8,128]{2,1,0:T(8,128)S(1)}, f32[2,8,128]{2,1,0:T(8,128)S(1)}, u32[]{:S(2)}, u32[]{:S(2)}) collective-permute-start(f32[2,8,128]{2,1,0:T(8,128)S(1)} %pad_maximum_fusion.6), channel_id=1, source_target_pairs={{0,1},{1,0},{2,3},{3,2},{4,5},{5,4},{6,7},{7,6},{8,9},{9,8},{10,11... | collective-permute-start | bytes 24584 | tf_op jit(solution)/shard_map/ppermute | solution.py:485
  74.8 2.1 %collective-permute-done.13 = f32[2,8,128]{2,1,0:T(8,128)S(1)} collective-permute-done((f32[2,8,128]{2,1,0:T(8,128)S(1)}, f32[2,8,128]{2,1,0:T(8,128)S(1)}, u32[]{:S(2)}, u32[]{:S(2)}) %collective-permute-start.13) | collective-permute-done | bytes 8224 | tf_op jit(solution)/shard_map/ppermute | solution.py:485
  76.9 3.0 %collective-permute-start.14 = (f32[2,8,128]{2,1,0:T(8,128)S(1)}, f32[2,8,128]{2,1,0:T(8,128)S(1)}, u32[]{:S(2)}, u32[]{:S(2)}) collective-permute-start(f32[2,8,128]{2,1,0:T(8,128)S(1)} %pad_maximum_fusion.7), channel_id=1, source_target_pairs={{0,2},{1,3},{2,0},{3,1},{4,6},{5,7},{6,4},{7,5},{8,10},{9,11},{10,... | collective-permute-start | bytes 24584 | tf_op jit(solution)/shard_map/ppermute | solution.py:485
  79.8 0.5 slice.134
  80.4 5.0 %load.1 = (f32[3,24,40,128]{3,2,1,0:T(8,128)S(1)}, f32[24,40,128]{2,1,0:T(8,128)S(1)}, f32[24,40,128]{2,1,0:T(8,128)S(1)}, f32[24,40,128]{2,1,0:T(8,128)S(1)}, f32[3,24,40,128]{3,2,1,0:T(8,128)S(1)}) custom-call(f32[6,24,40,128]{3,2,1,0:T(8,128)S(1)} %get-tuple-element.23.base, f32[24,40,128]{2,1,0:T(8,128)S(1)} %get-tuple-element.24.cells, ...), custom_call_target="tpu_custom_call" | custom-call | flops 1000000 | bytes 1000000 | tf_op jit(solution)/shard_map/load/pallas_call | solution.py:38
  85.4 39.2 %sweeps.1 = (f32[3,8,16,128]{3,2,1,0:T(8,128)S(1)}, f32[8,16,128]{2,1,0:T(8,128)S(1)}) custom-call(f32[3,24,40,128]{3,2,1,0:T(8,128)S(1)} %get-tuple-element.26.rhs, f32[24,40,128]{2,1,0:T(8,128)S(1)} %get-tuple-element.27.stiff, f32[24,40,128]{2,1,0:T(8,128)S(1)} %get-tuple-element.28.weight, f32[24,40,128]{2,1,0:T(8,128)S(1)} %get-tuple-element.29.explicit, ...), custom_call_target="tpu_custom_call" | custom-call | flops 1000000 | bytes 1000000 | tf_op jit(solution)/shard_map/sweeps/pallas_call | solution.py:38
  124.6 0.0 collective-permute-done.14
  124.6 0.5 slice.131
  126.5 0.5 slice.133
  129.0 0.7 broadcast_multiply_fusion
  129.7 0.6 broadcast_multiply_fusion.1
  (23 shorter events, 0.2 us)
Async XLA Ops:
  0.6 0.9 copy-start
  1.6 0.8 copy-start.1
  2.6 5.4 %collective-permute-start = (f32[16,8,128]{2,1,0:T(8,128)S(1)}, f32[16,8,128]{2,1,0:T(8,128)S(1)}, u32[]{:S(2)}, u32[]{:S(2)}) collective-permute-start(f32[16,8,128]{2,1,0:T(8,128)S(1)} %get-tuple-element.18), channel_id=1, source_target_pairs={{0,1},{1,2},{2,3},{4,5},{5,6},{6,7},{8,9},{9,10},{10,11},{12,13},{... | collective-permute-start | bytes 196616 | tf_op jit(solution)/shard_map/ppermute | solution.py:447
  6.1 6.2 %collective-permute-start.1 = (f32[16,8,128]{2,1,0:T(8,128)S(1)}, f32[16,8,128]{2,1,0:T(8,128)S(1)}, u32[]{:S(2)}, u32[]{:S(2)}) collective-permute-start(f32[16,8,128]{2,1,0:T(8,128)S(1)} %get-tuple-element.19), channel_id=1, source_target_pairs={{1,0},{2,1},{3,2},{5,4},{6,5},{7,6},{9,8},{10,9},{11,10},{13,12},{... | collective-permute-start | bytes 196616 | tf_op jit(solution)/shard_map/ppermute | solution.py:447
  12.3 13.3 %collective-permute-start.3 = (f32[80,8,128]{2,1,0:T(8,128)S(1)}, f32[80,8,128]{2,1,0:T(8,128)S(1)}, u32[]{:S(2)}, u32[]{:S(2)}) collective-permute-start(f32[80,8,128]{2,1,0:T(8,128)S(1)} %pad_maximum_fusion.mid), channel_id=1, source_target_pairs={{32,0},{64,32},{96,64},{128,96},{160,128},{192,160},{224,192},{33,... | collective-permute-start | bytes 983048 | tf_op jit(solution)/shard_map/ppermute | solution.py:447
  13.6 12.1 %collective-permute-start.2 = (f32[80,8,128]{2,1,0:T(8,128)S(1)}, f32[80,8,128]{2,1,0:T(8,128)S(1)}, u32[]{:S(2)}, u32[]{:S(2)}) collective-permute-start(f32[80,8,128]{2,1,0:T(8,128)S(1)} %pad_maximum_fusion.mid), channel_id=1, source_target_pairs={{0,32},{32,64},{64,96},{96,128},{128,160},{160,192},{192,224},{1,3... | collective-permute-start | bytes 983048 | tf_op jit(solution)/shard_map/ppermute | solution.py:447
  18.2 7.4 %collective-permute-start.4 = (f32[9,8,128]{2,1,0:T(8,128)S(1)}, f32[9,8,128]{2,1,0:T(8,128)S(1)}, u32[]{:S(2)}, u32[]{:S(2)}) collective-permute-start(f32[9,8,128]{2,1,0:T(8,128)S(1)} %constant_dynamic-update-slice_fusion), channel_id=1, source_target_pairs={{64,0},{96,32},{128,64},{160,96},{192,128},{224,160},{65,1},{97,33... | collective-permute-start | bytes 110600 | tf_op jit(solution)/shard_map/ppermute | solution.py:447
  25.8 12.3 %collective-permute-start.6 = (f32[141,8,128]{2,1,0:T(8,128)S(1)}, f32[141,8,128]{2,1,0:T(8,128)S(1)}, u32[]{:S(2)}, u32[]{:S(2)}) collective-permute-start(f32[141,8,128]{2,1,0:T(8,128)S(1)} %get-tuple-element.21), channel_id=1, source_target_pairs={{4,0},{8,4},{12,8},{16,12},{20,16},{24,20},{28,24},{5,1},{9,5},{13... | collective-permute-start | bytes 1732616 | tf_op jit(solution)/shard_map/ppermute | solution.py:447
  27.7 10.4 %collective-permute-start.5 = (f32[126,8,128]{2,1,0:T(8,128)S(1)}, f32[126,8,128]{2,1,0:T(8,128)S(1)}, u32[]{:S(2)}, u32[]{:S(2)}) collective-permute-start(f32[126,8,128]{2,1,0:T(8,128)S(1)} %get-tuple-element.20), channel_id=1, source_target_pairs={{0,4},{4,8},{8,12},{12,16},{16,20},{20,24},{24,28},{1,5},{5,9},{9,... | collective-permute-start | bytes 1548296 | tf_op jit(solution)/shard_map/ppermute | solution.py:447
  44.4 4.5 %collective-permute-start.7 = (f32[2,8,128]{2,1,0:T(8,128)S(1)}, f32[2,8,128]{2,1,0:T(8,128)S(1)}, u32[]{:S(2)}, u32[]{:S(2)}) collective-permute-start(f32[2,8,128]{2,1,0:T(8,128)S(1)} %get-tuple-element.22.stats), channel_id=1, source_target_pairs={{0,32},{32,0},{64,96},{96,64},{128,160},{160,128},{192,224},{224,1... | collective-permute-start | bytes 24584 | tf_op jit(solution)/shard_map/ppermute | solution.py:485
  48.9 6.2 %collective-permute-start.8 = (f32[2,8,128]{2,1,0:T(8,128)S(1)}, f32[2,8,128]{2,1,0:T(8,128)S(1)}, u32[]{:S(2)}, u32[]{:S(2)}) collective-permute-start(f32[2,8,128]{2,1,0:T(8,128)S(1)} %pad_maximum_fusion.1), channel_id=1, source_target_pairs={{0,64},{32,96},{64,0},{96,32},{128,192},{160,224},{192,128},{224,1... | collective-permute-start | bytes 24584 | tf_op jit(solution)/shard_map/ppermute | solution.py:485
  55.2 7.6 %collective-permute-start.9 = (f32[2,8,128]{2,1,0:T(8,128)S(1)}, f32[2,8,128]{2,1,0:T(8,128)S(1)}, u32[]{:S(2)}, u32[]{:S(2)}) collective-permute-start(f32[2,8,128]{2,1,0:T(8,128)S(1)} %pad_maximum_fusion.2), channel_id=1, source_target_pairs={{0,128},{32,160},{64,192},{96,224},{128,0},{160,32},{192,64},{224,... | collective-permute-start | bytes 24584 | tf_op jit(solution)/shard_map/ppermute | solution.py:485
  62.8 1.3 collective-permute-start.10
  64.1 3.7 %collective-permute-start.11 = (f32[2,8,128]{2,1,0:T(8,128)S(1)}, f32[2,8,128]{2,1,0:T(8,128)S(1)}, u32[]{:S(2)}, u32[]{:S(2)}) collective-permute-start(f32[2,8,128]{2,1,0:T(8,128)S(1)} %pad_maximum_fusion.4), channel_id=1, source_target_pairs={{0,8},{4,12},{8,0},{12,4},{16,24},{20,28},{24,16},{28,20},{1,9},{5... | collective-permute-start | bytes 24584 | tf_op jit(solution)/shard_map/ppermute | solution.py:485
  67.9 5.2 %collective-permute-start.12 = (f32[2,8,128]{2,1,0:T(8,128)S(1)}, f32[2,8,128]{2,1,0:T(8,128)S(1)}, u32[]{:S(2)}, u32[]{:S(2)}) collective-permute-start(f32[2,8,128]{2,1,0:T(8,128)S(1)} %pad_maximum_fusion.5), channel_id=1, source_target_pairs={{0,16},{4,20},{8,24},{12,28},{16,0},{20,4},{24,8},{28,12},{1,17},{... | collective-permute-start | bytes 24584 | tf_op jit(solution)/shard_map/ppermute | solution.py:485
  73.1 3.8 %collective-permute-start.13 = (f32[2,8,128]{2,1,0:T(8,128)S(1)}, f32[2,8,128]{2,1,0:T(8,128)S(1)}, u32[]{:S(2)}, u32[]{:S(2)}) collective-permute-start(f32[2,8,128]{2,1,0:T(8,128)S(1)} %pad_maximum_fusion.6), channel_id=1, source_target_pairs={{0,1},{1,0},{2,3},{3,2},{4,5},{5,4},{6,7},{7,6},{8,9},{9,8},{10,11... | collective-permute-start | bytes 24584 | tf_op jit(solution)/shard_map/ppermute | solution.py:485
  76.9 47.7 %collective-permute-start.14 = (f32[2,8,128]{2,1,0:T(8,128)S(1)}, f32[2,8,128]{2,1,0:T(8,128)S(1)}, u32[]{:S(2)}, u32[]{:S(2)}) collective-permute-start(f32[2,8,128]{2,1,0:T(8,128)S(1)} %pad_maximum_fusion.7), channel_id=1, source_target_pairs={{0,2},{1,3},{2,0},{3,1},{4,6},{5,7},{6,4},{7,5},{8,10},{9,11},{10,... | collective-permute-start | bytes 24584 | tf_op jit(solution)/shard_map/ppermute | solution.py:485

commit v2 on v1

--- a/solution.py
+++ b/solution.py
@@ -25,6 +25,8 @@
 ROWS = 40
 F32 = jnp.float32
 VM = 24 * 1024 * 1024
+GROUP = 3
+BUSY = 20_000_000
 
 
 def tile(value):
@@ -78,7 +80,7 @@
     out = [jnp.where(lane == 127, rolled(strip, 127 - 32 * g, 1), moved[g]) for g in range(4)]
     tail = rolled(strip, -1, 1)
     for g in range(4):
-        tail = jnp.where(lane == 32 * g + 31, rolled(moved[g], 32 * g + 32, 1), tail)
+        tail = jnp.where(lane == 32 * g + 31, rolled(main[g], 32 * g + 31, 1), tail)
     return join(out, tail)
 
 
@@ -89,7 +91,7 @@
     out = [jnp.where(lane == 0, rolled(strip, 97 - 32 * g, 1), moved[g]) for g in range(4)]
     tail = rolled(strip, 1, 1)
     for g in range(4):
-        tail = jnp.where(lane == 32 * g, rolled(moved[g], 32 * g, 1), tail)
+        tail = jnp.where(lane == 32 * g, rolled(main[g], 32 * g + 1, 1), tail)
     return join(out, tail)
 
 
@@ -263,7 +265,71 @@
     ]
 
 
-def stress_kernel(mid, low, high, far, below, above, base, cells, stress, stats, disp, line, edge, corners):
+def in_groups(lo, hi, size, body):
+    full = (hi - lo) // size
+
+    def step(i, carry):
+        body(lo + size * i, size)
+        return carry
+
+    if full:
+        lax.fori_loop(0, full, step, 0)
+    if lo + size * full < hi:
+        body(lo + size * full, hi - lo - size * full)
+
+
+def own_kernel(mid, high, above, below, stats):
+    lane = lanes()
+    row = rows()
+
+    def node(c, x):
+        src, i, k = (mid, 8 * c + x, x % 4) if x < 8 else (high, 8 * c, 0)
+        s = 1 if x < 8 else 2
+        x = x % 8
+        strip = src[64 + 4 * c + k]
+        base = 64 if x >= 4 else 0
+        far_strip = above[99 + 8 * s + 2 * c + x % 2]
+        at = 64 * (x // 4) + (32 if k >= 2 else 0)
+        main = [src[2 * i], src[2 * i + 1], above[32 * s + i]]
+        edge = [rolled(strip, 127 - base, 1), rolled(strip, 95 - base, 1), rolled(far_strip, 127 - at, 1)]
+        after = [jnp.where(lane == 127, edge[t], rolled(main[t], -1, 1)) for t in range(3)]
+        both = [after[t] + main[t] for t in range(3)]
+        change = [after[t] - main[t] for t in range(3)]
+
+        def follow(v):
+            turned = [rolled(t, -1, 0) for t in v]
+            return [jnp.where(row == 7, turned[t + 1], turned[t]) for t in range(2)]
+
+        both_next, change_next = follow(both), follow(change)
+        join2 = lambda v: jnp.concatenate(v[:2], axis=0)
+        both, change, both_next, change_next = join2(both), join2(change), join2(both_next), join2(change_next)
+        return both_next + both, both_next - both, change_next + change
+
+    scores = []
+    old = [node(c, 0) for c in range(3)]
+    for x in range(8):
+        new = [node(c, x + 1) for c in range(3)]
+        values = scaled_stress(strain_of(new, old), 0.25 * shear_modulus)
+        old = new
+        dens = mid[48 + 2 * x : 50 + 2 * x].reshape(BY, 128)
+        scores.append(power_scale * jnp.sqrt(dens * mises(values) + 1.0))
+    most = functools.reduce(jnp.maximum, scores)
+    top = jnp.max(most, axis=(0, 1), keepdims=True)
+    total = sum(jnp.exp(score - top) for score in scores)
+    total = jnp.sum(total, axis=(0, 1), keepdims=True)
+    stats[0] = jnp.broadcast_to(top, (8, 128))
+    stats[1] = jnp.broadcast_to(total, (8, 128))
+
+
+def beside(body, ins, outs):
+    def run(*refs):
+        refs[ins + 1 + outs][...] = refs[ins][...]
+        body(*refs[:ins], *refs[ins + 1 : ins + 1 + outs], *refs[ins + 2 + outs :])
+
+    return run
+
+
+def widen_kernel(mid, low, high, far, below, above, disp, line, edge, cells):
     sources = (low, mid, high)
     for p in range(NODES):
         for c in range(4 if p < CELLS else 3):
@@ -275,36 +341,34 @@
                 line[c, p] = beyond[0]
                 edge[c, p] = beyond[1]
 
+
+def stress_kernel(disp, line, edge, cells, base, stress, highest, corners):
     def planes(p):
         return [corner_sums(disp[c, p], (line[c, p], edge[c, p])) for c in range(3)]
 
     put_corners(corners, planes(0))
-
-    def step(p, most):
-        new = planes(p + 1)
-        values = scaled_stress(strain_of(new, get_corners(corners)), 0.25 * shear_modulus)
-        put_corners(corners, new)
-        dens = cells[p]
-        for i in range(6):
-            base[i, p] = values[i]
-        local = jnp.sqrt(dens * mises(values) + 1.0)
-        stress[p] = local
-        return jnp.maximum(most, jnp.where(dens > 0.0, local, 0.0))
-
-    most = lax.fori_loop(0, CELLS, step, jnp.zeros((ROWS, 128), F32))
-    top = power_scale * jnp.max(most, axis=(0, 1), keepdims=True)
-
-    def add(p, total):
-        return total + jnp.exp(power_scale * stress[p, 8:24, :] - top)
-
-    total = lax.fori_loop(8, 16, add, jnp.zeros((BY, 128), F32))
-    total = jnp.sum(total, axis=(0, 1), keepdims=True)
-    stats[0] = jnp.broadcast_to(top, (8, 128))
-    stats[1] = jnp.broadcast_to(total, (8, 128))
-
-
-def load_kernel(base, cells, stress, stats, rhs, stiff, weight, explicit, field, held, kept):
-    top = stats[0, 0:1, 0:1]
+    highest[...] = jnp.zeros((ROWS, 128), F32)
+
+    def step(p, n):
+        news = [get_corners(corners)] + [planes(p + 1 + j) for j in range(n)]
+        most = highest[...]
+        for j in range(n):
+            values = scaled_stress(strain_of(news[j + 1], news[j]), 0.25 * shear_modulus)
+            dens = cells[p + j]
+            for i in range(6):
+                base[i, p + j] = values[i]
+            local = jnp.sqrt(dens * mises(values) + 1.0)
+            stress[p + j] = local
+            most = jnp.maximum(most, jnp.where(dens > 0.0, local, 0.0))
+        highest[...] = most
+        put_corners(corners, news[n])
+
+    in_groups(0, CELLS, GROUP, step)
+
+
+def load_kernel(base, cells, stress, highest, rhs, stiff, weight, explicit, field, reference, held, kept):
+    top = power_scale * jnp.max(highest[...], axis=(0, 1), keepdims=True)
+    reference[...] = jnp.broadcast_to(top, (8, 128))
 
     def element(p):
         dens = cells[p]
@@ -321,30 +385,33 @@
     for i in range(6):
         held[i] = part[i]
     kept[...] = rigid
-
-    def step(p, carry):
-        part, rigid = element(p)
-        load = forces([held[i] for i in range(6)], part)
+    for c in range(3):
+        field[c, 0] = jnp.zeros((ROWS, 128), F32)
+        field[c, CELLS] = jnp.zeros((ROWS, 128), F32)
+
+    def step(p, n):
+        parts = [([held[i] for i in range(6)], kept[...])] + [element(p + j) for j in range(n)]
         for i in range(6):
-            held[i] = part[i]
-        total = kept[...] + rigid
-        kept[...] = rigid
-        total = total + y_prev(total)
-        total = total + z_prev(total)
-        own = jnp.where(cells[p] > 0.0, damping / (diag_factor * total + shift_term), 0.0)
-        weight[p] = own
-        for c in range(3):
-            value = own * load[c]
-            rhs[c, p] = value
-            field[c, p] = value
-        return carry
-
-    lax.fori_loop(1, CELLS, step, 0)
-
-
-def sweep_into(field, rhs, stiff, weight, held, corners, lo, hi):
+            held[i] = parts[n][0][i]
+        kept[...] = parts[n][1]
+        for j in range(n):
+            load = forces(parts[j][0], parts[j + 1][0])
+            total = parts[j][1] + parts[j + 1][1]
+            total = total + y_prev(total)
+            total = total + z_prev(total)
+            own = jnp.where(cells[p + j] > 0.0, damping / (diag_factor * total + shift_term), 0.0)
+            weight[p + j] = own
+            for c in range(3):
+                value = own * load[c]
+                rhs[c, p + j] = value
+                field[c, p + j] = value
+
+    in_groups(1, CELLS, GROUP, step)
+
+
+def sweep_kernel(lo, hi, start, rhs, stiff, weight, field, held, corners):
     def planes(p):
-        return [corner_sums(v) for v in get3(field, p)]
+        return [corner_sums(v) for v in get3(start, p)]
 
     def element(new, old, p):
         return scaled_stress(strain_of(new, old), stiff[p])
@@ -355,20 +422,23 @@
         held[i] = part[i]
     put_corners(corners, second)
 
-    def step(p, carry):
-        new = planes(p + 1)
-        part = element(new, get_corners(corners), p)
-        put_corners(corners, new)
-        force = forces([held[i] for i in range(6)], part)
+    def step(p, n):
+        news = [get_corners(corners)] + [planes(p + 1 + j) for j in range(n)]
+        put_corners(corners, news[n])
+        part = [held[i] for i in range(6)]
+        for j in range(n):
+            here = element(news[j + 1], news[j], p + j)
+            force = forces(part, here)
+            part = here
+            own = weight[p + j]
+            keep = 1.0 - shift_term * own
+            for c in range(3):
+                field[c, p + j] = keep * start[c, p + j] + rhs[c, p + j] - own * force[c]
         for i in range(6):
             held[i] = part[i]
-        own = weight[p]
-        keep = 1.0 - shift_term * own
-        for c in range(3):
-            field[c, p] = keep * field[c, p] + rhs[c, p] - own * force[c]
-        return carry
-
-    lax.fori_loop(lo, hi + 1, step, 0)
+
+    count = -(-(hi + 1 - lo) // GROUP) * GROUP
+    in_groups(lo, lo + count, GROUP, step)
 
 
 def positions(axis, length, cell):
@@ -377,18 +447,15 @@
     return lambda o: ((place + o >= 0) & (place + o < whole)).astype(F32)
 
 
-def sweeps_kernel(rhs, stiff, weight, explicit, base, cells, start, adjoint, sens, field, held, corners, near, side, out):
+def final_kernel(field, explicit, base, cells, reference, everyone, adjoint, sens, aggregate, corners, near, side, out):
+    elements = BX * BY * BZ * lax.axis_size("gx") * lax.axis_size("gy") * lax.axis_size("gz")
+    top, total = everyone[0], everyone[1]
+    scale = jnp.exp(reference[...] - top) / total * float(elements)
+    aggregate[...] = (top + jnp.log(total)) / power_scale
+    scale = jnp.broadcast_to(scale[0:1, 0:1], (BY, 128))
     for c in range(3):
-        for p in range(1, CELLS):
-            field[c, p] = start[c, p]
-    for k in range(1, ITERS):
-        sweep_into(field, rhs, stiff, weight, held, corners, 1 + k, 23 - k)
-    final_part(field, explicit, base, cells, adjoint, sens, corners, near, side, out)
-
-
-def final_part(field, explicit, base, cells, adjoint, sens, corners, near, side, out):
-    for c in range(3):
-        adjoint[c] = field[c, 8:16, 8:24, :]
+        for p in range(8):
+            adjoint[c, p] = scale * field[c, 8 + p, 8:24, :]
 
     row = lax.broadcasted_iota(jnp.int32, (ROWS, 128), 0)
     lane = lax.broadcasted_iota(jnp.int32, (ROWS, 128), 1)
@@ -413,33 +480,34 @@
 
     put_corners(corners, planes(6))
 
-    def step(p, carry):
-        new = planes(p + 1)
-        strain = strain_of(new, get_corners(corners))
-        put_corners(corners, new)
-        dens = cells[p]
-        worked = base[0, p] * strain[0]
-        for i in range(1, 6):
-            worked = worked + base[i, p] * strain[i]
-        raw = explicit[p] - (0.25 * 2.97) * dens * dens * worked
-        in_x = positions("gx", BX, p - 8)
-        hsum = near_0 + near_1 * (in_x(-1) + in_x(1)) + near_2 * (in_x(-2) + in_x(2))
-        value = jnp.where(dens > 0.0, raw / jnp.where(dens > 0.0, hsum, 1.0), 0.0)
-        above, under = z_next(value), z_prev(value)
-        left, right = y_next(value), y_prev(value)
-        row_pair = above + under
-        unit = row_pair + (left + right)
-        corner = y_next(row_pair) + y_prev(row_pair)
-        two = z_next(above) + z_prev(under) + y_next(left) + y_prev(right)
-        near[p - 6] = (2.5 * value + W1 * unit + W2 * corner + W4 * two)[8:24]
-        side[p - 6] = (W1 * value + W2 * unit + W3 * corner)[8:24]
-        out[p - 6] = (W4 * value)[8:24]
-        return carry
-
-    lax.fori_loop(6, 18, step, 0)
+    def step(p, n):
+        news = [get_corners(corners)] + [planes(p + 1 + j) for j in range(n)]
+        put_corners(corners, news[n])
+        for j in range(n):
+            q = p + j
+            strain = strain_of(news[j + 1], news[j])
+            dens = cells[q]
+            worked = base[0, q] * strain[0]
+            for i in range(1, 6):
+                worked = worked + base[i, q] * strain[i]
+            raw = explicit[q] - (0.25 * 2.97) * dens * dens * worked
+            in_x = positions("gx", BX, q - 8)
+            hsum = near_0 + near_1 * (in_x(-1) + in_x(1)) + near_2 * (in_x(-2) + in_x(2))
+            value = jnp.where(dens > 0.0, raw / jnp.where(dens > 0.0, hsum, 1.0), 0.0)
+            above, under = z_next(value), z_prev(value)
+            left, right = y_next(value), y_prev(value)
+            row_pair = above + under
+            unit = row_pair + (left + right)
+            corner = y_next(row_pair) + y_prev(row_pair)
+            two = z_next(above) + z_prev(under) + y_next(left) + y_prev(right)
+            near[q - 6] = (2.5 * value + W1 * unit + W2 * corner + W4 * two)[8:24]
+            side[q - 6] = (W1 * value + W2 * unit + W3 * corner)[8:24]
+            out[q - 6] = (W4 * value)[8:24]
+
+    in_groups(6, 18, GROUP, step)
     for p in range(8):
         q = p + 2
-        sens[p] = near[q] + (side[q - 1] + side[q + 1]) + (out[q - 2] + out[q + 2])
+        sens[p] = scale * (near[q] + (side[q - 1] + side[q + 1]) + (out[q - 2] + out[q + 2]))
 
 
 def passed(block, axis, distance):
@@ -466,49 +534,61 @@
     low, high, far = passed(mid, "gx", 1), passed(mid, "gx", -1), passed(far, "gx", -2)
     up, down = kernel_call(pack_y, [(126, 8, 128), (141, 8, 128)], "pack_y")(mid, low, high, far)
     below, above = passed(up, "gy", 1), passed(down, "gy", -1)
-    base, cells, stress, stats = kernel_call(
+    (known,) = kernel_call(own_kernel, [(2, 8, 128)], "own")(mid, high, above, below)
+    rounds = iter([("gy", 1), ("gy", 2), ("gy", 4), ("gx", 1), ("gx", 2), ("gx", 4), ("gz", 1), ("gz", 2)])
+
+    def under(body, outs, name, scratch, aliases=None):
+        def run(*args):
+            nonlocal known
+            axis, hop = next(rounds)
+            other = lax.ppermute(known, axis, [(i, i ^ hop) for i in range(lax.axis_size(axis))])
+            shapes = [*outs, (2, 8, 128)]
+            call = kernel_call(beside(body, len(args), len(outs)), shapes, name, scratch, BUSY, aliases)
+            *result, mine = call(*args, known)
+            known = merged(mine, other)
+            return result
+
+        return run
+
+    disp, line, edge, cells = under(
+        widen_kernel,
+        [(3, NODES, *plane), (3, NODES, 8, 128), (3, NODES, 8, 128), (CELLS, *plane)],
+        "widen",
+        [],
+    )(mid, low, high, far, below, above)
+    base, stress, highest = under(
         stress_kernel,
-        [(6, CELLS, *plane), (CELLS, *plane), (CELLS, *plane), (2, 8, 128)],
+        [(6, CELLS, *plane), (CELLS, *plane), plane],
         "stress",
-        [
-            pltpu.VMEM((3, NODES, *plane), F32),
-            pltpu.VMEM((3, NODES, 8, 128), F32),
-            pltpu.VMEM((3, NODES, 8, 128), F32),
-            pltpu.VMEM((9, *plane), F32),
-        ],
-    )(mid, low, high, far, below, above)
-    own_top = stats[0, 0, 0]
-    everyone = stats
-    for axis in AXES:
-        count, hop = lax.axis_size(axis), 1
-        while hop < count:
-            other = lax.ppermute(everyone, axis, [(i, i ^ hop) for i in range(count)])
-            everyone = merged(everyone, other)
-            hop *= 2
-    rhs, stiff, weight, explicit, field = kernel_call(
+        [pltpu.VMEM((9, *plane), F32)],
+    )(disp, line, edge, cells)
+    rhs, stiff, weight, explicit, field, reference = under(
         load_kernel,
-        [(3, CELLS, *plane), (CELLS, *plane), (CELLS, *plane), (CELLS, *plane), (3, CELLS, *plane)],
+        [(3, CELLS, *plane), (CELLS, *plane), (CELLS, *plane), (CELLS, *plane), (3, NODES, *plane), (8, 128)],
         "load",
         [pltpu.VMEM((6, *plane), F32), pltpu.VMEM(plane, F32)],
-    )(base, cells, stress, stats)
-    adjoint, sens = kernel_call(
-        sweeps_kernel,
-        [(3, BX, BY, BZ), (BX, BY, BZ)],
-        "sweeps",
+    )(base, cells, stress, highest)
+    for k in range(1, ITERS):
+        (field,) = under(
+            functools.partial(sweep_kernel, 1 + k, 23 - k),
+            [(3, NODES, *plane)],
+            f"sweep{k}",
+            [pltpu.VMEM((6, *plane), F32), pltpu.VMEM((9, *plane), F32)],
+            {0: 0},
+        )(field, rhs, stiff, weight)
+    everyone = known
+    adjoint, sens, aggregate = kernel_call(
+        final_kernel,
+        [(3, BX, BY, BZ), (BX, BY, BZ), (8, 128)],
+        "final",
         [
-            pltpu.VMEM((3, CELLS, *plane), F32),
-            pltpu.VMEM((6, *plane), F32),
             pltpu.VMEM((9, *plane), F32),
             pltpu.VMEM((12, BY, 128), F32),
             pltpu.VMEM((12, BY, 128), F32),
             pltpu.VMEM((12, BY, 128), F32),
         ],
-    )(rhs, stiff, weight, explicit, base, cells, field)
-    top, total = everyone[0, 0, 0], everyone[1, 0, 0]
-    elements = BX * BY * BZ * lax.axis_size("gx") * lax.axis_size("gy") * lax.axis_size("gz")
-    scale = jnp.exp(own_top - top) / total * float(elements)
-    aggregate = (top + jnp.log(total)) / power_scale
-    return aggregate, scale * adjoint, scale * sens
+    )(field, explicit, base, cells, reference, everyone)
+    return aggregate[0, 0], adjoint, sens
 
 
 def solution(mesh):

time: 132 us -> 87 us (0.66)
  Pallas kernels: 50.8 us -> 27.6 us
  waiting for transfers between devices: 35.2 us -> 22.6 us
  between operations: 5.33 us -> 0.97 us
  starting transfers between devices: 35.4 us -> 32.5 us
  other arithmetic: 1.47 us -> 0.14 us
    pallas_call x5 -> x12, Pallas kernels: 50.8 us -> 27.6 us  [run(): pl.pallas_call(body, out_shape=[tile(shape) for shape in outs], in_specs=...]
    ppermute x8, waiting for transfers between devices: 16.2 us -> 3.61 us  [run(): lax.ppermute(known, axis, [(i, i ^ hop) for i in range(lax.axis_size(axis...]
    ppermute x8, starting transfers between devices: 19.1 us -> 16.3 us  [run(): lax.ppermute(known, axis, [(i, i ^ hop) for i in range(lax.axis_size(axis...]
    mul x2 -> x0, other arithmetic: 1.33 us -> none  [on_device(): return (aggregate, scale * adjoint, scale * sens)]
  transfers between devices with their start and end apart: 15 -> 15, of which waited for: 11 -> 7; matrix products, arithmetic and copies ran while one was open for 0% -> 0% of each run, Pallas kernels for 34% -> 28%
where the time goes in v2:
time: 87 us; the launch traced here: 86.1 us
  starting transfers between devices  32.5 us (37%)
  Pallas kernels  27.6 us (32%)
  waiting for transfers between devices  22.6 us (26%)
  local copies, waits for them, and re-layouts  2.29 us (3%)
  between operations  0.97 us (1%)
    pallas_call x12, Pallas kernels, run(): pl.pallas_call(body, out_shape=[tile(shape) for shape in outs], in_specs=...  27.6 us
    ppermute x7, waiting for transfers between devices, passed(): lax.ppermute(block, axis, [(i, i + distance) for i in range(count) if 0 <...  19 us
    ppermute x8, starting transfers between devices, run(): lax.ppermute(known, axis, [(i, i ^ hop) for i in range(lax.axis_size(axis...  16.3 us
    ppermute x7, starting transfers between devices, passed(): lax.ppermute(block, axis, [(i, i + distance) for i in range(count) if 0 <...  16.3 us
    ppermute x8, waiting for transfers between devices, run(): lax.ppermute(known, axis, [(i, i ^ hop) for i in range(lax.axis_size(axis...  3.61 us
    unnamed x9, local copies, waits for them, and re-layouts  1.77 us
  transfers between devices with their start and end apart: 15, of which 7 were waited for; matrix products, arithmetic and copies ran while one was open for 0% of the time, Pallas kernels for 28%

profile of v2, /device:TPU:2, one launch (start us, length us, event | category | flops | bytes accessed | tf_op | source)
XLA Modules:
  0.0 86.1 jit_solution(3937485464326871131)
XLA Ops:
  0.6 0.0 copy-start
  0.6 0.9 %copy-done = f32[3,8,16,128]{3,2,1,0:T(8,128)S(1)} copy-done((f32[3,8,16,128]{3,2,1,0:T(8,128)S(1)}, f32[3,8,16,128]{3,2,1,0:T(8,128)}, u32[]{:S(2)}) %copy-start) | copy-done | bytes 196632
  1.6 0.0 copy-start.1
  1.6 0.8 copy-done.1
  2.4 0.2 pack_z.1
  2.6 3.5 %collective-permute-start = (f32[16,8,128]{2,1,0:T(8,128)S(1)}, f32[16,8,128]{2,1,0:T(8,128)S(1)}, u32[]{:S(2)}, u32[]{:S(2)}) collective-permute-start(f32[16,8,128]{2,1,0:T(8,128)S(1)} %get-tuple-element.36), channel_id=1, source_target_pairs={{0,1},{1,2},{2,3},{4,5},{5,6},{6,7},{8,9},{9,10},{10,11},{12,13},{... | collective-permute-start | bytes 196616 | tf_op jit(solution)/shard_map/ppermute | solution.py:515
  6.1 1.3 %collective-permute-start.1 = (f32[16,8,128]{2,1,0:T(8,128)S(1)}, f32[16,8,128]{2,1,0:T(8,128)S(1)}, u32[]{:S(2)}, u32[]{:S(2)}) collective-permute-start(f32[16,8,128]{2,1,0:T(8,128)S(1)} %get-tuple-element.37), channel_id=1, source_target_pairs={{1,0},{2,1},{3,2},{5,4},{6,5},{7,6},{9,8},{10,9},{11,10},{13,12},{... | collective-permute-start | bytes 196616 | tf_op jit(solution)/shard_map/ppermute | solution.py:515
  7.4 0.6 collective-permute-done
  7.9 4.3 %collective-permute-done.1 = f32[16,8,128]{2,1,0:T(8,128)S(1)} collective-permute-done((f32[16,8,128]{2,1,0:T(8,128)S(1)}, f32[16,8,128]{2,1,0:T(8,128)S(1)}, u32[]{:S(2)}, u32[]{:S(2)}) %collective-permute-start.1) | collective-permute-done | bytes 65568 | tf_op jit(solution)/shard_map/ppermute | solution.py:515
  12.3 1.3 %collective-permute-start.3 = (f32[80,8,128]{2,1,0:T(8,128)S(1)}, f32[80,8,128]{2,1,0:T(8,128)S(1)}, u32[]{:S(2)}, u32[]{:S(2)}) collective-permute-start(f32[80,8,128]{2,1,0:T(8,128)S(1)} %pad_maximum_fusion.mid.refs_0_), channel_id=1, source_target_pairs={{32,0},{64,32},{96,64},{128,96},{160,128},{192,160},{224,192},{33,... | collective-permute-start | bytes 983048 | tf_op jit(solution)/shard_map/ppermute | solution.py:515
  13.6 4.6 %collective-permute-start.2 = (f32[80,8,128]{2,1,0:T(8,128)S(1)}, f32[80,8,128]{2,1,0:T(8,128)S(1)}, u32[]{:S(2)}, u32[]{:S(2)}) collective-permute-start(f32[80,8,128]{2,1,0:T(8,128)S(1)} %pad_maximum_fusion.mid.refs_0_), channel_id=1, source_target_pairs={{0,32},{32,64},{64,96},{96,128},{128,160},{160,192},{192,224},{1,3... | collective-permute-start | bytes 983048 | tf_op jit(solution)/shard_map/ppermute | solution.py:515
  18.2 1.3 %collective-permute-start.4 = (f32[9,8,128]{2,1,0:T(8,128)S(1)}, f32[9,8,128]{2,1,0:T(8,128)S(1)}, u32[]{:S(2)}, u32[]{:S(2)}) collective-permute-start(f32[9,8,128]{2,1,0:T(8,128)S(1)} %constant_dynamic-update-slice_fusion), channel_id=1, source_target_pairs={{64,0},{96,32},{128,64},{160,96},{192,128},{224,160},{65,1},{97,33... | collective-permute-start | bytes 110600 | tf_op jit(solution)/shard_map/ppermute | solution.py:515
  19.5 6.1 %collective-permute-done.4.far.refs_3_ = f32[9,8,128]{2,1,0:T(8,128)S(1)} collective-permute-done((f32[9,8,128]{2,1,0:T(8,128)S(1)}, f32[9,8,128]{2,1,0:T(8,128)S(1)}, u32[]{:S(2)}, u32[]{:S(2)}) %collective-permute-start.4) | collective-permute-done | bytes 36896 | tf_op jit(solution)/shard_map/ppermute | solution.py:515
  25.6 0.0 collective-permute-done.3.high.refs_2_
  25.6 0.0 collective-permute-done.2.low.refs_1_
  25.6 0.2 pack_y.1
  25.8 1.9 %collective-permute-start.6 = (f32[141,8,128]{2,1,0:T(8,128)S(1)}, f32[141,8,128]{2,1,0:T(8,128)S(1)}, u32[]{:S(2)}, u32[]{:S(2)}) collective-permute-start(f32[141,8,128]{2,1,0:T(8,128)S(1)} %get-tuple-element.39), channel_id=1, source_target_pairs={{4,0},{8,4},{12,8},{16,12},{20,16},{24,20},{28,24},{5,1},{9,5},{13... | collective-permute-start | bytes 1732616 | tf_op jit(solution)/shard_map/ppermute | solution.py:515
  27.7 2.4 %collective-permute-start.5 = (f32[126,8,128]{2,1,0:T(8,128)S(1)}, f32[126,8,128]{2,1,0:T(8,128)S(1)}, u32[]{:S(2)}, u32[]{:S(2)}) collective-permute-start(f32[126,8,128]{2,1,0:T(8,128)S(1)} %get-tuple-element.38), channel_id=1, source_target_pairs={{0,4},{4,8},{8,12},{12,16},{16,20},{20,24},{24,28},{1,5},{5,9},{9,... | collective-permute-start | bytes 1548296 | tf_op jit(solution)/shard_map/ppermute | solution.py:515
  30.1 8.0 %collective-permute-done.5.below.refs_4_ = f32[126,8,128]{2,1,0:T(8,128)S(1)} collective-permute-done((f32[126,8,128]{2,1,0:T(8,128)S(1)}, f32[126,8,128]{2,1,0:T(8,128)S(1)}, u32[]{:S(2)}, u32[]{:S(2)}) %collective-permute-start.5) | collective-permute-done | bytes 516128 | tf_op jit(solution)/shard_map/ppermute | solution.py:515
  38.1 0.0 collective-permute-done.6.above.refs_5_
  38.1 0.6 own.1.refs_6_
  38.7 0.1 collective-permute-start.7
  38.8 0.4 widen.1
  39.2 0.7 collective-permute-done.7
  40.0 0.1 collective-permute-start.8
  40.1 4.0 %stress.1 = (f32[6,24,40,128]{3,2,1,0:T(8,128)S(1)}, f32[24,40,128]{2,1,0:T(8,128)S(1)}, f32[40,128]{1,0:T(8,128)S(1)}, f32[2,8,128]{2,1,0:T(8,128)S(1)}) custom-call(f32[3,25,40,128]{3,2,1,0:T(8,128)S(1)} %get-tuple-element.40.refs_0_, f32[3,25,8,128]{3,2,1,0:T(8,128)S(1)} %get-tuple-element.41.refs_1_, f32[3,25,8,128]{3,2,1,0:T(8,128)S(1)} %get-tuple-element.42.refs_2_, ...), custom_call_target="tpu_custom_call" | custom-call | flops 20000000 | bytes 1000000 | tf_op jit(solution)/shard_map/stress/pallas_call | solution.py:40
  44.1 0.0 collective-permute-done.8
  44.2 3.0 %collective-permute-start.9 = (f32[2,8,128]{2,1,0:T(8,128)S(1)}, f32[2,8,128]{2,1,0:T(8,128)S(1)}, u32[]{:S(2)}, u32[]{:S(2)}) collective-permute-start(f32[2,8,128]{2,1,0:T(8,128)S(1)} %pad_maximum_fusion.2.refs_4_), channel_id=1, source_target_pairs={{0,16},{4,20},{8,24},{12,28},{16,0},{20,4},{24,8},{28,12},{1,17},{... | collective-permute-start | bytes 24584 | tf_op jit(solution)/shard_map/ppermute | solution.py:544
  47.2 3.1 %load.1 = (f32[3,24,40,128]{3,2,1,0:T(8,128)S(1)}, f32[24,40,128]{2,1,0:T(8,128)S(1)}, f32[24,40,128]{2,1,0:T(8,128)S(1)}, f32[24,40,128]{2,1,0:T(8,128)S(1)}, f...) custom-call(f32[6,24,40,128]{3,2,1,0:T(8,128)S(1)} %get-tuple-element.45.refs_0_.base, ...), custom_call_target="tpu_custom_call" | custom-call | flops 20000000 | bytes 1000000 | tf_op jit(solution)/shard_map/load/pallas_call | solution.py:40
  50.3 0.0 collective-permute-done.9
  50.4 2.9 %collective-permute-start.10 = (f32[2,8,128]{2,1,0:T(8,128)S(1)}, f32[2,8,128]{2,1,0:T(8,128)S(1)}, u32[]{:S(2)}, u32[]{:S(2)}) collective-permute-start(f32[2,8,128]{2,1,0:T(8,128)S(1)} %pad_maximum_fusion.3.refs_4_), channel_id=1, source_target_pairs={{0,32},{32,0},{64,96},{96,64},{128,160},{160,128},{192,224},{224,1... | collective-permute-start | bytes 24584 | tf_op jit(solution)/shard_map/ppermute | solution.py:544
  53.2 3.8 %sweep1.1 = (f32[3,25,40,128]{3,2,1,0:T(8,128)S(1)}, f32[2,8,128]{2,1,0:T(8,128)S(1)}) custom-call(f32[3,25,40,128]{3,2,1,0:T(8,128)S(1)} %get-tuple-element.49.refs_0_, f32[3,24,40,128]{3,2,1,0:T(8,128)S(1)} %get-tuple-element.50.refs_1_, f32[24,40,128]{2,1,0:T(8,128)S(1)} %get-tuple-element.51.refs_2_, ...), custom_call_target="tpu_custom_call", output_to_operand_aliasing={{0}: (0, {})} | custom-call | flops 20000000 | bytes 1000000 | tf_op jit(solution)/shard_map/sweep1/pallas_call | solution.py:40
  57.1 0.0 collective-permute-done.10
  57.1 4.6 %collective-permute-start.11 = (f32[2,8,128]{2,1,0:T(8,128)S(1)}, f32[2,8,128]{2,1,0:T(8,128)S(1)}, u32[]{:S(2)}, u32[]{:S(2)}) collective-permute-start(f32[2,8,128]{2,1,0:T(8,128)S(1)} %pad_maximum_fusion.4.refs_4_), channel_id=1, source_target_pairs={{0,64},{32,96},{64,0},{96,32},{128,192},{160,224},{192,128},{224,1... | collective-permute-start | bytes 24584 | tf_op jit(solution)/shard_map/ppermute | solution.py:544
  61.7 3.8 %sweep2.1 = (f32[3,25,40,128]{3,2,1,0:T(8,128)S(1)}, f32[2,8,128]{2,1,0:T(8,128)S(1)}) custom-call(f32[3,25,40,128]{3,2,1,0:T(8,128)S(1)} %get-tuple-element.54.refs_0_, f32[3,24,40,128]{3,2,1,0:T(8,128)S(1)} %get-tuple-element.50.refs_1_, f32[24,40,128]{2,1,0:T(8,128)S(1)} %get-tuple-element.51.refs_2_, ...), custom_call_target="tpu_custom_call", output_to_operand_aliasing={{0}: (0, {})} | custom-call | flops 20000000 | bytes 1000000 | tf_op jit(solution)/shard_map/sweep2/pallas_call | solution.py:40
  65.5 0.0 collective-permute-done.11
  65.5 1.7 %collective-permute-start.12 = (f32[2,8,128]{2,1,0:T(8,128)S(1)}, f32[2,8,128]{2,1,0:T(8,128)S(1)}, u32[]{:S(2)}, u32[]{:S(2)}) collective-permute-start(f32[2,8,128]{2,1,0:T(8,128)S(1)} %pad_maximum_fusion.5.refs_4_), channel_id=1, source_target_pairs={{0,128},{32,160},{64,192},{96,224},{128,0},{160,32},{192,64},{224,... | collective-permute-start | bytes 24584 | tf_op jit(solution)/shard_map/ppermute | solution.py:544
  67.2 3.3 %sweep3.1 = (f32[3,25,40,128]{3,2,1,0:T(8,128)S(1)}, f32[2,8,128]{2,1,0:T(8,128)S(1)}) custom-call(f32[3,25,40,128]{3,2,1,0:T(8,128)S(1)} %get-tuple-element.56.refs_0_, f32[3,24,40,128]{3,2,1,0:T(8,128)S(1)} %get-tuple-element.50.refs_1_, f32[24,40,128]{2,1,0:T(8,128)S(1)} %get-tuple-element.51.refs_2_, ...), custom_call_target="tpu_custom_call", output_to_operand_aliasing={{0}: (0, {})} | custom-call | flops 20000000 | bytes 1000000 | tf_op jit(solution)/shard_map/sweep3/pallas_call | solution.py:40
  70.5 2.7 %collective-permute-done.12 = f32[2,8,128]{2,1,0:T(8,128)S(1)} collective-permute-done((f32[2,8,128]{2,1,0:T(8,128)S(1)}, f32[2,8,128]{2,1,0:T(8,128)S(1)}, u32[]{:S(2)}, u32[]{:S(2)}) %collective-permute-start.12) | collective-permute-done | bytes 8224 | tf_op jit(solution)/shard_map/ppermute | solution.py:544
  73.2 1.7 %collective-permute-start.13 = (f32[2,8,128]{2,1,0:T(8,128)S(1)}, f32[2,8,128]{2,1,0:T(8,128)S(1)}, u32[]{:S(2)}, u32[]{:S(2)}) collective-permute-start(f32[2,8,128]{2,1,0:T(8,128)S(1)} %pad_maximum_fusion.6.refs_4_), channel_id=1, source_target_pairs={{0,1},{1,0},{2,3},{3,2},{4,5},{5,4},{6,7},{7,6},{8,9},{9,8},{10,11... | collective-permute-start | bytes 24584 | tf_op jit(solution)/shard_map/ppermute | solution.py:544
  74.9 2.8 %sweep4.1 = (f32[3,25,40,128]{3,2,1,0:T(8,128)S(1)}, f32[2,8,128]{2,1,0:T(8,128)S(1)}) custom-call(f32[3,25,40,128]{3,2,1,0:T(8,128)S(1)} %get-tuple-element.58.refs_0_, f32[3,24,40,128]{3,2,1,0:T(8,128)S(1)} %get-tuple-element.50.refs_1_, f32[24,40,128]{2,1,0:T(8,128)S(1)} %get-tuple-element.51.refs_2_, ...), custom_call_target="tpu_custom_call", output_to_operand_aliasing={{0}: (0, {})} | custom-call | flops 20000000 | bytes 1000000 | tf_op jit(solution)/shard_map/sweep4/pallas_call | solution.py:40
  77.6 0.0 collective-permute-done.13
  77.7 2.3 %collective-permute-start.14 = (f32[2,8,128]{2,1,0:T(8,128)S(1)}, f32[2,8,128]{2,1,0:T(8,128)S(1)}, u32[]{:S(2)}, u32[]{:S(2)}) collective-permute-start(f32[2,8,128]{2,1,0:T(8,128)S(1)} %pad_maximum_fusion.7.refs_4_), channel_id=1, source_target_pairs={{0,2},{1,3},{2,0},{3,1},{4,6},{5,7},{6,4},{7,5},{8,10},{9,11},{10,... | collective-permute-start | bytes 24584 | tf_op jit(solution)/shard_map/ppermute | solution.py:544
  79.9 2.8 %sweep5.1 = (f32[3,25,40,128]{3,2,1,0:T(8,128)S(1)}, f32[2,8,128]{2,1,0:T(8,128)S(1)}) custom-call(f32[3,25,40,128]{3,2,1,0:T(8,128)S(1)} %get-tuple-element.60.refs_0_, f32[3,24,40,128]{3,2,1,0:T(8,128)S(1)} %get-tuple-element.50.refs_1_, f32[24,40,128]{2,1,0:T(8,128)S(1)} %get-tuple-element.51.refs_2_, ...), custom_call_target="tpu_custom_call", output_to_operand_aliasing={{0}: (0, {})} | custom-call | flops 20000000 | bytes 1000000 | tf_op jit(solution)/shard_map/sweep5/pallas_call | solution.py:40
  82.7 0.2 collective-permute-done.14
  82.9 2.7 %final.1 = (f32[3,8,16,128]{3,2,1,0:T(8,128)}, f32[8,16,128]{2,1,0:T(8,128)}, f32[8,128]{1,0:T(8,128)S(1)}) custom-call(f32[3,25,40,128]{3,2,1,0:T(8,128)S(1)} %get-tuple-element.62.field, f32[24,40,128]{2,1,0:T(8,128)S(1)} %get-tuple-element.63.explicit, f32[6,24,40,128]{3,2,1,0:T(8,128)S(1)} %get-tuple-element.45.refs_0_.base, ...), custom_call_target="tpu_custom_call" | custom-call | flops 1000000 | bytes 1000000 | tf_op jit(solution)/shard_map/final/pallas_call | solution.py:40
  85.6 0.5 slice.203
  (24 shorter events, 0.2 us)
Async XLA Ops:
  0.6 0.9 %copy-start = (f32[3,8,16,128]{3,2,1,0:T(8,128)S(1)}, f32[3,8,16,128]{3,2,1,0:T(8,128)}, u32[]{:S(2)}) copy-start(f32[3,8,16,128]{3,2,1,0:T(8,128)} %disp.1) | copy-start | bytes 589828
  1.6 0.8 copy-start.1
  2.6 5.4 %collective-permute-start = (f32[16,8,128]{2,1,0:T(8,128)S(1)}, f32[16,8,128]{2,1,0:T(8,128)S(1)}, u32[]{:S(2)}, u32[]{:S(2)}) collective-permute-start(f32[16,8,128]{2,1,0:T(8,128)S(1)} %get-tuple-element.36), channel_id=1, source_target_pairs={{0,1},{1,2},{2,3},{4,5},{5,6},{6,7},{8,9},{9,10},{10,11},{12,13},{... | collective-permute-start | bytes 196616 | tf_op jit(solution)/shard_map/ppermute | solution.py:515
  6.1 6.2 %collective-permute-start.1 = (f32[16,8,128]{2,1,0:T(8,128)S(1)}, f32[16,8,128]{2,1,0:T(8,128)S(1)}, u32[]{:S(2)}, u32[]{:S(2)}) collective-permute-start(f32[16,8,128]{2,1,0:T(8,128)S(1)} %get-tuple-element.37), channel_id=1, source_target_pairs={{1,0},{2,1},{3,2},{5,4},{6,5},{7,6},{9,8},{10,9},{11,10},{13,12},{... | collective-permute-start | bytes 196616 | tf_op jit(solution)/shard_map/ppermute | solution.py:515
  12.3 13.3 %collective-permute-start.3 = (f32[80,8,128]{2,1,0:T(8,128)S(1)}, f32[80,8,128]{2,1,0:T(8,128)S(1)}, u32[]{:S(2)}, u32[]{:S(2)}) collective-permute-start(f32[80,8,128]{2,1,0:T(8,128)S(1)} %pad_maximum_fusion.mid.refs_0_), channel_id=1, source_target_pairs={{32,0},{64,32},{96,64},{128,96},{160,128},{192,160},{224,192},{33,... | collective-permute-start | bytes 983048 | tf_op jit(solution)/shard_map/ppermute | solution.py:515
  13.6 12.1 %collective-permute-start.2 = (f32[80,8,128]{2,1,0:T(8,128)S(1)}, f32[80,8,128]{2,1,0:T(8,128)S(1)}, u32[]{:S(2)}, u32[]{:S(2)}) collective-permute-start(f32[80,8,128]{2,1,0:T(8,128)S(1)} %pad_maximum_fusion.mid.refs_0_), channel_id=1, source_target_pairs={{0,32},{32,64},{64,96},{96,128},{128,160},{160,192},{192,224},{1,3... | collective-permute-start | bytes 983048 | tf_op jit(solution)/shard_map/ppermute | solution.py:515
  18.2 7.4 %collective-permute-start.4 = (f32[9,8,128]{2,1,0:T(8,128)S(1)}, f32[9,8,128]{2,1,0:T(8,128)S(1)}, u32[]{:S(2)}, u32[]{:S(2)}) collective-permute-start(f32[9,8,128]{2,1,0:T(8,128)S(1)} %constant_dynamic-update-slice_fusion), channel_id=1, source_target_pairs={{64,0},{96,32},{128,64},{160,96},{192,128},{224,160},{65,1},{97,33... | collective-permute-start | bytes 110600 | tf_op jit(solution)/shard_map/ppermute | solution.py:515
  25.8 12.3 %collective-permute-start.6 = (f32[141,8,128]{2,1,0:T(8,128)S(1)}, f32[141,8,128]{2,1,0:T(8,128)S(1)}, u32[]{:S(2)}, u32[]{:S(2)}) collective-permute-start(f32[141,8,128]{2,1,0:T(8,128)S(1)} %get-tuple-element.39), channel_id=1, source_target_pairs={{4,0},{8,4},{12,8},{16,12},{20,16},{24,20},{28,24},{5,1},{9,5},{13... | collective-permute-start | bytes 1732616 | tf_op jit(solution)/shard_map/ppermute | solution.py:515
  27.7 10.4 %collective-permute-start.5 = (f32[126,8,128]{2,1,0:T(8,128)S(1)}, f32[126,8,128]{2,1,0:T(8,128)S(1)}, u32[]{:S(2)}, u32[]{:S(2)}) collective-permute-start(f32[126,8,128]{2,1,0:T(8,128)S(1)} %get-tuple-element.38), channel_id=1, source_target_pairs={{0,4},{4,8},{8,12},{12,16},{16,20},{20,24},{24,28},{1,5},{5,9},{9,... | collective-permute-start | bytes 1548296 | tf_op jit(solution)/shard_map/ppermute | solution.py:515
  38.7 1.3 %collective-permute-start.7 = (f32[2,8,128]{2,1,0:T(8,128)S(1)}, f32[2,8,128]{2,1,0:T(8,128)S(1)}, u32[]{:S(2)}, u32[]{:S(2)}) collective-permute-start(f32[2,8,128]{2,1,0:T(8,128)S(1)} %own.1.refs_6_), channel_id=1, source_target_pairs={{0,4},{4,0},{8,12},{12,8},{16,20},{20,16},{24,28},{28,24},{1,5},{5... | collective-permute-start | bytes 24584 | tf_op jit(solution)/shard_map/ppermute | solution.py:544
  40.0 4.2 %collective-permute-start.8 = (f32[2,8,128]{2,1,0:T(8,128)S(1)}, f32[2,8,128]{2,1,0:T(8,128)S(1)}, u32[]{:S(2)}, u32[]{:S(2)}) collective-permute-start(f32[2,8,128]{2,1,0:T(8,128)S(1)} %pad_maximum_fusion.1.refs_4_), channel_id=1, source_target_pairs={{0,8},{4,12},{8,0},{12,4},{16,24},{20,28},{24,16},{28,20},{1,9},{5... | collective-permute-start | bytes 24584 | tf_op jit(solution)/shard_map/ppermute | solution.py:544
  44.2 6.2 %collective-permute-start.9 = (f32[2,8,128]{2,1,0:T(8,128)S(1)}, f32[2,8,128]{2,1,0:T(8,128)S(1)}, u32[]{:S(2)}, u32[]{:S(2)}) collective-permute-start(f32[2,8,128]{2,1,0:T(8,128)S(1)} %pad_maximum_fusion.2.refs_4_), channel_id=1, source_target_pairs={{0,16},{4,20},{8,24},{12,28},{16,0},{20,4},{24,8},{28,12},{1,17},{... | collective-permute-start | bytes 24584 | tf_op jit(solution)/shard_map/ppermute | solution.py:544
  50.4 6.7 %collective-permute-start.10 = (f32[2,8,128]{2,1,0:T(8,128)S(1)}, f32[2,8,128]{2,1,0:T(8,128)S(1)}, u32[]{:S(2)}, u32[]{:S(2)}) collective-permute-start(f32[2,8,128]{2,1,0:T(8,128)S(1)} %pad_maximum_fusion.3.refs_4_), channel_id=1, source_target_pairs={{0,32},{32,0},{64,96},{96,64},{128,160},{160,128},{192,224},{224,1... | collective-permute-start | bytes 24584 | tf_op jit(solution)/shard_map/ppermute | solution.py:544
  57.1 8.4 %collective-permute-start.11 = (f32[2,8,128]{2,1,0:T(8,128)S(1)}, f32[2,8,128]{2,1,0:T(8,128)S(1)}, u32[]{:S(2)}, u32[]{:S(2)}) collective-permute-start(f32[2,8,128]{2,1,0:T(8,128)S(1)} %pad_maximum_fusion.4.refs_4_), channel_id=1, source_target_pairs={{0,64},{32,96},{64,0},{96,32},{128,192},{160,224},{192,128},{224,1... | collective-permute-start | bytes 24584 | tf_op jit(solution)/shard_map/ppermute | solution.py:544
  65.5 7.6 %collective-permute-start.12 = (f32[2,8,128]{2,1,0:T(8,128)S(1)}, f32[2,8,128]{2,1,0:T(8,128)S(1)}, u32[]{:S(2)}, u32[]{:S(2)}) collective-permute-start(f32[2,8,128]{2,1,0:T(8,128)S(1)} %pad_maximum_fusion.5.refs_4_), channel_id=1, source_target_pairs={{0,128},{32,160},{64,192},{96,224},{128,0},{160,32},{192,64},{224,... | collective-permute-start | bytes 24584 | tf_op jit(solution)/shard_map/ppermute | solution.py:544
  73.2 4.4 %collective-permute-start.13 = (f32[2,8,128]{2,1,0:T(8,128)S(1)}, f32[2,8,128]{2,1,0:T(8,128)S(1)}, u32[]{:S(2)}, u32[]{:S(2)}) collective-permute-start(f32[2,8,128]{2,1,0:T(8,128)S(1)} %pad_maximum_fusion.6.refs_4_), channel_id=1, source_target_pairs={{0,1},{1,0},{2,3},{3,2},{4,5},{5,4},{6,7},{7,6},{8,9},{9,8},{10,11... | collective-permute-start | bytes 24584 | tf_op jit(solution)/shard_map/ppermute | solution.py:544
  77.7 5.2 %collective-permute-start.14 = (f32[2,8,128]{2,1,0:T(8,128)S(1)}, f32[2,8,128]{2,1,0:T(8,128)S(1)}, u32[]{:S(2)}, u32[]{:S(2)}) collective-permute-start(f32[2,8,128]{2,1,0:T(8,128)S(1)} %pad_maximum_fusion.7.refs_4_), channel_id=1, source_target_pairs={{0,2},{1,3},{2,0},{3,1},{4,6},{5,7},{6,4},{7,5},{8,10},{9,11},{10,... | collective-permute-start | bytes 24584 | tf_op jit(solution)/shard_map/ppermute | solution.py:544

commit v3 on v2

--- a/solution.py
+++ b/solution.py
@@ -133,39 +133,47 @@
             down[4 * c + k] = bottom
 
 
+def masked(value, real):
+    return value if real is None else value * real
+
+
 def pack_y(mid, low, high, far, up, down):
     lane = lanes()
     odd = (lane // 32) % 2 == 1
     sources = (low, mid, high)
     for s, src in enumerate(sources):
+        real = None if s == 1 else within("gx", s - 1)
         for i in range(32):
-            up[32 * s + i] = src[2 * i + 1]
-            down[32 * s + i] = src[2 * i]
+            up[32 * s + i] = masked(src[2 * i + 1], real)
+            down[32 * s + i] = masked(src[2 * i], real)
         for c in range(4):
             for k in range(2):
                 first, second = src[64 + 4 * c + k], src[64 + 4 * c + k + 2]
-                up[99 + 8 * s + 2 * c + k] = jnp.where(odd, first, rolled(second, -32, 1))
-                down[99 + 8 * s + 2 * c + k] = jnp.where(odd, rolled(second, 32, 1), first)
+                up[99 + 8 * s + 2 * c + k] = masked(jnp.where(odd, first, rolled(second, -32, 1)), real)
+                down[99 + 8 * s + 2 * c + k] = masked(jnp.where(odd, rolled(second, 32, 1), first), real)
         for i in range(24):
             r = 24 * s + i
-            down[126 + r // 8, r % 8 : r % 8 + 1, :] = src[2 * i + 1, 0:1, :]
+            down[126 + r // 8, r % 8 : r % 8 + 1, :] = masked(src[2 * i + 1, 0:1, :], real)
         for i in range(12):
             r = 12 * s + i
-            down[136 + r // 8, r % 8 : r % 8 + 1, :] = src[64 + i, 0:1, :]
+            down[136 + r // 8, r % 8 : r % 8 + 1, :] = masked(src[64 + i, 0:1, :], real)
+    real = within("gx", 2)
     for c in range(3):
-        up[96 + c] = far[2 * c + 1]
-        down[96 + c] = far[2 * c]
-        up[123 + c] = far[6 + c]
-        down[123 + c] = far[6 + c]
+        up[96 + c] = masked(far[2 * c + 1], real)
+        down[96 + c] = masked(far[2 * c], real)
+        up[123 + c] = masked(far[6 + c], real)
+        down[123 + c] = masked(far[6 + c], real)
         r = 72 + c
-        down[126 + r // 8, r % 8 : r % 8 + 1, :] = far[2 * c + 1, 0:1, :]
+        down[126 + r // 8, r % 8 : r % 8 + 1, :] = masked(far[2 * c + 1, 0:1, :], real)
         r = 36 + c
-        down[136 + r // 8, r % 8 : r % 8 + 1, :] = far[6 + c, 0:1, :]
+        down[136 + r // 8, r % 8 : r % 8 + 1, :] = masked(far[6 + c, 0:1, :], real)
 
 
 def unpacked(c, p, sources, far, below, above):
     lane = lanes()
     group = lane // 32
+    real = (within("gx", -1), None, within("gx", 1), within("gx", 2))[p // 8]
+    lower, upper = within("gy", -1), within("gy", 1)
     if p < 24:
         s, x = divmod(p, 8)
         src, i, k = sources[s], 8 * c + x, x % 4
@@ -182,12 +190,13 @@
         over = rolled(above[123 + c], 96, 1)
         main = [below[96 + c], far[2 * c], far[2 * c + 1], above[96 + c]]
         r, q, turn = 72 + c, 36 + c, 64
-    strip = jnp.where(group == 0, under, jnp.where(group == 3, over, own))
+    main = [main[0] * lower, masked(main[1], real), masked(main[2], real), main[3] * upper]
+    strip = jnp.where(group == 0, under * lower, jnp.where(group == 3, over * upper, masked(own, real)))
     if c == 3:
         return join(main, strip), None
     line = jnp.broadcast_to(above[126 + r // 8, r % 8 : r % 8 + 1, :], (8, 128))
     edge = jnp.broadcast_to(above[136 + q // 8, q % 8 : q % 8 + 1, :], (8, 128))
-    return join(main, strip), (line, rolled(edge, turn, 1))
+    return join(main, strip), (line * upper, rolled(edge, turn, 1) * upper)
 
 
 def corner_sums(value, beyond=None):
@@ -290,7 +299,10 @@
         base = 64 if x >= 4 else 0
         far_strip = above[99 + 8 * s + 2 * c + x % 2]
         at = 64 * (x // 4) + (32 if k >= 2 else 0)
-        main = [src[2 * i], src[2 * i + 1], above[32 * s + i]]
+        real = None if s == 1 else within("gx", 1)
+        upper = within("gy", 1)
+        main = [masked(src[2 * i], real), masked(src[2 * i + 1], real), above[32 * s + i] * upper]
+        strip, far_strip = masked(strip, real), far_strip * upper
         edge = [rolled(strip, 127 - base, 1), rolled(strip, 95 - base, 1), rolled(far_strip, 127 - at, 1)]
         after = [jnp.where(lane == 127, edge[t], rolled(main[t], -1, 1)) for t in range(3)]
         both = [after[t] + main[t] for t in range(3)]
@@ -512,7 +524,12 @@
 
 def passed(block, axis, distance):
     count = lax.axis_size(axis)
-    return lax.ppermute(block, axis, [(i, i + distance) for i in range(count) if 0 <= i + distance < count])
+    return lax.ppermute(block, axis, [(i, (i + distance) % count) for i in range(count)])
+
+
+def within(axis, distance):
+    place = lax.axis_index(axis) + distance
+    return ((place >= 0) & (place < lax.axis_size(axis))).astype(F32)
 
 
 def merged(mine, other):
@@ -527,8 +544,9 @@
     plane = (ROWS, 128)
     up, down = kernel_call(pack_z, [(16, 8, 128)] * 2, "pack_z")(displacement, density)
     below_z, above_z = passed(up, "gz", 1), passed(down, "gz", -1)
+    strips = below_z * within("gz", -1) + above_z * within("gz", 1)
     mid = jnp.concatenate(
-        [displacement.reshape(48, 8, 128), density.reshape(16, 8, 128), below_z + above_z], axis=0
+        [displacement.reshape(48, 8, 128), density.reshape(16, 8, 128), strips], axis=0
     )
     far = jnp.concatenate([mid[t : t + n] for t, n in ((0, 2), (16, 2), (32, 2), (64, 1), (68, 1), (72, 1))], axis=0)
     low, high, far = passed(mid, "gx", 1), passed(mid, "gx", -1), passed(far, "gx", -2)

time: 87 us -> 76.5 us (0.88)
  starting transfers between devices: 32.5 us -> 26 us
  waiting for transfers between devices: 22.6 us -> 19.5 us
    ppermute x7, starting transfers between devices: 16.3 us -> 12.2 us  [passed(): lax.ppermute(block, axis, [(i, (i + distance) % count) for i in range(cou...]
    ppermute x8, starting transfers between devices: 16.3 us -> 13.7 us  [run(): lax.ppermute(known, axis, [(i, i ^ hop) for i in range(lax.axis_size(axis...]
    ppermute x7, waiting for transfers between devices: 19 us -> 17.1 us  [passed(): lax.ppermute(block, axis, [(i, (i + distance) % count) for i in range(cou...]
    ppermute x8, waiting for transfers between devices: 3.61 us -> 2.35 us  [run(): lax.ppermute(known, axis, [(i, i ^ hop) for i in range(lax.axis_size(axis...]
  transfers between devices with their start and end apart: 15 -> 15, of which waited for: 7 -> 8; matrix products, arithmetic and copies ran while one was open for 0% -> 0% of each run, Pallas kernels for 28% -> 31%
where the time goes in v3:
time: 76.5 us; the launch traced here: 76.3 us
  Pallas kernels  27.6 us (36%)
  starting transfers between devices  26 us (34%)
  waiting for transfers between devices  19.5 us (25%)
  local copies, waits for them, and re-layouts  2.28 us (3%)
  between operations  0.88 us (1%)
    pallas_call x12, Pallas kernels, run(): pl.pallas_call(body, out_shape=[tile(shape) for shape in outs], in_specs=...  27.6 us
    ppermute x7, waiting for transfers between devices, passed(): lax.ppermute(block, axis, [(i, (i + distance) % count) for i in range(cou...  17.1 us
    ppermute x8, starting transfers between devices, run(): lax.ppermute(known, axis, [(i, i ^ hop) for i in range(lax.axis_size(axis...  13.7 us
    ppermute x7, starting transfers between devices, passed(): lax.ppermute(block, axis, [(i, (i + distance) % count) for i in range(cou...  12.2 us
    ppermute x8, waiting for transfers between devices, run(): lax.ppermute(known, axis, [(i, i ^ hop) for i in range(lax.axis_size(axis...  2.35 us
    unnamed x9, local copies, waits for them, and re-layouts  1.77 us
  transfers between devices with their start and end apart: 15, of which 8 were waited for; matrix products, arithmetic and copies ran while one was open for 0% of the time, Pallas kernels for 31%

profile of v3, /device:TPU:2, one launch (start us, length us, event | category | flops | bytes accessed | tf_op | source)
XLA Modules:
  0.0 76.3 jit_solution(6499717357697432203)
XLA Ops:
  0.6 0.0 copy-start
  0.6 0.9 %copy-done = f32[3,8,16,128]{3,2,1,0:T(8,128)S(1)} copy-done((f32[3,8,16,128]{3,2,1,0:T(8,128)S(1)}, f32[3,8,16,128]{3,2,1,0:T(8,128)}, u32[]{:S(2)}) %copy-start) | copy-done | bytes 196632
  1.6 0.0 copy-start.1
  1.6 0.8 %copy-done.1 = f32[8,16,128]{2,1,0:T(8,128)S(1)} copy-done((f32[8,16,128]{2,1,0:T(8,128)S(1)}, f32[8,16,128]{2,1,0:T(8,128)}, u32[]{:S(2)}) %copy-start.1) | copy-done | bytes 65560
  2.4 0.2 pack_z.1
  2.6 1.7 %collective-permute-start = (f32[16,8,128]{2,1,0:T(8,128)S(1)}, f32[16,8,128]{2,1,0:T(8,128)S(1)}, u32[]{:S(2)}, u32[]{:S(2)}) collective-permute-start(f32[16,8,128]{2,1,0:T(8,128)S(1)} %get-tuple-element.36), channel_id=1, source_target_pairs={{0,1},{1,2},{2,3},{3,0},{4,5},{5,6},{6,7},{7,4},{8,9},{9,10},{10,1... | collective-permute-start | bytes 196616 | tf_op jit(solution)/shard_map/ppermute | solution.py:527
  4.2 1.7 %collective-permute-start.1 = (f32[16,8,128]{2,1,0:T(8,128)S(1)}, f32[16,8,128]{2,1,0:T(8,128)S(1)}, u32[]{:S(2)}, u32[]{:S(2)}) collective-permute-start(f32[16,8,128]{2,1,0:T(8,128)S(1)} %get-tuple-element.37), channel_id=1, source_target_pairs={{0,3},{1,0},{2,1},{3,2},{4,7},{5,4},{6,5},{7,6},{8,11},{9,8},{10,9... | collective-permute-start | bytes 196616 | tf_op jit(solution)/shard_map/ppermute | solution.py:527
  5.9 2.2 %collective-permute-done = f32[16,8,128]{2,1,0:T(8,128)S(1)} collective-permute-done((f32[16,8,128]{2,1,0:T(8,128)S(1)}, f32[16,8,128]{2,1,0:T(8,128)S(1)}, u32[]{:S(2)}, u32[]{:S(2)}) %collective-permute-start) | collective-permute-done | bytes 65568 | tf_op jit(solution)/shard_map/ppermute | solution.py:527
  8.1 0.4 collective-permute-done.1
  8.5 5.9 %collective-permute-start.3 = (f32[80,8,128]{2,1,0:T(8,128)S(1)}, f32[80,8,128]{2,1,0:T(8,128)S(1)}, u32[]{:S(2)}, u32[]{:S(2)}) collective-permute-start(f32[80,8,128]{2,1,0:T(8,128)S(1)} %pad_maximum_fusion.mid.refs_0_), channel_id=1, source_target_pairs={{0,224},{32,0},{64,32},{96,64},{128,96},{160,128},{192,160},{224,1... | collective-permute-start | bytes 983048 | tf_op jit(solution)/shard_map/ppermute | solution.py:527
  14.5 0.0 collective-permute-start.2
  14.5 2.5 %collective-permute-start.4 = (f32[9,8,128]{2,1,0:T(8,128)S(1)}, f32[9,8,128]{2,1,0:T(8,128)S(1)}, u32[]{:S(2)}, u32[]{:S(2)}) collective-permute-start(f32[9,8,128]{2,1,0:T(8,128)S(1)} %constant_dynamic-update-slice_fusion), channel_id=1, source_target_pairs={{0,192},{32,224},{64,0},{96,32},{128,64},{160,96},{192,128},{224,1... | collective-permute-start | bytes 110600 | tf_op jit(solution)/shard_map/ppermute | solution.py:527
  16.9 4.6 %collective-permute-done.4.far.refs_3_ = f32[9,8,128]{2,1,0:T(8,128)S(1)} collective-permute-done((f32[9,8,128]{2,1,0:T(8,128)S(1)}, f32[9,8,128]{2,1,0:T(8,128)S(1)}, u32[]{:S(2)}, u32[]{:S(2)}) %collective-permute-start.4) | collective-permute-done | bytes 36896 | tf_op jit(solution)/shard_map/ppermute | solution.py:527
  21.6 0.0 collective-permute-done.3.high.refs_2_
  21.6 1.8 %collective-permute-done.2.low.refs_1_ = f32[80,8,128]{2,1,0:T(8,128)S(1)} collective-permute-done((f32[80,8,128]{2,1,0:T(8,128)S(1)}, f32[80,8,128]{2,1,0:T(8,128)S(1)}, u32[]{:S(2)}, u32[]{:S(2)}) %collective-permute-start.2) | collective-permute-done | bytes 327712 | tf_op jit(solution)/shard_map/ppermute | solution.py:527
  23.4 0.2 pack_y.1
  23.6 0.0 collective-permute-start.6
  23.6 0.5 collective-permute-start.5
  24.1 8.0 %collective-permute-done.5.below.refs_4_ = f32[126,8,128]{2,1,0:T(8,128)S(1)} collective-permute-done((f32[126,8,128]{2,1,0:T(8,128)S(1)}, f32[126,8,128]{2,1,0:T(8,128)S(1)}, u32[]{:S(2)}, u32[]{:S(2)}) %collective-permute-start.5) | collective-permute-done | bytes 516128 | tf_op jit(solution)/shard_map/ppermute | solution.py:527
  32.1 0.0 collective-permute-done.6.above.refs_5_
  32.2 0.6 own.1.refs_6_
  32.7 0.6 collective-permute-start.7
  33.3 0.4 widen.1
  33.8 0.4 collective-permute-done.7
  34.2 1.7 %collective-permute-start.8 = (f32[2,8,128]{2,1,0:T(8,128)S(1)}, f32[2,8,128]{2,1,0:T(8,128)S(1)}, u32[]{:S(2)}, u32[]{:S(2)}) collective-permute-start(f32[2,8,128]{2,1,0:T(8,128)S(1)} %pad_maximum_fusion.1.refs_4_), channel_id=1, source_target_pairs={{0,8},{4,12},{8,0},{12,4},{16,24},{20,28},{24,16},{28,20},{1,9},{5... | collective-permute-start | bytes 24584 | tf_op jit(solution)/shard_map/ppermute | solution.py:562
  35.8 4.0 %stress.1 = (f32[6,24,40,128]{3,2,1,0:T(8,128)S(1)}, f32[24,40,128]{2,1,0:T(8,128)S(1)}, f32[40,128]{1,0:T(8,128)S(1)}, f32[2,8,128]{2,1,0:T(8,128)S(1)}) custom-call(f32[3,25,40,128]{3,2,1,0:T(8,128)S(1)} %get-tuple-element.40.refs_0_, f32[3,25,8,128]{3,2,1,0:T(8,128)S(1)} %get-tuple-element.41.refs_1_, f32[3,25,8,128]{3,2,1,0:T(8,128)S(1)} %get-tuple-element.42.refs_2_, ...), custom_call_target="tpu_custom_call" | custom-call | flops 20000000 | bytes 1000000 | tf_op jit(solution)/shard_map/stress/pallas_call | solution.py:40
  39.9 0.0 collective-permute-done.8
  39.9 1.3 %collective-permute-start.9 = (f32[2,8,128]{2,1,0:T(8,128)S(1)}, f32[2,8,128]{2,1,0:T(8,128)S(1)}, u32[]{:S(2)}, u32[]{:S(2)}) collective-permute-start(f32[2,8,128]{2,1,0:T(8,128)S(1)} %pad_maximum_fusion.2.refs_4_), channel_id=1, source_target_pairs={{0,16},{4,20},{8,24},{12,28},{16,0},{20,4},{24,8},{28,12},{1,17},{... | collective-permute-start | bytes 24584 | tf_op jit(solution)/shard_map/ppermute | solution.py:562
  41.2 3.1 %load.1 = (f32[3,24,40,128]{3,2,1,0:T(8,128)S(1)}, f32[24,40,128]{2,1,0:T(8,128)S(1)}, f32[24,40,128]{2,1,0:T(8,128)S(1)}, f32[24,40,128]{2,1,0:T(8,128)S(1)}, f...) custom-call(f32[6,24,40,128]{3,2,1,0:T(8,128)S(1)} %get-tuple-element.45.refs_0_.base, ...), custom_call_target="tpu_custom_call" | custom-call | flops 20000000 | bytes 1000000 | tf_op jit(solution)/shard_map/load/pallas_call | solution.py:40
  44.4 0.8 %collective-permute-done.9 = f32[2,8,128]{2,1,0:T(8,128)S(1)} collective-permute-done((f32[2,8,128]{2,1,0:T(8,128)S(1)}, f32[2,8,128]{2,1,0:T(8,128)S(1)}, u32[]{:S(2)}, u32[]{:S(2)}) %collective-permute-start.9) | collective-permute-done | bytes 8224 | tf_op jit(solution)/shard_map/ppermute | solution.py:562
  45.2 0.1 collective-permute-start.10
  45.3 3.8 %sweep1.1 = (f32[3,25,40,128]{3,2,1,0:T(8,128)S(1)}, f32[2,8,128]{2,1,0:T(8,128)S(1)}) custom-call(f32[3,25,40,128]{3,2,1,0:T(8,128)S(1)} %get-tuple-element.49.refs_0_, f32[3,24,40,128]{3,2,1,0:T(8,128)S(1)} %get-tuple-element.50.refs_1_, f32[24,40,128]{2,1,0:T(8,128)S(1)} %get-tuple-element.51.refs_2_, ...), custom_call_target="tpu_custom_call", output_to_operand_aliasing={{0}: (0, {})} | custom-call | flops 20000000 | bytes 1000000 | tf_op jit(solution)/shard_map/sweep1/pallas_call | solution.py:40
  49.1 0.0 collective-permute-done.10
  49.1 2.2 %collective-permute-start.11 = (f32[2,8,128]{2,1,0:T(8,128)S(1)}, f32[2,8,128]{2,1,0:T(8,128)S(1)}, u32[]{:S(2)}, u32[]{:S(2)}) collective-permute-start(f32[2,8,128]{2,1,0:T(8,128)S(1)} %pad_maximum_fusion.4.refs_4_), channel_id=1, source_target_pairs={{0,64},{32,96},{64,0},{96,32},{128,192},{160,224},{192,128},{224,1... | collective-permute-start | bytes 24584 | tf_op jit(solution)/shard_map/ppermute | solution.py:562
  51.4 3.8 %sweep2.1 = (f32[3,25,40,128]{3,2,1,0:T(8,128)S(1)}, f32[2,8,128]{2,1,0:T(8,128)S(1)}) custom-call(f32[3,25,40,128]{3,2,1,0:T(8,128)S(1)} %get-tuple-element.54.refs_0_, f32[3,24,40,128]{3,2,1,0:T(8,128)S(1)} %get-tuple-element.50.refs_1_, f32[24,40,128]{2,1,0:T(8,128)S(1)} %get-tuple-element.51.refs_2_, ...), custom_call_target="tpu_custom_call", output_to_operand_aliasing={{0}: (0, {})} | custom-call | flops 20000000 | bytes 1000000 | tf_op jit(solution)/shard_map/sweep2/pallas_call | solution.py:40
  55.2 0.0 collective-permute-done.11
  55.2 3.2 %collective-permute-start.12 = (f32[2,8,128]{2,1,0:T(8,128)S(1)}, f32[2,8,128]{2,1,0:T(8,128)S(1)}, u32[]{:S(2)}, u32[]{:S(2)}) collective-permute-start(f32[2,8,128]{2,1,0:T(8,128)S(1)} %pad_maximum_fusion.5.refs_4_), channel_id=1, source_target_pairs={{0,128},{32,160},{64,192},{96,224},{128,0},{160,32},{192,64},{224,... | collective-permute-start | bytes 24584 | tf_op jit(solution)/shard_map/ppermute | solution.py:562
  58.4 3.3 %sweep3.1 = (f32[3,25,40,128]{3,2,1,0:T(8,128)S(1)}, f32[2,8,128]{2,1,0:T(8,128)S(1)}) custom-call(f32[3,25,40,128]{3,2,1,0:T(8,128)S(1)} %get-tuple-element.56.refs_0_, f32[3,24,40,128]{3,2,1,0:T(8,128)S(1)} %get-tuple-element.50.refs_1_, f32[24,40,128]{2,1,0:T(8,128)S(1)} %get-tuple-element.51.refs_2_, ...), custom_call_target="tpu_custom_call", output_to_operand_aliasing={{0}: (0, {})} | custom-call | flops 20000000 | bytes 1000000 | tf_op jit(solution)/shard_map/sweep3/pallas_call | solution.py:40
  61.7 1.1 %collective-permute-done.12 = f32[2,8,128]{2,1,0:T(8,128)S(1)} collective-permute-done((f32[2,8,128]{2,1,0:T(8,128)S(1)}, f32[2,8,128]{2,1,0:T(8,128)S(1)}, u32[]{:S(2)}, u32[]{:S(2)}) %collective-permute-start.12) | collective-permute-done | bytes 8224 | tf_op jit(solution)/shard_map/ppermute | solution.py:562
  62.9 1.8 %collective-permute-start.13 = (f32[2,8,128]{2,1,0:T(8,128)S(1)}, f32[2,8,128]{2,1,0:T(8,128)S(1)}, u32[]{:S(2)}, u32[]{:S(2)}) collective-permute-start(f32[2,8,128]{2,1,0:T(8,128)S(1)} %pad_maximum_fusion.6.refs_4_), channel_id=1, source_target_pairs={{0,1},{1,0},{2,3},{3,2},{4,5},{5,4},{6,7},{7,6},{8,9},{9,8},{10,11... | collective-permute-start | bytes 24584 | tf_op jit(solution)/shard_map/ppermute | solution.py:562
  64.7 2.8 %sweep4.1 = (f32[3,25,40,128]{3,2,1,0:T(8,128)S(1)}, f32[2,8,128]{2,1,0:T(8,128)S(1)}) custom-call(f32[3,25,40,128]{3,2,1,0:T(8,128)S(1)} %get-tuple-element.58.refs_0_, f32[3,24,40,128]{3,2,1,0:T(8,128)S(1)} %get-tuple-element.50.refs_1_, f32[24,40,128]{2,1,0:T(8,128)S(1)} %get-tuple-element.51.refs_2_, ...), custom_call_target="tpu_custom_call", output_to_operand_aliasing={{0}: (0, {})} | custom-call | flops 20000000 | bytes 1000000 | tf_op jit(solution)/shard_map/sweep4/pallas_call | solution.py:40
  67.4 0.0 collective-permute-done.13
  67.5 2.9 %collective-permute-start.14 = (f32[2,8,128]{2,1,0:T(8,128)S(1)}, f32[2,8,128]{2,1,0:T(8,128)S(1)}, u32[]{:S(2)}, u32[]{:S(2)}) collective-permute-start(f32[2,8,128]{2,1,0:T(8,128)S(1)} %pad_maximum_fusion.7.refs_4_), channel_id=1, source_target_pairs={{0,2},{1,3},{2,0},{3,1},{4,6},{5,7},{6,4},{7,5},{8,10},{9,11},{10,... | collective-permute-start | bytes 24584 | tf_op jit(solution)/shard_map/ppermute | solution.py:562
  70.3 2.8 %sweep5.1 = (f32[3,25,40,128]{3,2,1,0:T(8,128)S(1)}, f32[2,8,128]{2,1,0:T(8,128)S(1)}) custom-call(f32[3,25,40,128]{3,2,1,0:T(8,128)S(1)} %get-tuple-element.60.refs_0_, f32[3,24,40,128]{3,2,1,0:T(8,128)S(1)} %get-tuple-element.50.refs_1_, f32[24,40,128]{2,1,0:T(8,128)S(1)} %get-tuple-element.51.refs_2_, ...), custom_call_target="tpu_custom_call", output_to_operand_aliasing={{0}: (0, {})} | custom-call | flops 20000000 | bytes 1000000 | tf_op jit(solution)/shard_map/sweep5/pallas_call | solution.py:40
  73.1 0.0 collective-permute-done.14
  73.1 2.7 %final.1 = (f32[3,8,16,128]{3,2,1,0:T(8,128)}, f32[8,16,128]{2,1,0:T(8,128)}, f32[8,128]{1,0:T(8,128)S(1)}) custom-call(f32[3,25,40,128]{3,2,1,0:T(8,128)S(1)} %get-tuple-element.62.field, f32[24,40,128]{2,1,0:T(8,128)S(1)} %get-tuple-element.63.explicit, f32[6,24,40,128]{3,2,1,0:T(8,128)S(1)} %get-tuple-element.45.refs_0_.base, ...), custom_call_target="tpu_custom_call" | custom-call | flops 1000000 | bytes 1000000 | tf_op jit(solution)/shard_map/final/pallas_call | solution.py:40
  75.8 0.5 slice.203
  (24 shorter events, 0.2 us)
Async XLA Ops:
  0.6 0.9 %copy-start = (f32[3,8,16,128]{3,2,1,0:T(8,128)S(1)}, f32[3,8,16,128]{3,2,1,0:T(8,128)}, u32[]{:S(2)}) copy-start(f32[3,8,16,128]{3,2,1,0:T(8,128)} %disp.1) | copy-start | bytes 589828
  1.6 0.8 %copy-start.1 = (f32[8,16,128]{2,1,0:T(8,128)S(1)}, f32[8,16,128]{2,1,0:T(8,128)}, u32[]{:S(2)}) copy-start(f32[8,16,128]{2,1,0:T(8,128)} %dens.1) | copy-start | bytes 196612
  2.6 5.6 %collective-permute-start = (f32[16,8,128]{2,1,0:T(8,128)S(1)}, f32[16,8,128]{2,1,0:T(8,128)S(1)}, u32[]{:S(2)}, u32[]{:S(2)}) collective-permute-start(f32[16,8,128]{2,1,0:T(8,128)S(1)} %get-tuple-element.36), channel_id=1, source_target_pairs={{0,1},{1,2},{2,3},{3,0},{4,5},{5,6},{6,7},{7,4},{8,9},{9,10},{10,1... | collective-permute-start | bytes 196616 | tf_op jit(solution)/shard_map/ppermute | solution.py:527
  4.2 4.3 %collective-permute-start.1 = (f32[16,8,128]{2,1,0:T(8,128)S(1)}, f32[16,8,128]{2,1,0:T(8,128)S(1)}, u32[]{:S(2)}, u32[]{:S(2)}) collective-permute-start(f32[16,8,128]{2,1,0:T(8,128)S(1)} %get-tuple-element.37), channel_id=1, source_target_pairs={{0,3},{1,0},{2,1},{3,2},{4,7},{5,4},{6,5},{7,6},{8,11},{9,8},{10,9... | collective-permute-start | bytes 196616 | tf_op jit(solution)/shard_map/ppermute | solution.py:527
  8.5 13.1 %collective-permute-start.3 = (f32[80,8,128]{2,1,0:T(8,128)S(1)}, f32[80,8,128]{2,1,0:T(8,128)S(1)}, u32[]{:S(2)}, u32[]{:S(2)}) collective-permute-start(f32[80,8,128]{2,1,0:T(8,128)S(1)} %pad_maximum_fusion.mid.refs_0_), channel_id=1, source_target_pairs={{0,224},{32,0},{64,32},{96,64},{128,96},{160,128},{192,160},{224,1... | collective-permute-start | bytes 983048 | tf_op jit(solution)/shard_map/ppermute | solution.py:527
  14.5 9.0 %collective-permute-start.2 = (f32[80,8,128]{2,1,0:T(8,128)S(1)}, f32[80,8,128]{2,1,0:T(8,128)S(1)}, u32[]{:S(2)}, u32[]{:S(2)}) collective-permute-start(f32[80,8,128]{2,1,0:T(8,128)S(1)} %pad_maximum_fusion.mid.refs_0_), channel_id=1, source_target_pairs={{0,32},{32,64},{64,96},{96,128},{128,160},{160,192},{192,224},{224... | collective-permute-start | bytes 983048 | tf_op jit(solution)/shard_map/ppermute | solution.py:527
  14.5 7.1 %collective-permute-start.4 = (f32[9,8,128]{2,1,0:T(8,128)S(1)}, f32[9,8,128]{2,1,0:T(8,128)S(1)}, u32[]{:S(2)}, u32[]{:S(2)}) collective-permute-start(f32[9,8,128]{2,1,0:T(8,128)S(1)} %constant_dynamic-update-slice_fusion), channel_id=1, source_target_pairs={{0,192},{32,224},{64,0},{96,32},{128,64},{160,96},{192,128},{224,1... | collective-permute-start | bytes 110600 | tf_op jit(solution)/shard_map/ppermute | solution.py:527
  23.6 8.6 %collective-permute-start.6 = (f32[141,8,128]{2,1,0:T(8,128)S(1)}, f32[141,8,128]{2,1,0:T(8,128)S(1)}, u32[]{:S(2)}, u32[]{:S(2)}) collective-permute-start(f32[141,8,128]{2,1,0:T(8,128)S(1)} %get-tuple-element.39), channel_id=1, source_target_pairs={{0,28},{4,0},{8,4},{12,8},{16,12},{20,16},{24,20},{28,24},{1,29},{... | collective-permute-start | bytes 1732616 | tf_op jit(solution)/shard_map/ppermute | solution.py:527
  23.6 8.5 %collective-permute-start.5 = (f32[126,8,128]{2,1,0:T(8,128)S(1)}, f32[126,8,128]{2,1,0:T(8,128)S(1)}, u32[]{:S(2)}, u32[]{:S(2)}) collective-permute-start(f32[126,8,128]{2,1,0:T(8,128)S(1)} %get-tuple-element.38), channel_id=1, source_target_pairs={{0,4},{4,8},{8,12},{12,16},{16,20},{20,24},{24,28},{28,0},{1,5},{5... | collective-permute-start | bytes 1548296 | tf_op jit(solution)/shard_map/ppermute | solution.py:527
  32.7 1.4 %collective-permute-start.7 = (f32[2,8,128]{2,1,0:T(8,128)S(1)}, f32[2,8,128]{2,1,0:T(8,128)S(1)}, u32[]{:S(2)}, u32[]{:S(2)}) collective-permute-start(f32[2,8,128]{2,1,0:T(8,128)S(1)} %own.1.refs_6_), channel_id=1, source_target_pairs={{0,4},{4,0},{8,12},{12,8},{16,20},{20,16},{24,28},{28,24},{1,5},{5... | collective-permute-start | bytes 24584 | tf_op jit(solution)/shard_map/ppermute | solution.py:562
  34.2 5.7 %collective-permute-start.8 = (f32[2,8,128]{2,1,0:T(8,128)S(1)}, f32[2,8,128]{2,1,0:T(8,128)S(1)}, u32[]{:S(2)}, u32[]{:S(2)}) collective-permute-start(f32[2,8,128]{2,1,0:T(8,128)S(1)} %pad_maximum_fusion.1.refs_4_), channel_id=1, source_target_pairs={{0,8},{4,12},{8,0},{12,4},{16,24},{20,28},{24,16},{28,20},{1,9},{5... | collective-permute-start | bytes 24584 | tf_op jit(solution)/shard_map/ppermute | solution.py:562
  39.9 5.2 %collective-permute-start.9 = (f32[2,8,128]{2,1,0:T(8,128)S(1)}, f32[2,8,128]{2,1,0:T(8,128)S(1)}, u32[]{:S(2)}, u32[]{:S(2)}) collective-permute-start(f32[2,8,128]{2,1,0:T(8,128)S(1)} %pad_maximum_fusion.2.refs_4_), channel_id=1, source_target_pairs={{0,16},{4,20},{8,24},{12,28},{16,0},{20,4},{24,8},{28,12},{1,17},{... | collective-permute-start | bytes 24584 | tf_op jit(solution)/shard_map/ppermute | solution.py:562
  45.2 3.9 %collective-permute-start.10 = (f32[2,8,128]{2,1,0:T(8,128)S(1)}, f32[2,8,128]{2,1,0:T(8,128)S(1)}, u32[]{:S(2)}, u32[]{:S(2)}) collective-permute-start(f32[2,8,128]{2,1,0:T(8,128)S(1)} %pad_maximum_fusion.3.refs_4_), channel_id=1, source_target_pairs={{0,32},{32,0},{64,96},{96,64},{128,160},{160,128},{192,224},{224,1... | collective-permute-start | bytes 24584 | tf_op jit(solution)/shard_map/ppermute | solution.py:562
  49.1 6.0 %collective-permute-start.11 = (f32[2,8,128]{2,1,0:T(8,128)S(1)}, f32[2,8,128]{2,1,0:T(8,128)S(1)}, u32[]{:S(2)}, u32[]{:S(2)}) collective-permute-start(f32[2,8,128]{2,1,0:T(8,128)S(1)} %pad_maximum_fusion.4.refs_4_), channel_id=1, source_target_pairs={{0,64},{32,96},{64,0},{96,32},{128,192},{160,224},{192,128},{224,1... | collective-permute-start | bytes 24584 | tf_op jit(solution)/shard_map/ppermute | solution.py:562
  55.2 7.6 %collective-permute-start.12 = (f32[2,8,128]{2,1,0:T(8,128)S(1)}, f32[2,8,128]{2,1,0:T(8,128)S(1)}, u32[]{:S(2)}, u32[]{:S(2)}) collective-permute-start(f32[2,8,128]{2,1,0:T(8,128)S(1)} %pad_maximum_fusion.5.refs_4_), channel_id=1, source_target_pairs={{0,128},{32,160},{64,192},{96,224},{128,0},{160,32},{192,64},{224,... | collective-permute-start | bytes 24584 | tf_op jit(solution)/shard_map/ppermute | solution.py:562
  62.9 4.6 %collective-permute-start.13 = (f32[2,8,128]{2,1,0:T(8,128)S(1)}, f32[2,8,128]{2,1,0:T(8,128)S(1)}, u32[]{:S(2)}, u32[]{:S(2)}) collective-permute-start(f32[2,8,128]{2,1,0:T(8,128)S(1)} %pad_maximum_fusion.6.refs_4_), channel_id=1, source_target_pairs={{0,1},{1,0},{2,3},{3,2},{4,5},{5,4},{6,7},{7,6},{8,9},{9,8},{10,11... | collective-permute-start | bytes 24584 | tf_op jit(solution)/shard_map/ppermute | solution.py:562
  67.5 5.6 %collective-permute-start.14 = (f32[2,8,128]{2,1,0:T(8,128)S(1)}, f32[2,8,128]{2,1,0:T(8,128)S(1)}, u32[]{:S(2)}, u32[]{:S(2)}) collective-permute-start(f32[2,8,128]{2,1,0:T(8,128)S(1)} %pad_maximum_fusion.7.refs_4_), channel_id=1, source_target_pairs={{0,2},{1,3},{2,0},{3,1},{4,6},{5,7},{6,4},{7,5},{8,10},{9,11},{10,... | collective-permute-start | bytes 24584 | tf_op jit(solution)/shard_map/ppermute | solution.py:562

commit v4 on v3

--- a/solution.py
+++ b/solution.py
@@ -75,24 +75,16 @@
 
 def z_next(value):
     main, strip = split(value)
-    lane = lanes()
-    moved = [rolled(m, -1, 1) for m in main]
-    out = [jnp.where(lane == 127, rolled(strip, 127 - 32 * g, 1), moved[g]) for g in range(4)]
-    tail = rolled(strip, -1, 1)
-    for g in range(4):
-        tail = jnp.where(lane == 32 * g + 31, rolled(main[g], 32 * g + 31, 1), tail)
-    return join(out, tail)
+    last = lanes() == 127
+    out = [jnp.where(last, rolled(strip, 120 - 32 * g, 1), rolled(main[g], -1, 1)) for g in range(4)]
+    return join(out, rolled(strip, -1, 1))
 
 
 def z_prev(value):
     main, strip = split(value)
-    lane = lanes()
-    moved = [rolled(m, 1, 1) for m in main]
-    out = [jnp.where(lane == 0, rolled(strip, 97 - 32 * g, 1), moved[g]) for g in range(4)]
-    tail = rolled(strip, 1, 1)
-    for g in range(4):
-        tail = jnp.where(lane == 32 * g, rolled(main[g], 32 * g + 1, 1), tail)
-    return join(out, tail)
+    first = lanes() == 0
+    out = [jnp.where(first, rolled(strip, -23 - 32 * g, 1), rolled(main[g], 1, 1)) for g in range(4)]
+    return join(out, rolled(strip, 1, 1))
 
 
 def y_next(value, beyond=None):
@@ -118,19 +110,23 @@
     return join(out, jnp.where(row == 0, rolled(tail, 32, 1), tail))
 
 
-def pack_z(disp, dens, up, down):
+def pack_z(disp, dens, up, down, inner):
     lane = lanes()
     for c in range(4):
+        short = 0 if c < 3 else 1
         for k in range(4):
-            top = bottom = jnp.zeros((8, 128), F32)
+            top = bottom = own = jnp.zeros((8, 128), F32)
             for q in range(4):
                 x, t = k + 4 * (q // 2), 8 * (q % 2)
                 value = disp[c, x, t : t + 8, :] if c < 3 else dens[x, t : t + 8, :]
-                mine = (lane >= 32 * q) & (lane < 32 * q + 32)
-                top = jnp.where(mine & (lane >= 32 * q + 24), rolled(value, 32 * q + 32, 1), top)
-                bottom = jnp.where(mine & (lane < 32 * q + 9), rolled(value, 32 * q, 1), bottom)
+                place = lane - 32 * q
+                top = jnp.where((place >= 16) & (place < 24), rolled(value, 32 * q + 24, 1), top)
+                bottom = jnp.where((place >= 7) & (place < 16 - short), rolled(value, 32 * q + 7, 1), bottom)
+                own = jnp.where((place >= 24) & (place < 32 - short), rolled(value, 32 * q + 24, 1), own)
+                own = jnp.where((place >= 0) & (place < 7), rolled(value, 32 * q + 7, 1), own)
             up[4 * c + k] = top
             down[4 * c + k] = bottom
+            inner[4 * c + k] = own
 
 
 def masked(value, real):
@@ -303,7 +299,7 @@
         upper = within("gy", 1)
         main = [masked(src[2 * i], real), masked(src[2 * i + 1], real), above[32 * s + i] * upper]
         strip, far_strip = masked(strip, real), far_strip * upper
-        edge = [rolled(strip, 127 - base, 1), rolled(strip, 95 - base, 1), rolled(far_strip, 127 - at, 1)]
+        edge = [rolled(strip, 120 - base, 1), rolled(strip, 88 - base, 1), rolled(far_strip, 120 - at, 1)]
         after = [jnp.where(lane == 127, edge[t], rolled(main[t], -1, 1)) for t in range(3)]
         both = [after[t] + main[t] for t in range(3)]
         change = [after[t] - main[t] for t in range(3)]
@@ -474,7 +470,7 @@
     group, place = lane // 32, lane % 32
     main = row < 32
     y_cell = jnp.where(main, row - 8, 8 * group + row - 40)
-    z_cell = jnp.where(main, lane, jnp.where(place < 16, 128 + place, place - 32))
+    z_cell = jnp.where(main, lane, jnp.where(place < 16, 121 + place, place - 24))
     in_y, in_z = positions("gy", BY, y_cell), positions("gz", BZ, z_cell)
     ys, zs = {o: in_y(o) for o in range(-2, 3)}, {o: in_z(o) for o in range(-2, 3)}
     beside = ys[-1] + ys[1]
@@ -542,9 +538,9 @@
 
 def on_device(displacement, density):
     plane = (ROWS, 128)
-    up, down = kernel_call(pack_z, [(16, 8, 128)] * 2, "pack_z")(displacement, density)
+    up, down, inner = kernel_call(pack_z, [(16, 8, 128)] * 3, "pack_z")(displacement, density)
     below_z, above_z = passed(up, "gz", 1), passed(down, "gz", -1)
-    strips = below_z * within("gz", -1) + above_z * within("gz", 1)
+    strips = inner + below_z * within("gz", -1) + above_z * within("gz", 1)
     mid = jnp.concatenate(
         [displacement.reshape(48, 8, 128), density.reshape(16, 8, 128), strips], axis=0
     )

time: 76.5 us -> 74.9 us (0.979)
  Pallas kernels: 27.6 us -> 24.3 us
  waiting for transfers between devices: 19.5 us -> 20.5 us
  other arithmetic: 0.14 us -> 1.11 us
    pallas_call x12, Pallas kernels: 27.6 us -> 24.3 us  [run(): pl.pallas_call(body, out_shape=[tile(shape) for shape in outs], in_specs=...]
    ppermute x8, waiting for transfers between devices: 2.35 us -> 3.36 us  [run(): lax.ppermute(known, axis, [(i, i ^ hop) for i in range(lax.axis_size(axis...]
    concatenate x1, other arithmetic: 0.02 us -> 0.99 us  [on_device(): jnp.concatenate([displacement.reshape(48, 8, 128), density.reshape(16, 8,...]
  transfers between devices with their start and end apart: 15 -> 15, of which waited for: 8 -> 9; matrix products, arithmetic and copies ran while one was open for 0% -> 0% of each run, Pallas kernels for 31% -> 28%
where the time goes in v4:
time: 74.9 us; the launch traced here: 74.8 us
  starting transfers between devices  25.8 us (34%)
  Pallas kernels  24.3 us (32%)
  waiting for transfers between devices  20.5 us (27%)
  local copies, waits for them, and re-layouts  2.28 us (3%)
  other arithmetic  1.11 us (1%)
  between operations  0.82 us (1%)
    pallas_call x12, Pallas kernels, run(): pl.pallas_call(body, out_shape=[tile(shape) for shape in outs], in_specs=...  24.3 us
    ppermute x7, waiting for transfers between devices, passed(): lax.ppermute(block, axis, [(i, (i + distance) % count) for i in range(cou...  17.1 us
    ppermute x8, starting transfers between devices, run(): lax.ppermute(known, axis, [(i, i ^ hop) for i in range(lax.axis_size(axis...  13.6 us
    ppermute x7, starting transfers between devices, passed(): lax.ppermute(block, axis, [(i, (i + distance) % count) for i in range(cou...  12.2 us
    ppermute x8, waiting for transfers between devices, run(): lax.ppermute(known, axis, [(i, i ^ hop) for i in range(lax.axis_size(axis...  3.36 us
    unnamed x9, local copies, waits for them, and re-layouts  1.77 us
  transfers between devices with their start and end apart: 15, of which 9 were waited for; matrix products, arithmetic and copies ran while one was open for 0% of the time, Pallas kernels for 28%

profile of v4, /device:TPU:2, one launch (start us, length us, event | category | flops | bytes accessed | tf_op | source)
XLA Modules:
  0.0 74.8 jit_solution(9307504044634658673)
XLA Ops:
  0.6 0.0 copy-start
  0.6 0.9 %copy-done = f32[3,8,16,128]{3,2,1,0:T(8,128)S(1)} copy-done((f32[3,8,16,128]{3,2,1,0:T(8,128)S(1)}, f32[3,8,16,128]{3,2,1,0:T(8,128)}, u32[]{:S(2)}) %copy-start) | copy-done | bytes 196632
  1.6 0.0 copy-start.1
  1.6 0.8 %copy-done.1 = f32[8,16,128]{2,1,0:T(8,128)S(1)} copy-done((f32[8,16,128]{2,1,0:T(8,128)S(1)}, f32[8,16,128]{2,1,0:T(8,128)}, u32[]{:S(2)}) %copy-start.1) | copy-done | bytes 65560
  2.4 0.2 pack_z.1
  2.6 1.7 %collective-permute-start = (f32[16,8,128]{2,1,0:T(8,128)S(1)}, f32[16,8,128]{2,1,0:T(8,128)S(1)}, u32[]{:S(2)}, u32[]{:S(2)}) collective-permute-start(f32[16,8,128]{2,1,0:T(8,128)S(1)} %get-tuple-element.38), channel_id=1, source_target_pairs={{0,1},{1,2},{2,3},{3,0},{4,5},{5,6},{6,7},{7,4},{8,9},{9,10},{10,1... | collective-permute-start | bytes 196616 | tf_op jit(solution)/shard_map/ppermute | solution.py:523
  4.3 1.7 %collective-permute-start.1 = (f32[16,8,128]{2,1,0:T(8,128)S(1)}, f32[16,8,128]{2,1,0:T(8,128)S(1)}, u32[]{:S(2)}, u32[]{:S(2)}) collective-permute-start(f32[16,8,128]{2,1,0:T(8,128)S(1)} %get-tuple-element.39), channel_id=1, source_target_pairs={{0,3},{1,0},{2,1},{3,2},{4,7},{5,4},{6,5},{7,6},{8,11},{9,8},{10,9... | collective-permute-start | bytes 196616 | tf_op jit(solution)/shard_map/ppermute | solution.py:523
  5.9 2.2 %collective-permute-done = f32[16,8,128]{2,1,0:T(8,128)S(1)} collective-permute-done((f32[16,8,128]{2,1,0:T(8,128)S(1)}, f32[16,8,128]{2,1,0:T(8,128)S(1)}, u32[]{:S(2)}, u32[]{:S(2)}) %collective-permute-start) | collective-permute-done | bytes 65568 | tf_op jit(solution)/shard_map/ppermute | solution.py:523
  8.2 0.4 collective-permute-done.1
  8.5 1.0 %pad_maximum_fusion.mid.refs_0_ = f32[80,8,128]{2,1,0:T(8,128)S(1)} fusion(f32[16,8,128]{2,1,0:T(8,128)S(1)} %multiply_add_fusion, f32[16,8,128]{2,1,0:T(8,128)} %bitcast.7, f32[48,8,128]{2,1,0:T(8,128)} %bitcast.3), kind=kLoop, calls=%fused_computation | loop fusion | flops 163840 | bytes 655360 | tf_op jit(solution)/shard_map/concatenate | solution.py:544
  9.5 5.9 %collective-permute-start.3 = (f32[80,8,128]{2,1,0:T(8,128)S(1)}, f32[80,8,128]{2,1,0:T(8,128)S(1)}, u32[]{:S(2)}, u32[]{:S(2)}) collective-permute-start(f32[80,8,128]{2,1,0:T(8,128)S(1)} %pad_maximum_fusion.mid.refs_0_), channel_id=1, source_target_pairs={{0,224},{32,0},{64,32},{96,64},{128,96},{160,128},{192,160},{224,1... | collective-permute-start | bytes 983048 | tf_op jit(solution)/shard_map/ppermute | solution.py:523
  15.5 0.0 collective-permute-start.2
  15.5 2.5 %collective-permute-start.4 = (f32[9,8,128]{2,1,0:T(8,128)S(1)}, f32[9,8,128]{2,1,0:T(8,128)S(1)}, u32[]{:S(2)}, u32[]{:S(2)}) collective-permute-start(f32[9,8,128]{2,1,0:T(8,128)S(1)} %constant_dynamic-update-slice_fusion), channel_id=1, source_target_pairs={{0,192},{32,224},{64,0},{96,32},{128,64},{160,96},{192,128},{224,1... | collective-permute-start | bytes 110600 | tf_op jit(solution)/shard_map/ppermute | solution.py:523
  17.9 4.6 %collective-permute-done.4.far.refs_3_ = f32[9,8,128]{2,1,0:T(8,128)S(1)} collective-permute-done((f32[9,8,128]{2,1,0:T(8,128)S(1)}, f32[9,8,128]{2,1,0:T(8,128)S(1)}, u32[]{:S(2)}, u32[]{:S(2)}) %collective-permute-start.4) | collective-permute-done | bytes 36896 | tf_op jit(solution)/shard_map/ppermute | solution.py:523
  22.6 0.0 collective-permute-done.3.high.refs_2_
  22.6 1.8 %collective-permute-done.2.low.refs_1_ = f32[80,8,128]{2,1,0:T(8,128)S(1)} collective-permute-done((f32[80,8,128]{2,1,0:T(8,128)S(1)}, f32[80,8,128]{2,1,0:T(8,128)S(1)}, u32[]{:S(2)}, u32[]{:S(2)}) %collective-permute-start.2) | collective-permute-done | bytes 327712 | tf_op jit(solution)/shard_map/ppermute | solution.py:523
  24.4 0.2 pack_y.1
  24.6 0.0 collective-permute-start.6
  24.6 0.5 collective-permute-start.5
  25.1 8.0 %collective-permute-done.5.below.refs_4_ = f32[126,8,128]{2,1,0:T(8,128)S(1)} collective-permute-done((f32[126,8,128]{2,1,0:T(8,128)S(1)}, f32[126,8,128]{2,1,0:T(8,128)S(1)}, u32[]{:S(2)}, u32[]{:S(2)}) %collective-permute-start.5) | collective-permute-done | bytes 516128 | tf_op jit(solution)/shard_map/ppermute | solution.py:523
  33.2 0.0 collective-permute-done.6.above.refs_5_
  33.2 0.6 own.1.refs_6_
  33.7 0.6 collective-permute-start.7
  34.3 0.4 widen.1
  34.8 0.4 collective-permute-done.7
  35.2 1.7 %collective-permute-start.8 = (f32[2,8,128]{2,1,0:T(8,128)S(1)}, f32[2,8,128]{2,1,0:T(8,128)S(1)}, u32[]{:S(2)}, u32[]{:S(2)}) collective-permute-start(f32[2,8,128]{2,1,0:T(8,128)S(1)} %pad_maximum_fusion.1.refs_4_), channel_id=1, source_target_pairs={{0,8},{4,12},{8,0},{12,4},{16,24},{20,28},{24,16},{28,20},{1,9},{5... | collective-permute-start | bytes 24584 | tf_op jit(solution)/shard_map/ppermute | solution.py:558
  36.8 3.8 %stress.1 = (f32[6,24,40,128]{3,2,1,0:T(8,128)S(1)}, f32[24,40,128]{2,1,0:T(8,128)S(1)}, f32[40,128]{1,0:T(8,128)S(1)}, f32[2,8,128]{2,1,0:T(8,128)S(1)}) custom-call(f32[3,25,40,128]{3,2,1,0:T(8,128)S(1)} %get-tuple-element.42.refs_0_, f32[3,25,8,128]{3,2,1,0:T(8,128)S(1)} %get-tuple-element.43.refs_1_, f32[3,25,8,128]{3,2,1,0:T(8,128)S(1)} %get-tuple-element.44.refs_2_, ...), custom_call_target="tpu_custom_call" | custom-call | flops 20000000 | bytes 1000000 | tf_op jit(solution)/shard_map/stress/pallas_call | solution.py:40
  40.6 0.0 collective-permute-done.8
  40.6 1.3 %collective-permute-start.9 = (f32[2,8,128]{2,1,0:T(8,128)S(1)}, f32[2,8,128]{2,1,0:T(8,128)S(1)}, u32[]{:S(2)}, u32[]{:S(2)}) collective-permute-start(f32[2,8,128]{2,1,0:T(8,128)S(1)} %pad_maximum_fusion.2.refs_4_), channel_id=1, source_target_pairs={{0,16},{4,20},{8,24},{12,28},{16,0},{20,4},{24,8},{28,12},{1,17},{... | collective-permute-start | bytes 24584 | tf_op jit(solution)/shard_map/ppermute | solution.py:558
  41.9 2.9 %load.1 = (f32[3,24,40,128]{3,2,1,0:T(8,128)S(1)}, f32[24,40,128]{2,1,0:T(8,128)S(1)}, f32[24,40,128]{2,1,0:T(8,128)S(1)}, f32[24,40,128]{2,1,0:T(8,128)S(1)}, f...) custom-call(f32[6,24,40,128]{3,2,1,0:T(8,128)S(1)} %get-tuple-element.47.refs_0_.base, ...), custom_call_target="tpu_custom_call" | custom-call | flops 20000000 | bytes 1000000 | tf_op jit(solution)/shard_map/load/pallas_call | solution.py:40
  44.8 1.1 %collective-permute-done.9 = f32[2,8,128]{2,1,0:T(8,128)S(1)} collective-permute-done((f32[2,8,128]{2,1,0:T(8,128)S(1)}, f32[2,8,128]{2,1,0:T(8,128)S(1)}, u32[]{:S(2)}, u32[]{:S(2)}) %collective-permute-start.9) | collective-permute-done | bytes 8224 | tf_op jit(solution)/shard_map/ppermute | solution.py:558
  45.9 0.1 collective-permute-start.10
  46.0 3.2 %sweep1.1 = (f32[3,25,40,128]{3,2,1,0:T(8,128)S(1)}, f32[2,8,128]{2,1,0:T(8,128)S(1)}) custom-call(f32[3,25,40,128]{3,2,1,0:T(8,128)S(1)} %get-tuple-element.51.refs_0_, f32[3,24,40,128]{3,2,1,0:T(8,128)S(1)} %get-tuple-element.52.refs_1_, f32[24,40,128]{2,1,0:T(8,128)S(1)} %get-tuple-element.53.refs_2_, ...), custom_call_target="tpu_custom_call", output_to_operand_aliasing={{0}: (0, {})} | custom-call | flops 20000000 | bytes 1000000 | tf_op jit(solution)/shard_map/sweep1/pallas_call | solution.py:40
  49.2 0.4 collective-permute-done.10
  49.6 1.8 %collective-permute-start.11 = (f32[2,8,128]{2,1,0:T(8,128)S(1)}, f32[2,8,128]{2,1,0:T(8,128)S(1)}, u32[]{:S(2)}, u32[]{:S(2)}) collective-permute-start(f32[2,8,128]{2,1,0:T(8,128)S(1)} %pad_maximum_fusion.4.refs_4_), channel_id=1, source_target_pairs={{0,64},{32,96},{64,0},{96,32},{128,192},{160,224},{192,128},{224,1... | collective-permute-start | bytes 24584 | tf_op jit(solution)/shard_map/ppermute | solution.py:558
  51.5 3.2 %sweep2.1 = (f32[3,25,40,128]{3,2,1,0:T(8,128)S(1)}, f32[2,8,128]{2,1,0:T(8,128)S(1)}) custom-call(f32[3,25,40,128]{3,2,1,0:T(8,128)S(1)} %get-tuple-element.56.refs_0_, f32[3,24,40,128]{3,2,1,0:T(8,128)S(1)} %get-tuple-element.52.refs_1_, f32[24,40,128]{2,1,0:T(8,128)S(1)} %get-tuple-element.53.refs_2_, ...), custom_call_target="tpu_custom_call", output_to_operand_aliasing={{0}: (0, {})} | custom-call | flops 20000000 | bytes 1000000 | tf_op jit(solution)/shard_map/sweep2/pallas_call | solution.py:40
  54.7 0.0 collective-permute-done.11
  54.7 3.5 %collective-permute-start.12 = (f32[2,8,128]{2,1,0:T(8,128)S(1)}, f32[2,8,128]{2,1,0:T(8,128)S(1)}, u32[]{:S(2)}, u32[]{:S(2)}) collective-permute-start(f32[2,8,128]{2,1,0:T(8,128)S(1)} %pad_maximum_fusion.5.refs_4_), channel_id=1, source_target_pairs={{0,128},{32,160},{64,192},{96,224},{128,0},{160,32},{192,64},{224,... | collective-permute-start | bytes 24584 | tf_op jit(solution)/shard_map/ppermute | solution.py:558
  58.2 2.8 %sweep3.1 = (f32[3,25,40,128]{3,2,1,0:T(8,128)S(1)}, f32[2,8,128]{2,1,0:T(8,128)S(1)}) custom-call(f32[3,25,40,128]{3,2,1,0:T(8,128)S(1)} %get-tuple-element.58.refs_0_, f32[3,24,40,128]{3,2,1,0:T(8,128)S(1)} %get-tuple-element.52.refs_1_, f32[24,40,128]{2,1,0:T(8,128)S(1)} %get-tuple-element.53.refs_2_, ...), custom_call_target="tpu_custom_call", output_to_operand_aliasing={{0}: (0, {})} | custom-call | flops 20000000 | bytes 1000000 | tf_op jit(solution)/shard_map/sweep3/pallas_call | solution.py:40
  61.0 1.4 %collective-permute-done.12 = f32[2,8,128]{2,1,0:T(8,128)S(1)} collective-permute-done((f32[2,8,128]{2,1,0:T(8,128)S(1)}, f32[2,8,128]{2,1,0:T(8,128)S(1)}, u32[]{:S(2)}, u32[]{:S(2)}) %collective-permute-start.12) | collective-permute-done | bytes 8224 | tf_op jit(solution)/shard_map/ppermute | solution.py:558
  62.4 1.8 %collective-permute-start.13 = (f32[2,8,128]{2,1,0:T(8,128)S(1)}, f32[2,8,128]{2,1,0:T(8,128)S(1)}, u32[]{:S(2)}, u32[]{:S(2)}) collective-permute-start(f32[2,8,128]{2,1,0:T(8,128)S(1)} %pad_maximum_fusion.6.refs_4_), channel_id=1, source_target_pairs={{0,1},{1,0},{2,3},{3,2},{4,5},{5,4},{6,7},{7,6},{8,9},{9,8},{10,11... | collective-permute-start | bytes 24584 | tf_op jit(solution)/shard_map/ppermute | solution.py:558
  64.2 2.3 %sweep4.1 = (f32[3,25,40,128]{3,2,1,0:T(8,128)S(1)}, f32[2,8,128]{2,1,0:T(8,128)S(1)}) custom-call(f32[3,25,40,128]{3,2,1,0:T(8,128)S(1)} %get-tuple-element.60.refs_0_, f32[3,24,40,128]{3,2,1,0:T(8,128)S(1)} %get-tuple-element.52.refs_1_, f32[24,40,128]{2,1,0:T(8,128)S(1)} %get-tuple-element.53.refs_2_, ...), custom_call_target="tpu_custom_call", output_to_operand_aliasing={{0}: (0, {})} | custom-call | flops 20000000 | bytes 1000000 | tf_op jit(solution)/shard_map/sweep4/pallas_call | solution.py:40
  66.5 0.0 collective-permute-done.13
  66.5 2.9 %collective-permute-start.14 = (f32[2,8,128]{2,1,0:T(8,128)S(1)}, f32[2,8,128]{2,1,0:T(8,128)S(1)}, u32[]{:S(2)}, u32[]{:S(2)}) collective-permute-start(f32[2,8,128]{2,1,0:T(8,128)S(1)} %pad_maximum_fusion.7.refs_4_), channel_id=1, source_target_pairs={{0,2},{1,3},{2,0},{3,1},{4,6},{5,7},{6,4},{7,5},{8,10},{9,11},{10,... | collective-permute-start | bytes 24584 | tf_op jit(solution)/shard_map/ppermute | solution.py:558
  69.4 2.3 %sweep5.1 = (f32[3,25,40,128]{3,2,1,0:T(8,128)S(1)}, f32[2,8,128]{2,1,0:T(8,128)S(1)}) custom-call(f32[3,25,40,128]{3,2,1,0:T(8,128)S(1)} %get-tuple-element.62.refs_0_, f32[3,24,40,128]{3,2,1,0:T(8,128)S(1)} %get-tuple-element.52.refs_1_, f32[24,40,128]{2,1,0:T(8,128)S(1)} %get-tuple-element.53.refs_2_, ...), custom_call_target="tpu_custom_call", output_to_operand_aliasing={{0}: (0, {})} | custom-call | flops 20000000 | bytes 1000000 | tf_op jit(solution)/shard_map/sweep5/pallas_call | solution.py:40
  71.7 0.0 collective-permute-done.14
  71.8 2.5 %final.1 = (f32[3,8,16,128]{3,2,1,0:T(8,128)}, f32[8,16,128]{2,1,0:T(8,128)}, f32[8,128]{1,0:T(8,128)S(1)}) custom-call(f32[3,25,40,128]{3,2,1,0:T(8,128)S(1)} %get-tuple-element.64.field, f32[24,40,128]{2,1,0:T(8,128)S(1)} %get-tuple-element.65.explicit, f32[6,24,40,128]{3,2,1,0:T(8,128)S(1)} %get-tuple-element.47.refs_0_.base, ...), custom_call_target="tpu_custom_call" | custom-call | flops 1000000 | bytes 1000000 | tf_op jit(solution)/shard_map/final/pallas_call | solution.py:40
  74.3 0.5 slice.203
  (23 shorter events, 0.1 us)
Async XLA Ops:
  0.6 0.9 %copy-start = (f32[3,8,16,128]{3,2,1,0:T(8,128)S(1)}, f32[3,8,16,128]{3,2,1,0:T(8,128)}, u32[]{:S(2)}) copy-start(f32[3,8,16,128]{3,2,1,0:T(8,128)} %disp.1) | copy-start | bytes 589828
  1.6 0.8 %copy-start.1 = (f32[8,16,128]{2,1,0:T(8,128)S(1)}, f32[8,16,128]{2,1,0:T(8,128)}, u32[]{:S(2)}) copy-start(f32[8,16,128]{2,1,0:T(8,128)} %dens.1) | copy-start | bytes 196612
  2.6 5.6 %collective-permute-start = (f32[16,8,128]{2,1,0:T(8,128)S(1)}, f32[16,8,128]{2,1,0:T(8,128)S(1)}, u32[]{:S(2)}, u32[]{:S(2)}) collective-permute-start(f32[16,8,128]{2,1,0:T(8,128)S(1)} %get-tuple-element.38), channel_id=1, source_target_pairs={{0,1},{1,2},{2,3},{3,0},{4,5},{5,6},{6,7},{7,4},{8,9},{9,10},{10,1... | collective-permute-start | bytes 196616 | tf_op jit(solution)/shard_map/ppermute | solution.py:523
  4.3 4.3 %collective-permute-start.1 = (f32[16,8,128]{2,1,0:T(8,128)S(1)}, f32[16,8,128]{2,1,0:T(8,128)S(1)}, u32[]{:S(2)}, u32[]{:S(2)}) collective-permute-start(f32[16,8,128]{2,1,0:T(8,128)S(1)} %get-tuple-element.39), channel_id=1, source_target_pairs={{0,3},{1,0},{2,1},{3,2},{4,7},{5,4},{6,5},{7,6},{8,11},{9,8},{10,9... | collective-permute-start | bytes 196616 | tf_op jit(solution)/shard_map/ppermute | solution.py:523
  9.5 13.1 %collective-permute-start.3 = (f32[80,8,128]{2,1,0:T(8,128)S(1)}, f32[80,8,128]{2,1,0:T(8,128)S(1)}, u32[]{:S(2)}, u32[]{:S(2)}) collective-permute-start(f32[80,8,128]{2,1,0:T(8,128)S(1)} %pad_maximum_fusion.mid.refs_0_), channel_id=1, source_target_pairs={{0,224},{32,0},{64,32},{96,64},{128,96},{160,128},{192,160},{224,1... | collective-permute-start | bytes 983048 | tf_op jit(solution)/shard_map/ppermute | solution.py:523
  15.5 9.0 %collective-permute-start.2 = (f32[80,8,128]{2,1,0:T(8,128)S(1)}, f32[80,8,128]{2,1,0:T(8,128)S(1)}, u32[]{:S(2)}, u32[]{:S(2)}) collective-permute-start(f32[80,8,128]{2,1,0:T(8,128)S(1)} %pad_maximum_fusion.mid.refs_0_), channel_id=1, source_target_pairs={{0,32},{32,64},{64,96},{96,128},{128,160},{160,192},{192,224},{224... | collective-permute-start | bytes 983048 | tf_op jit(solution)/shard_map/ppermute | solution.py:523
  15.5 7.1 %collective-permute-start.4 = (f32[9,8,128]{2,1,0:T(8,128)S(1)}, f32[9,8,128]{2,1,0:T(8,128)S(1)}, u32[]{:S(2)}, u32[]{:S(2)}) collective-permute-start(f32[9,8,128]{2,1,0:T(8,128)S(1)} %constant_dynamic-update-slice_fusion), channel_id=1, source_target_pairs={{0,192},{32,224},{64,0},{96,32},{128,64},{160,96},{192,128},{224,1... | collective-permute-start | bytes 110600 | tf_op jit(solution)/shard_map/ppermute | solution.py:523
  24.6 8.6 %collective-permute-start.6 = (f32[141,8,128]{2,1,0:T(8,128)S(1)}, f32[141,8,128]{2,1,0:T(8,128)S(1)}, u32[]{:S(2)}, u32[]{:S(2)}) collective-permute-start(f32[141,8,128]{2,1,0:T(8,128)S(1)} %get-tuple-element.41), channel_id=1, source_target_pairs={{0,28},{4,0},{8,4},{12,8},{16,12},{20,16},{24,20},{28,24},{1,29},{... | collective-permute-start | bytes 1732616 | tf_op jit(solution)/shard_map/ppermute | solution.py:523
  24.6 8.5 %collective-permute-start.5 = (f32[126,8,128]{2,1,0:T(8,128)S(1)}, f32[126,8,128]{2,1,0:T(8,128)S(1)}, u32[]{:S(2)}, u32[]{:S(2)}) collective-permute-start(f32[126,8,128]{2,1,0:T(8,128)S(1)} %get-tuple-element.40), channel_id=1, source_target_pairs={{0,4},{4,8},{8,12},{12,16},{16,20},{20,24},{24,28},{28,0},{1,5},{5... | collective-permute-start | bytes 1548296 | tf_op jit(solution)/shard_map/ppermute | solution.py:523
  33.7 1.4 %collective-permute-start.7 = (f32[2,8,128]{2,1,0:T(8,128)S(1)}, f32[2,8,128]{2,1,0:T(8,128)S(1)}, u32[]{:S(2)}, u32[]{:S(2)}) collective-permute-start(f32[2,8,128]{2,1,0:T(8,128)S(1)} %own.1.refs_6_), channel_id=1, source_target_pairs={{0,4},{4,0},{8,12},{12,8},{16,20},{20,16},{24,28},{28,24},{1,5},{5... | collective-permute-start | bytes 24584 | tf_op jit(solution)/shard_map/ppermute | solution.py:558
  35.2 5.4 %collective-permute-start.8 = (f32[2,8,128]{2,1,0:T(8,128)S(1)}, f32[2,8,128]{2,1,0:T(8,128)S(1)}, u32[]{:S(2)}, u32[]{:S(2)}) collective-permute-start(f32[2,8,128]{2,1,0:T(8,128)S(1)} %pad_maximum_fusion.1.refs_4_), channel_id=1, source_target_pairs={{0,8},{4,12},{8,0},{12,4},{16,24},{20,28},{24,16},{28,20},{1,9},{5... | collective-permute-start | bytes 24584 | tf_op jit(solution)/shard_map/ppermute | solution.py:558
  40.6 5.2 %collective-permute-start.9 = (f32[2,8,128]{2,1,0:T(8,128)S(1)}, f32[2,8,128]{2,1,0:T(8,128)S(1)}, u32[]{:S(2)}, u32[]{:S(2)}) collective-permute-start(f32[2,8,128]{2,1,0:T(8,128)S(1)} %pad_maximum_fusion.2.refs_4_), channel_id=1, source_target_pairs={{0,16},{4,20},{8,24},{12,28},{16,0},{20,4},{24,8},{28,12},{1,17},{... | collective-permute-start | bytes 24584 | tf_op jit(solution)/shard_map/ppermute | solution.py:558
  45.9 3.7 %collective-permute-start.10 = (f32[2,8,128]{2,1,0:T(8,128)S(1)}, f32[2,8,128]{2,1,0:T(8,128)S(1)}, u32[]{:S(2)}, u32[]{:S(2)}) collective-permute-start(f32[2,8,128]{2,1,0:T(8,128)S(1)} %pad_maximum_fusion.3.refs_4_), channel_id=1, source_target_pairs={{0,32},{32,0},{64,96},{96,64},{128,160},{160,128},{192,224},{224,1... | collective-permute-start | bytes 24584 | tf_op jit(solution)/shard_map/ppermute | solution.py:558
  49.6 5.0 %collective-permute-start.11 = (f32[2,8,128]{2,1,0:T(8,128)S(1)}, f32[2,8,128]{2,1,0:T(8,128)S(1)}, u32[]{:S(2)}, u32[]{:S(2)}) collective-permute-start(f32[2,8,128]{2,1,0:T(8,128)S(1)} %pad_maximum_fusion.4.refs_4_), channel_id=1, source_target_pairs={{0,64},{32,96},{64,0},{96,32},{128,192},{160,224},{192,128},{224,1... | collective-permute-start | bytes 24584 | tf_op jit(solution)/shard_map/ppermute | solution.py:558
  54.7 7.6 %collective-permute-start.12 = (f32[2,8,128]{2,1,0:T(8,128)S(1)}, f32[2,8,128]{2,1,0:T(8,128)S(1)}, u32[]{:S(2)}, u32[]{:S(2)}) collective-permute-start(f32[2,8,128]{2,1,0:T(8,128)S(1)} %pad_maximum_fusion.5.refs_4_), channel_id=1, source_target_pairs={{0,128},{32,160},{64,192},{96,224},{128,0},{160,32},{192,64},{224,... | collective-permute-start | bytes 24584 | tf_op jit(solution)/shard_map/ppermute | solution.py:558
  62.4 4.1 %collective-permute-start.13 = (f32[2,8,128]{2,1,0:T(8,128)S(1)}, f32[2,8,128]{2,1,0:T(8,128)S(1)}, u32[]{:S(2)}, u32[]{:S(2)}) collective-permute-start(f32[2,8,128]{2,1,0:T(8,128)S(1)} %pad_maximum_fusion.6.refs_4_), channel_id=1, source_target_pairs={{0,1},{1,0},{2,3},{3,2},{4,5},{5,4},{6,7},{7,6},{8,9},{9,8},{10,11... | collective-permute-start | bytes 24584 | tf_op jit(solution)/shard_map/ppermute | solution.py:558
  66.5 5.2 %collective-permute-start.14 = (f32[2,8,128]{2,1,0:T(8,128)S(1)}, f32[2,8,128]{2,1,0:T(8,128)S(1)}, u32[]{:S(2)}, u32[]{:S(2)}) collective-permute-start(f32[2,8,128]{2,1,0:T(8,128)S(1)} %pad_maximum_fusion.7.refs_4_), channel_id=1, source_target_pairs={{0,2},{1,3},{2,0},{3,1},{4,6},{5,7},{6,4},{7,5},{8,10},{9,11},{10,... | collective-permute-start | bytes 24584 | tf_op jit(solution)/shard_map/ppermute | solution.py:558

commit v5 on v4

--- a/solution.py
+++ b/solution.py
@@ -110,20 +110,22 @@
     return join(out, jnp.where(row == 0, rolled(tail, 32, 1), tail))
 
 
-def pack_z(disp, dens, up, down, inner):
+def pack_z(main, up, down, inner, first):
     lane = lanes()
     for c in range(4):
         short = 0 if c < 3 else 1
         for k in range(4):
             top = bottom = own = jnp.zeros((8, 128), F32)
             for q in range(4):
-                x, t = k + 4 * (q // 2), 8 * (q % 2)
-                value = disp[c, x, t : t + 8, :] if c < 3 else dens[x, t : t + 8, :]
+                value = main[16 * c + 2 * (k + 4 * (q // 2)) + q % 2]
                 place = lane - 32 * q
                 top = jnp.where((place >= 16) & (place < 24), rolled(value, 32 * q + 24, 1), top)
                 bottom = jnp.where((place >= 7) & (place < 16 - short), rolled(value, 32 * q + 7, 1), bottom)
                 own = jnp.where((place >= 24) & (place < 32 - short), rolled(value, 32 * q + 24, 1), own)
                 own = jnp.where((place >= 0) & (place < 7), rolled(value, 32 * q + 7, 1), own)
+            if k == 0 and c < 3:
+                first[2 * c] = main[16 * c]
+                first[2 * c + 1] = main[16 * c + 1]
             up[4 * c + k] = top
             down[4 * c + k] = bottom
             inner[4 * c + k] = own
@@ -371,7 +373,7 @@
         highest[...] = most
         put_corners(corners, news[n])
 
-    in_groups(0, CELLS, GROUP, step)
+    in_groups(0, CELLS, 2, step)
 
 
 def load_kernel(base, cells, stress, highest, rhs, stiff, weight, explicit, field, reference, held, kept):
@@ -459,7 +461,7 @@
     elements = BX * BY * BZ * lax.axis_size("gx") * lax.axis_size("gy") * lax.axis_size("gz")
     top, total = everyone[0], everyone[1]
     scale = jnp.exp(reference[...] - top) / total * float(elements)
-    aggregate[...] = (top + jnp.log(total)) / power_scale
+    aggregate[...] = ((top + jnp.log(total)) / power_scale)[0:1, 0:1]
     scale = jnp.broadcast_to(scale[0:1, 0:1], (BY, 128))
     for c in range(3):
         for p in range(8):
@@ -538,13 +540,12 @@
 
 def on_device(displacement, density):
     plane = (ROWS, 128)
-    up, down, inner = kernel_call(pack_z, [(16, 8, 128)] * 3, "pack_z")(displacement, density)
+    main = jnp.concatenate([displacement.reshape(48, 8, 128), density.reshape(16, 8, 128)], axis=0)
+    up, down, inner, first = kernel_call(pack_z, [(16, 8, 128)] * 3 + [(6, 8, 128)], "pack_z")(main)
     below_z, above_z = passed(up, "gz", 1), passed(down, "gz", -1)
     strips = inner + below_z * within("gz", -1) + above_z * within("gz", 1)
-    mid = jnp.concatenate(
-        [displacement.reshape(48, 8, 128), density.reshape(16, 8, 128), strips], axis=0
-    )
-    far = jnp.concatenate([mid[t : t + n] for t, n in ((0, 2), (16, 2), (32, 2), (64, 1), (68, 1), (72, 1))], axis=0)
+    mid = jnp.concatenate([main, strips], axis=0)
+    far = jnp.concatenate([first, strips[0:1], strips[4:5], strips[8:9]], axis=0)
     low, high, far = passed(mid, "gx", 1), passed(mid, "gx", -1), passed(far, "gx", -2)
     up, down = kernel_call(pack_y, [(126, 8, 128), (141, 8, 128)], "pack_y")(mid, low, high, far)
     below, above = passed(up, "gy", 1), passed(down, "gy", -1)
@@ -593,7 +594,7 @@
     everyone = known
     adjoint, sens, aggregate = kernel_call(
         final_kernel,
-        [(3, BX, BY, BZ), (BX, BY, BZ), (8, 128)],
+        [(3, BX, BY, BZ), (BX, BY, BZ), (1, 1)],
         "final",
         [
             pltpu.VMEM((9, *plane), F32),
@@ -602,7 +603,7 @@
             pltpu.VMEM((12, BY, 128), F32),
         ],
     )(field, explicit, base, cells, reference, everyone)
-    return aggregate[0, 0], adjoint, sens
+    return aggregate.reshape(()), adjoint, sens
 
 
 def solution(mesh):

time: 74.9 us -> 73.2 us (0.977)
  local copies, waits for them, and re-layouts: 2.28 us -> 0.01 us
  other arithmetic: 1.11 us -> 2.11 us
    unnamed x9 -> x0, local copies, waits for them, and re-layouts: 1.77 us -> none
    concatenate x0 -> x2, other arithmetic: none -> 1 us  [the longest x1 0.99 us: on_device(): mid = jnp.concatenate([main, strips], axis=0)]
where the time goes in v5:
time: 73.2 us; the launch traced here: 73.1 us
  starting transfers between devices  25.8 us (35%)
  Pallas kernels  23.9 us (33%)
  waiting for transfers between devices  20.5 us (28%)
  other arithmetic  2.11 us (3%)
  between operations  0.8 us (1%)
    pallas_call x12, Pallas kernels, run(): pl.pallas_call(body, out_shape=[tile(shape) for shape in outs], in_specs=...  23.9 us
    ppermute x7, waiting for transfers between devices, passed(): lax.ppermute(block, axis, [(i, (i + distance) % count) for i in range(cou...  17.1 us
    ppermute x8, starting transfers between devices, run(): lax.ppermute(known, axis, [(i, i ^ hop) for i in range(lax.axis_size(axis...  13.6 us
    ppermute x7, starting transfers between devices, passed(): lax.ppermute(block, axis, [(i, (i + distance) % count) for i in range(cou...  12.2 us
    ppermute x8, waiting for transfers between devices, run(): lax.ppermute(known, axis, [(i, i ^ hop) for i in range(lax.axis_size(axis...  3.36 us
  transfers between devices with their start and end apart: 15, of which 9 were waited for; matrix products, arithmetic and copies ran while one was open for 0% of the time, Pallas kernels for 28%

profile of v5, /device:TPU:2, one launch (start us, length us, event | category | flops | bytes accessed | tf_op | source)
XLA Modules:
  0.0 73.1 jit_solution(6886580207209088939)
XLA Ops:
  0.6 1.0 %pad_maximum_fusion.1.main = f32[64,8,128]{2,1,0:T(8,128)S(1)} fusion(f32[16,8,128]{2,1,0:T(8,128)} %bitcast.5, f32[48,8,128]{2,1,0:T(8,128)} %bitcast.3), kind=kLoop, calls=%fused_computation.1 | loop fusion | flops 65536 | bytes 524288 | tf_op jit(solution)/shard_map/concatenate | solution.py:543
  1.6 0.2 pack_z.1
  1.8 1.7 %collective-permute-start = (f32[16,8,128]{2,1,0:T(8,128)S(1)}, f32[16,8,128]{2,1,0:T(8,128)S(1)}, u32[]{:S(2)}, u32[]{:S(2)}) collective-permute-start(f32[16,8,128]{2,1,0:T(8,128)S(1)} %get-tuple-element.39), channel_id=1, source_target_pairs={{0,1},{1,2},{2,3},{3,0},{4,5},{5,6},{6,7},{7,4},{8,9},{9,10},{10,1... | collective-permute-start | bytes 196616 | tf_op jit(solution)/shard_map/ppermute | solution.py:525
  3.5 1.7 %collective-permute-start.1 = (f32[16,8,128]{2,1,0:T(8,128)S(1)}, f32[16,8,128]{2,1,0:T(8,128)S(1)}, u32[]{:S(2)}, u32[]{:S(2)}) collective-permute-start(f32[16,8,128]{2,1,0:T(8,128)S(1)} %get-tuple-element.40), channel_id=1, source_target_pairs={{0,3},{1,0},{2,1},{3,2},{4,7},{5,4},{6,5},{7,6},{8,11},{9,8},{10,9... | collective-permute-start | bytes 196616 | tf_op jit(solution)/shard_map/ppermute | solution.py:525
  5.1 2.2 %collective-permute-done = f32[16,8,128]{2,1,0:T(8,128)S(1)} collective-permute-done((f32[16,8,128]{2,1,0:T(8,128)S(1)}, f32[16,8,128]{2,1,0:T(8,128)S(1)}, u32[]{:S(2)}, u32[]{:S(2)}) %collective-permute-start) | collective-permute-done | bytes 65568 | tf_op jit(solution)/shard_map/ppermute | solution.py:525
  7.4 0.4 collective-permute-done.1
  7.8 1.0 %pad_maximum_fusion.mid.refs_0_ = f32[80,8,128]{2,1,0:T(8,128)S(1)} fusion(f32[16,8,128]{2,1,0:T(8,128)S(1)} %multiply_add_fusion, f32[16,8,128]{2,1,0:T(8,128)} %bitcast.6, f32[48,8,128]{2,1,0:T(8,128)} %bitcast.4), kind=kLoop, calls=%fused_computation | loop fusion | flops 163840 | bytes 655360 | tf_op jit(solution)/shard_map/concatenate | solution.py:547
  8.8 5.9 %collective-permute-start.3 = (f32[80,8,128]{2,1,0:T(8,128)S(1)}, f32[80,8,128]{2,1,0:T(8,128)S(1)}, u32[]{:S(2)}, u32[]{:S(2)}) collective-permute-start(f32[80,8,128]{2,1,0:T(8,128)S(1)} %pad_maximum_fusion.mid.refs_0_), channel_id=1, source_target_pairs={{0,224},{32,0},{64,32},{96,64},{128,96},{160,128},{192,160},{224,1... | collective-permute-start | bytes 983048 | tf_op jit(solution)/shard_map/ppermute | solution.py:525
  14.7 0.0 collective-permute-start.2
  14.7 2.5 %collective-permute-start.4 = (f32[9,8,128]{2,1,0:T(8,128)S(1)}, f32[9,8,128]{2,1,0:T(8,128)S(1)}, u32[]{:S(2)}, u32[]{:S(2)}) collective-permute-start(f32[9,8,128]{2,1,0:T(8,128)S(1)} %pad_maximum_fusion.2), channel_id=1, source_target_pairs={{0,192},{32,224},{64,0},{96,32},{128,64},{160,96},{192,128},{224,1... | collective-permute-start | bytes 110600 | tf_op jit(solution)/shard_map/ppermute | solution.py:525
  17.2 4.6 %collective-permute-done.4.far.refs_3_ = f32[9,8,128]{2,1,0:T(8,128)S(1)} collective-permute-done((f32[9,8,128]{2,1,0:T(8,128)S(1)}, f32[9,8,128]{2,1,0:T(8,128)S(1)}, u32[]{:S(2)}, u32[]{:S(2)}) %collective-permute-start.4) | collective-permute-done | bytes 36896 | tf_op jit(solution)/shard_map/ppermute | solution.py:525
  21.8 0.0 collective-permute-done.3.high.refs_2_
  21.8 1.8 %collective-permute-done.2.low.refs_1_ = f32[80,8,128]{2,1,0:T(8,128)S(1)} collective-permute-done((f32[80,8,128]{2,1,0:T(8,128)S(1)}, f32[80,8,128]{2,1,0:T(8,128)S(1)}, u32[]{:S(2)}, u32[]{:S(2)}) %collective-permute-start.2) | collective-permute-done | bytes 327712 | tf_op jit(solution)/shard_map/ppermute | solution.py:525
  23.6 0.2 pack_y.1
  23.8 0.0 collective-permute-start.6
  23.8 0.5 collective-permute-start.5
  24.3 8.0 %collective-permute-done.5.below.refs_4_ = f32[126,8,128]{2,1,0:T(8,128)S(1)} collective-permute-done((f32[126,8,128]{2,1,0:T(8,128)S(1)}, f32[126,8,128]{2,1,0:T(8,128)S(1)}, u32[]{:S(2)}, u32[]{:S(2)}) %collective-permute-start.5) | collective-permute-done | bytes 516128 | tf_op jit(solution)/shard_map/ppermute | solution.py:525
  32.4 0.0 collective-permute-done.6.above.refs_5_
  32.4 0.6 own.1.refs_6_
  33.0 0.6 collective-permute-start.7
  33.5 0.4 widen.1
  34.0 0.4 collective-permute-done.7
  34.4 1.7 %collective-permute-start.8 = (f32[2,8,128]{2,1,0:T(8,128)S(1)}, f32[2,8,128]{2,1,0:T(8,128)S(1)}, u32[]{:S(2)}, u32[]{:S(2)}) collective-permute-start(f32[2,8,128]{2,1,0:T(8,128)S(1)} %pad_maximum_fusion.3.refs_4_), channel_id=1, source_target_pairs={{0,8},{4,12},{8,0},{12,4},{16,24},{20,28},{24,16},{28,20},{1,9},{5... | collective-permute-start | bytes 24584 | tf_op jit(solution)/shard_map/ppermute | solution.py:559
  36.1 3.4 %stress.1 = (f32[6,24,40,128]{3,2,1,0:T(8,128)S(1)}, f32[24,40,128]{2,1,0:T(8,128)S(1)}, f32[40,128]{1,0:T(8,128)S(1)}, f32[2,8,128]{2,1,0:T(8,128)S(1)}) custom-call(f32[3,25,40,128]{3,2,1,0:T(8,128)S(1)} %get-tuple-element.44.refs_0_, f32[3,25,8,128]{3,2,1,0:T(8,128)S(1)} %get-tuple-element.45.refs_1_, f32[3,25,8,128]{3,2,1,0:T(8,128)S(1)} %get-tuple-element.46.refs_2_, ...), custom_call_target="tpu_custom_call" | custom-call | flops 20000000 | bytes 1000000 | tf_op jit(solution)/shard_map/stress/pallas_call | solution.py:40
  39.4 0.0 collective-permute-done.8
  39.5 1.3 %collective-permute-start.9 = (f32[2,8,128]{2,1,0:T(8,128)S(1)}, f32[2,8,128]{2,1,0:T(8,128)S(1)}, u32[]{:S(2)}, u32[]{:S(2)}) collective-permute-start(f32[2,8,128]{2,1,0:T(8,128)S(1)} %pad_maximum_fusion.4.refs_4_), channel_id=1, source_target_pairs={{0,16},{4,20},{8,24},{12,28},{16,0},{20,4},{24,8},{28,12},{1,17},{... | collective-permute-start | bytes 24584 | tf_op jit(solution)/shard_map/ppermute | solution.py:559
  40.8 2.9 %load.1 = (f32[3,24,40,128]{3,2,1,0:T(8,128)S(1)}, f32[24,40,128]{2,1,0:T(8,128)S(1)}, f32[24,40,128]{2,1,0:T(8,128)S(1)}, f32[24,40,128]{2,1,0:T(8,128)S(1)}, f...) custom-call(f32[6,24,40,128]{3,2,1,0:T(8,128)S(1)} %get-tuple-element.49.refs_0_.base, ...), custom_call_target="tpu_custom_call" | custom-call | flops 20000000 | bytes 1000000 | tf_op jit(solution)/shard_map/load/pallas_call | solution.py:40
  43.6 1.1 %collective-permute-done.9 = f32[2,8,128]{2,1,0:T(8,128)S(1)} collective-permute-done((f32[2,8,128]{2,1,0:T(8,128)S(1)}, f32[2,8,128]{2,1,0:T(8,128)S(1)}, u32[]{:S(2)}, u32[]{:S(2)}) %collective-permute-start.9) | collective-permute-done | bytes 8224 | tf_op jit(solution)/shard_map/ppermute | solution.py:559
  44.7 0.1 collective-permute-start.10
  44.8 3.2 %sweep1.1 = (f32[3,25,40,128]{3,2,1,0:T(8,128)S(1)}, f32[2,8,128]{2,1,0:T(8,128)S(1)}) custom-call(f32[3,25,40,128]{3,2,1,0:T(8,128)S(1)} %get-tuple-element.53.refs_0_, f32[3,24,40,128]{3,2,1,0:T(8,128)S(1)} %get-tuple-element.54.refs_1_, f32[24,40,128]{2,1,0:T(8,128)S(1)} %get-tuple-element.55.refs_2_, ...), custom_call_target="tpu_custom_call", output_to_operand_aliasing={{0}: (0, {})} | custom-call | flops 20000000 | bytes 1000000 | tf_op jit(solution)/shard_map/sweep1/pallas_call | solution.py:40
  48.0 0.4 collective-permute-done.10
  48.5 1.8 %collective-permute-start.11 = (f32[2,8,128]{2,1,0:T(8,128)S(1)}, f32[2,8,128]{2,1,0:T(8,128)S(1)}, u32[]{:S(2)}, u32[]{:S(2)}) collective-permute-start(f32[2,8,128]{2,1,0:T(8,128)S(1)} %pad_maximum_fusion.6.refs_4_), channel_id=1, source_target_pairs={{0,64},{32,96},{64,0},{96,32},{128,192},{160,224},{192,128},{224,1... | collective-permute-start | bytes 24584 | tf_op jit(solution)/shard_map/ppermute | solution.py:559
  50.3 3.2 %sweep2.1 = (f32[3,25,40,128]{3,2,1,0:T(8,128)S(1)}, f32[2,8,128]{2,1,0:T(8,128)S(1)}) custom-call(f32[3,25,40,128]{3,2,1,0:T(8,128)S(1)} %get-tuple-element.58.refs_0_, f32[3,24,40,128]{3,2,1,0:T(8,128)S(1)} %get-tuple-element.54.refs_1_, f32[24,40,128]{2,1,0:T(8,128)S(1)} %get-tuple-element.55.refs_2_, ...), custom_call_target="tpu_custom_call", output_to_operand_aliasing={{0}: (0, {})} | custom-call | flops 20000000 | bytes 1000000 | tf_op jit(solution)/shard_map/sweep2/pallas_call | solution.py:40
  53.5 0.0 collective-permute-done.11
  53.6 3.5 %collective-permute-start.12 = (f32[2,8,128]{2,1,0:T(8,128)S(1)}, f32[2,8,128]{2,1,0:T(8,128)S(1)}, u32[]{:S(2)}, u32[]{:S(2)}) collective-permute-start(f32[2,8,128]{2,1,0:T(8,128)S(1)} %pad_maximum_fusion.7.refs_4_), channel_id=1, source_target_pairs={{0,128},{32,160},{64,192},{96,224},{128,0},{160,32},{192,64},{224,... | collective-permute-start | bytes 24584 | tf_op jit(solution)/shard_map/ppermute | solution.py:559
  57.0 2.8 %sweep3.1 = (f32[3,25,40,128]{3,2,1,0:T(8,128)S(1)}, f32[2,8,128]{2,1,0:T(8,128)S(1)}) custom-call(f32[3,25,40,128]{3,2,1,0:T(8,128)S(1)} %get-tuple-element.60.refs_0_, f32[3,24,40,128]{3,2,1,0:T(8,128)S(1)} %get-tuple-element.54.refs_1_, f32[24,40,128]{2,1,0:T(8,128)S(1)} %get-tuple-element.55.refs_2_, ...), custom_call_target="tpu_custom_call", output_to_operand_aliasing={{0}: (0, {})} | custom-call | flops 20000000 | bytes 1000000 | tf_op jit(solution)/shard_map/sweep3/pallas_call | solution.py:40
  59.8 1.4 %collective-permute-done.12 = f32[2,8,128]{2,1,0:T(8,128)S(1)} collective-permute-done((f32[2,8,128]{2,1,0:T(8,128)S(1)}, f32[2,8,128]{2,1,0:T(8,128)S(1)}, u32[]{:S(2)}, u32[]{:S(2)}) %collective-permute-start.12) | collective-permute-done | bytes 8224 | tf_op jit(solution)/shard_map/ppermute | solution.py:559
  61.2 1.8 %collective-permute-start.13 = (f32[2,8,128]{2,1,0:T(8,128)S(1)}, f32[2,8,128]{2,1,0:T(8,128)S(1)}, u32[]{:S(2)}, u32[]{:S(2)}) collective-permute-start(f32[2,8,128]{2,1,0:T(8,128)S(1)} %pad_maximum_fusion.8.refs_4_), channel_id=1, source_target_pairs={{0,1},{1,0},{2,3},{3,2},{4,5},{5,4},{6,7},{7,6},{8,9},{9,8},{10,11... | collective-permute-start | bytes 24584 | tf_op jit(solution)/shard_map/ppermute | solution.py:559
  63.0 2.3 %sweep4.1 = (f32[3,25,40,128]{3,2,1,0:T(8,128)S(1)}, f32[2,8,128]{2,1,0:T(8,128)S(1)}) custom-call(f32[3,25,40,128]{3,2,1,0:T(8,128)S(1)} %get-tuple-element.62.refs_0_, f32[3,24,40,128]{3,2,1,0:T(8,128)S(1)} %get-tuple-element.54.refs_1_, f32[24,40,128]{2,1,0:T(8,128)S(1)} %get-tuple-element.55.refs_2_, ...), custom_call_target="tpu_custom_call", output_to_operand_aliasing={{0}: (0, {})} | custom-call | flops 20000000 | bytes 1000000 | tf_op jit(solution)/shard_map/sweep4/pallas_call | solution.py:40
  65.4 0.0 collective-permute-done.13
  65.4 2.9 %collective-permute-start.14 = (f32[2,8,128]{2,1,0:T(8,128)S(1)}, f32[2,8,128]{2,1,0:T(8,128)S(1)}, u32[]{:S(2)}, u32[]{:S(2)}) collective-permute-start(f32[2,8,128]{2,1,0:T(8,128)S(1)} %pad_maximum_fusion.9.refs_4_), channel_id=1, source_target_pairs={{0,2},{1,3},{2,0},{3,1},{4,6},{5,7},{6,4},{7,5},{8,10},{9,11},{10,... | collective-permute-start | bytes 24584 | tf_op jit(solution)/shard_map/ppermute | solution.py:559
  68.3 2.3 %sweep5.1 = (f32[3,25,40,128]{3,2,1,0:T(8,128)S(1)}, f32[2,8,128]{2,1,0:T(8,128)S(1)}) custom-call(f32[3,25,40,128]{3,2,1,0:T(8,128)S(1)} %get-tuple-element.64.refs_0_, f32[3,24,40,128]{3,2,1,0:T(8,128)S(1)} %get-tuple-element.54.refs_1_, f32[24,40,128]{2,1,0:T(8,128)S(1)} %get-tuple-element.55.refs_2_, ...), custom_call_target="tpu_custom_call", output_to_operand_aliasing={{0}: (0, {})} | custom-call | flops 20000000 | bytes 1000000 | tf_op jit(solution)/shard_map/sweep5/pallas_call | solution.py:40
  70.6 0.0 collective-permute-done.14
  70.6 2.5 %final.1 = (f32[3,8,16,128]{3,2,1,0:T(8,128)}, f32[8,16,128]{2,1,0:T(8,128)}, f32[1,1]{1,0:T(1,128)}) custom-call(f32[3,25,40,128]{3,2,1,0:T(8,128)S(1)} %get-tuple-element.66.field, f32[24,40,128]{2,1,0:T(8,128)S(1)} %get-tuple-element.67.explicit, f32[6,24,40,128]{3,2,1,0:T(8,128)S(1)} %get-tuple-element.49.refs_0_.base, ...), custom_call_target="tpu_custom_call" | custom-call | flops 1000000 | bytes 1000000 | tf_op jit(solution)/shard_map/final/pallas_call | solution.py:40
  (19 shorter events, 0.1 us)
Async XLA Ops:
  1.8 5.6 %collective-permute-start = (f32[16,8,128]{2,1,0:T(8,128)S(1)}, f32[16,8,128]{2,1,0:T(8,128)S(1)}, u32[]{:S(2)}, u32[]{:S(2)}) collective-permute-start(f32[16,8,128]{2,1,0:T(8,128)S(1)} %get-tuple-element.39), channel_id=1, source_target_pairs={{0,1},{1,2},{2,3},{3,0},{4,5},{5,6},{6,7},{7,4},{8,9},{9,10},{10,1... | collective-permute-start | bytes 196616 | tf_op jit(solution)/shard_map/ppermute | solution.py:525
  3.5 4.3 %collective-permute-start.1 = (f32[16,8,128]{2,1,0:T(8,128)S(1)}, f32[16,8,128]{2,1,0:T(8,128)S(1)}, u32[]{:S(2)}, u32[]{:S(2)}) collective-permute-start(f32[16,8,128]{2,1,0:T(8,128)S(1)} %get-tuple-element.40), channel_id=1, source_target_pairs={{0,3},{1,0},{2,1},{3,2},{4,7},{5,4},{6,5},{7,6},{8,11},{9,8},{10,9... | collective-permute-start | bytes 196616 | tf_op jit(solution)/shard_map/ppermute | solution.py:525
  8.8 13.1 %collective-permute-start.3 = (f32[80,8,128]{2,1,0:T(8,128)S(1)}, f32[80,8,128]{2,1,0:T(8,128)S(1)}, u32[]{:S(2)}, u32[]{:S(2)}) collective-permute-start(f32[80,8,128]{2,1,0:T(8,128)S(1)} %pad_maximum_fusion.mid.refs_0_), channel_id=1, source_target_pairs={{0,224},{32,0},{64,32},{96,64},{128,96},{160,128},{192,160},{224,1... | collective-permute-start | bytes 983048 | tf_op jit(solution)/shard_map/ppermute | solution.py:525
  14.7 9.0 %collective-permute-start.2 = (f32[80,8,128]{2,1,0:T(8,128)S(1)}, f32[80,8,128]{2,1,0:T(8,128)S(1)}, u32[]{:S(2)}, u32[]{:S(2)}) collective-permute-start(f32[80,8,128]{2,1,0:T(8,128)S(1)} %pad_maximum_fusion.mid.refs_0_), channel_id=1, source_target_pairs={{0,32},{32,64},{64,96},{96,128},{128,160},{160,192},{192,224},{224... | collective-permute-start | bytes 983048 | tf_op jit(solution)/shard_map/ppermute | solution.py:525
  14.7 7.1 %collective-permute-start.4 = (f32[9,8,128]{2,1,0:T(8,128)S(1)}, f32[9,8,128]{2,1,0:T(8,128)S(1)}, u32[]{:S(2)}, u32[]{:S(2)}) collective-permute-start(f32[9,8,128]{2,1,0:T(8,128)S(1)} %pad_maximum_fusion.2), channel_id=1, source_target_pairs={{0,192},{32,224},{64,0},{96,32},{128,64},{160,96},{192,128},{224,1... | collective-permute-start | bytes 110600 | tf_op jit(solution)/shard_map/ppermute | solution.py:525
  23.8 8.6 %collective-permute-start.6 = (f32[141,8,128]{2,1,0:T(8,128)S(1)}, f32[141,8,128]{2,1,0:T(8,128)S(1)}, u32[]{:S(2)}, u32[]{:S(2)}) collective-permute-start(f32[141,8,128]{2,1,0:T(8,128)S(1)} %get-tuple-element.43), channel_id=1, source_target_pairs={{0,28},{4,0},{8,4},{12,8},{16,12},{20,16},{24,20},{28,24},{1,29},{... | collective-permute-start | bytes 1732616 | tf_op jit(solution)/shard_map/ppermute | solution.py:525
  23.8 8.5 %collective-permute-start.5 = (f32[126,8,128]{2,1,0:T(8,128)S(1)}, f32[126,8,128]{2,1,0:T(8,128)S(1)}, u32[]{:S(2)}, u32[]{:S(2)}) collective-permute-start(f32[126,8,128]{2,1,0:T(8,128)S(1)} %get-tuple-element.42), channel_id=1, source_target_pairs={{0,4},{4,8},{8,12},{12,16},{16,20},{20,24},{24,28},{28,0},{1,5},{5... | collective-permute-start | bytes 1548296 | tf_op jit(solution)/shard_map/ppermute | solution.py:525
  33.0 1.4 %collective-permute-start.7 = (f32[2,8,128]{2,1,0:T(8,128)S(1)}, f32[2,8,128]{2,1,0:T(8,128)S(1)}, u32[]{:S(2)}, u32[]{:S(2)}) collective-permute-start(f32[2,8,128]{2,1,0:T(8,128)S(1)} %own.1.refs_6_), channel_id=1, source_target_pairs={{0,4},{4,0},{8,12},{12,8},{16,20},{20,16},{24,28},{28,24},{1,5},{5... | collective-permute-start | bytes 24584 | tf_op jit(solution)/shard_map/ppermute | solution.py:559
  34.4 5.0 %collective-permute-start.8 = (f32[2,8,128]{2,1,0:T(8,128)S(1)}, f32[2,8,128]{2,1,0:T(8,128)S(1)}, u32[]{:S(2)}, u32[]{:S(2)}) collective-permute-start(f32[2,8,128]{2,1,0:T(8,128)S(1)} %pad_maximum_fusion.3.refs_4_), channel_id=1, source_target_pairs={{0,8},{4,12},{8,0},{12,4},{16,24},{20,28},{24,16},{28,20},{1,9},{5... | collective-permute-start | bytes 24584 | tf_op jit(solution)/shard_map/ppermute | solution.py:559
  39.5 5.2 %collective-permute-start.9 = (f32[2,8,128]{2,1,0:T(8,128)S(1)}, f32[2,8,128]{2,1,0:T(8,128)S(1)}, u32[]{:S(2)}, u32[]{:S(2)}) collective-permute-start(f32[2,8,128]{2,1,0:T(8,128)S(1)} %pad_maximum_fusion.4.refs_4_), channel_id=1, source_target_pairs={{0,16},{4,20},{8,24},{12,28},{16,0},{20,4},{24,8},{28,12},{1,17},{... | collective-permute-start | bytes 24584 | tf_op jit(solution)/shard_map/ppermute | solution.py:559
  44.7 3.7 %collective-permute-start.10 = (f32[2,8,128]{2,1,0:T(8,128)S(1)}, f32[2,8,128]{2,1,0:T(8,128)S(1)}, u32[]{:S(2)}, u32[]{:S(2)}) collective-permute-start(f32[2,8,128]{2,1,0:T(8,128)S(1)} %pad_maximum_fusion.5.refs_4_), channel_id=1, source_target_pairs={{0,32},{32,0},{64,96},{96,64},{128,160},{160,128},{192,224},{224,1... | collective-permute-start | bytes 24584 | tf_op jit(solution)/shard_map/ppermute | solution.py:559
  48.5 5.0 %collective-permute-start.11 = (f32[2,8,128]{2,1,0:T(8,128)S(1)}, f32[2,8,128]{2,1,0:T(8,128)S(1)}, u32[]{:S(2)}, u32[]{:S(2)}) collective-permute-start(f32[2,8,128]{2,1,0:T(8,128)S(1)} %pad_maximum_fusion.6.refs_4_), channel_id=1, source_target_pairs={{0,64},{32,96},{64,0},{96,32},{128,192},{160,224},{192,128},{224,1... | collective-permute-start | bytes 24584 | tf_op jit(solution)/shard_map/ppermute | solution.py:559
  53.6 7.6 %collective-permute-start.12 = (f32[2,8,128]{2,1,0:T(8,128)S(1)}, f32[2,8,128]{2,1,0:T(8,128)S(1)}, u32[]{:S(2)}, u32[]{:S(2)}) collective-permute-start(f32[2,8,128]{2,1,0:T(8,128)S(1)} %pad_maximum_fusion.7.refs_4_), channel_id=1, source_target_pairs={{0,128},{32,160},{64,192},{96,224},{128,0},{160,32},{192,64},{224,... | collective-permute-start | bytes 24584 | tf_op jit(solution)/shard_map/ppermute | solution.py:559
  61.2 4.1 %collective-permute-start.13 = (f32[2,8,128]{2,1,0:T(8,128)S(1)}, f32[2,8,128]{2,1,0:T(8,128)S(1)}, u32[]{:S(2)}, u32[]{:S(2)}) collective-permute-start(f32[2,8,128]{2,1,0:T(8,128)S(1)} %pad_maximum_fusion.8.refs_4_), channel_id=1, source_target_pairs={{0,1},{1,0},{2,3},{3,2},{4,5},{5,4},{6,7},{7,6},{8,9},{9,8},{10,11... | collective-permute-start | bytes 24584 | tf_op jit(solution)/shard_map/ppermute | solution.py:559
  65.4 5.2 %collective-permute-start.14 = (f32[2,8,128]{2,1,0:T(8,128)S(1)}, f32[2,8,128]{2,1,0:T(8,128)S(1)}, u32[]{:S(2)}, u32[]{:S(2)}) collective-permute-start(f32[2,8,128]{2,1,0:T(8,128)S(1)} %pad_maximum_fusion.9.refs_4_), channel_id=1, source_target_pairs={{0,2},{1,3},{2,0},{3,1},{4,6},{5,7},{6,4},{7,5},{8,10},{9,11},{10,... | collective-permute-start | bytes 24584 | tf_op jit(solution)/shard_map/ppermute | solution.py:559

commit v6 on v5

--- a/solution.py
+++ b/solution.py
@@ -541,6 +541,7 @@
 def on_device(displacement, density):
     plane = (ROWS, 128)
     main = jnp.concatenate([displacement.reshape(48, 8, 128), density.reshape(16, 8, 128)], axis=0)
+    main = lax.optimization_barrier(main)
     up, down, inner, first = kernel_call(pack_z, [(16, 8, 128)] * 3 + [(6, 8, 128)], "pack_z")(main)
     below_z, above_z = passed(up, "gz", 1), passed(down, "gz", -1)
     strips = inner + below_z * within("gz", -1) + above_z * within("gz", 1)

time: 73.2 us -> 72.3 us (0.988)
  other arithmetic: 2.11 us -> 1.14 us
    concatenate x1, other arithmetic: 0.99 us -> 0.02 us  [on_device(): mid = jnp.concatenate([main, strips], axis=0)]
where the time goes in v6:
time: 72.3 us; the launch traced here: 72.2 us
  starting transfers between devices  25.8 us (36%)
  Pallas kernels  23.9 us (33%)
  waiting for transfers between devices  20.5 us (28%)
  other arithmetic  1.14 us (2%)
  between operations  0.81 us (1%)
    pallas_call x12, Pallas kernels, run(): pl.pallas_call(body, out_shape=[tile(shape) for shape in outs], in_specs=...  23.9 us
    ppermute x7, waiting for transfers between devices, passed(): lax.ppermute(block, axis, [(i, (i + distance) % count) for i in range(cou...  17.1 us
    ppermute x8, starting transfers between devices, run(): lax.ppermute(known, axis, [(i, i ^ hop) for i in range(lax.axis_size(axis...  13.6 us
    ppermute x7, starting transfers between devices, passed(): lax.ppermute(block, axis, [(i, (i + distance) % count) for i in range(cou...  12.2 us
    ppermute x8, waiting for transfers between devices, run(): lax.ppermute(known, axis, [(i, i ^ hop) for i in range(lax.axis_size(axis...  3.36 us
  transfers between devices with their start and end apart: 15, of which 9 were waited for; matrix products, arithmetic and copies ran while one was open for 0% of the time, Pallas kernels for 28%

profile of v6, /device:TPU:2, one launch (start us, length us, event | category | flops | bytes accessed | tf_op | source)
XLA Modules:
  0.0 72.2 jit_solution(4654166550583509954)
XLA Ops:
  0.6 1.0 %pad_maximum_fusion.1.main = f32[64,8,128]{2,1,0:T(8,128)S(1)} fusion(f32[16,8,128]{2,1,0:T(8,128)} %bitcast.4, f32[48,8,128]{2,1,0:T(8,128)} %bitcast.3), kind=kLoop, calls=%fused_computation.1 | loop fusion | flops 65536 | bytes 524288 | tf_op jit(solution)/shard_map/concatenate | solution.py:543
  1.6 0.2 pack_z.1
  1.8 1.7 %collective-permute-start = (f32[16,8,128]{2,1,0:T(8,128)S(1)}, f32[16,8,128]{2,1,0:T(8,128)S(1)}, u32[]{:S(2)}, u32[]{:S(2)}) collective-permute-start(f32[16,8,128]{2,1,0:T(8,128)S(1)} %get-tuple-element.39), channel_id=1, source_target_pairs={{0,1},{1,2},{2,3},{3,0},{4,5},{5,6},{6,7},{7,4},{8,9},{9,10},{10,1... | collective-permute-start | bytes 196616 | tf_op jit(solution)/shard_map/ppermute | solution.py:525
  3.5 1.7 %collective-permute-start.1 = (f32[16,8,128]{2,1,0:T(8,128)S(1)}, f32[16,8,128]{2,1,0:T(8,128)S(1)}, u32[]{:S(2)}, u32[]{:S(2)}) collective-permute-start(f32[16,8,128]{2,1,0:T(8,128)S(1)} %get-tuple-element.40), channel_id=1, source_target_pairs={{0,3},{1,0},{2,1},{3,2},{4,7},{5,4},{6,5},{7,6},{8,11},{9,8},{10,9... | collective-permute-start | bytes 196616 | tf_op jit(solution)/shard_map/ppermute | solution.py:525
  5.1 2.2 %collective-permute-done = f32[16,8,128]{2,1,0:T(8,128)S(1)} collective-permute-done((f32[16,8,128]{2,1,0:T(8,128)S(1)}, f32[16,8,128]{2,1,0:T(8,128)S(1)}, u32[]{:S(2)}, u32[]{:S(2)}) %collective-permute-start) | collective-permute-done | bytes 65568 | tf_op jit(solution)/shard_map/ppermute | solution.py:525
  7.4 0.4 collective-permute-done.1
  7.8 5.9 %collective-permute-start.3 = (f32[80,8,128]{2,1,0:T(8,128)S(1)}, f32[80,8,128]{2,1,0:T(8,128)S(1)}, u32[]{:S(2)}, u32[]{:S(2)}) collective-permute-start(f32[80,8,128]{2,1,0:T(8,128)S(1)} %pad_maximum_fusion.mid.refs_0_), channel_id=1, source_target_pairs={{0,224},{32,0},{64,32},{96,64},{128,96},{160,128},{192,160},{224,1... | collective-permute-start | bytes 983048 | tf_op jit(solution)/shard_map/ppermute | solution.py:525
  13.7 0.0 collective-permute-start.2
  13.7 2.5 %collective-permute-start.4 = (f32[9,8,128]{2,1,0:T(8,128)S(1)}, f32[9,8,128]{2,1,0:T(8,128)S(1)}, u32[]{:S(2)}, u32[]{:S(2)}) collective-permute-start(f32[9,8,128]{2,1,0:T(8,128)S(1)} %pad_maximum_fusion.2), channel_id=1, source_target_pairs={{0,192},{32,224},{64,0},{96,32},{128,64},{160,96},{192,128},{224,1... | collective-permute-start | bytes 110600 | tf_op jit(solution)/shard_map/ppermute | solution.py:525
  16.2 4.6 %collective-permute-done.4.far.refs_3_ = f32[9,8,128]{2,1,0:T(8,128)S(1)} collective-permute-done((f32[9,8,128]{2,1,0:T(8,128)S(1)}, f32[9,8,128]{2,1,0:T(8,128)S(1)}, u32[]{:S(2)}, u32[]{:S(2)}) %collective-permute-start.4) | collective-permute-done | bytes 36896 | tf_op jit(solution)/shard_map/ppermute | solution.py:525
  20.8 0.0 collective-permute-done.3.high.refs_2_
  20.9 1.8 %collective-permute-done.2.low.refs_1_ = f32[80,8,128]{2,1,0:T(8,128)S(1)} collective-permute-done((f32[80,8,128]{2,1,0:T(8,128)S(1)}, f32[80,8,128]{2,1,0:T(8,128)S(1)}, u32[]{:S(2)}, u32[]{:S(2)}) %collective-permute-start.2) | collective-permute-done | bytes 327712 | tf_op jit(solution)/shard_map/ppermute | solution.py:525
  22.7 0.2 pack_y.1
  22.9 0.0 collective-permute-start.6
  22.9 0.5 collective-permute-start.5
  23.4 8.0 %collective-permute-done.5.below.refs_4_ = f32[126,8,128]{2,1,0:T(8,128)S(1)} collective-permute-done((f32[126,8,128]{2,1,0:T(8,128)S(1)}, f32[126,8,128]{2,1,0:T(8,128)S(1)}, u32[]{:S(2)}, u32[]{:S(2)}) %collective-permute-start.5) | collective-permute-done | bytes 516128 | tf_op jit(solution)/shard_map/ppermute | solution.py:525
  31.4 0.0 collective-permute-done.6.above.refs_5_
  31.4 0.6 own.1.refs_6_
  32.0 0.6 collective-permute-start.7
  32.6 0.4 widen.1
  33.0 0.4 collective-permute-done.7
  33.4 1.7 %collective-permute-start.8 = (f32[2,8,128]{2,1,0:T(8,128)S(1)}, f32[2,8,128]{2,1,0:T(8,128)S(1)}, u32[]{:S(2)}, u32[]{:S(2)}) collective-permute-start(f32[2,8,128]{2,1,0:T(8,128)S(1)} %pad_maximum_fusion.3.refs_4_), channel_id=1, source_target_pairs={{0,8},{4,12},{8,0},{12,4},{16,24},{20,28},{24,16},{28,20},{1,9},{5... | collective-permute-start | bytes 24584 | tf_op jit(solution)/shard_map/ppermute | solution.py:560
  35.1 3.4 %stress.1 = (f32[6,24,40,128]{3,2,1,0:T(8,128)S(1)}, f32[24,40,128]{2,1,0:T(8,128)S(1)}, f32[40,128]{1,0:T(8,128)S(1)}, f32[2,8,128]{2,1,0:T(8,128)S(1)}) custom-call(f32[3,25,40,128]{3,2,1,0:T(8,128)S(1)} %get-tuple-element.44.refs_0_, f32[3,25,8,128]{3,2,1,0:T(8,128)S(1)} %get-tuple-element.45.refs_1_, f32[3,25,8,128]{3,2,1,0:T(8,128)S(1)} %get-tuple-element.46.refs_2_, ...), custom_call_target="tpu_custom_call" | custom-call | flops 20000000 | bytes 1000000 | tf_op jit(solution)/shard_map/stress/pallas_call | solution.py:40
  38.5 0.0 collective-permute-done.8
  38.5 1.3 %collective-permute-start.9 = (f32[2,8,128]{2,1,0:T(8,128)S(1)}, f32[2,8,128]{2,1,0:T(8,128)S(1)}, u32[]{:S(2)}, u32[]{:S(2)}) collective-permute-start(f32[2,8,128]{2,1,0:T(8,128)S(1)} %pad_maximum_fusion.4.refs_4_), channel_id=1, source_target_pairs={{0,16},{4,20},{8,24},{12,28},{16,0},{20,4},{24,8},{28,12},{1,17},{... | collective-permute-start | bytes 24584 | tf_op jit(solution)/shard_map/ppermute | solution.py:560
  39.8 2.9 %load.1 = (f32[3,24,40,128]{3,2,1,0:T(8,128)S(1)}, f32[24,40,128]{2,1,0:T(8,128)S(1)}, f32[24,40,128]{2,1,0:T(8,128)S(1)}, f32[24,40,128]{2,1,0:T(8,128)S(1)}, f...) custom-call(f32[6,24,40,128]{3,2,1,0:T(8,128)S(1)} %get-tuple-element.49.refs_0_.base, ...), custom_call_target="tpu_custom_call" | custom-call | flops 20000000 | bytes 1000000 | tf_op jit(solution)/shard_map/load/pallas_call | solution.py:40
  42.7 1.1 %collective-permute-done.9 = f32[2,8,128]{2,1,0:T(8,128)S(1)} collective-permute-done((f32[2,8,128]{2,1,0:T(8,128)S(1)}, f32[2,8,128]{2,1,0:T(8,128)S(1)}, u32[]{:S(2)}, u32[]{:S(2)}) %collective-permute-start.9) | collective-permute-done | bytes 8224 | tf_op jit(solution)/shard_map/ppermute | solution.py:560
  43.8 0.1 collective-permute-start.10
  43.9 3.2 %sweep1.1 = (f32[3,25,40,128]{3,2,1,0:T(8,128)S(1)}, f32[2,8,128]{2,1,0:T(8,128)S(1)}) custom-call(f32[3,25,40,128]{3,2,1,0:T(8,128)S(1)} %get-tuple-element.53.refs_0_, f32[3,24,40,128]{3,2,1,0:T(8,128)S(1)} %get-tuple-element.54.refs_1_, f32[24,40,128]{2,1,0:T(8,128)S(1)} %get-tuple-element.55.refs_2_, ...), custom_call_target="tpu_custom_call", output_to_operand_aliasing={{0}: (0, {})} | custom-call | flops 20000000 | bytes 1000000 | tf_op jit(solution)/shard_map/sweep1/pallas_call | solution.py:40
  47.1 0.4 collective-permute-done.10
  47.5 1.8 %collective-permute-start.11 = (f32[2,8,128]{2,1,0:T(8,128)S(1)}, f32[2,8,128]{2,1,0:T(8,128)S(1)}, u32[]{:S(2)}, u32[]{:S(2)}) collective-permute-start(f32[2,8,128]{2,1,0:T(8,128)S(1)} %pad_maximum_fusion.6.refs_4_), channel_id=1, source_target_pairs={{0,64},{32,96},{64,0},{96,32},{128,192},{160,224},{192,128},{224,1... | collective-permute-start | bytes 24584 | tf_op jit(solution)/shard_map/ppermute | solution.py:560
  49.3 3.2 %sweep2.1 = (f32[3,25,40,128]{3,2,1,0:T(8,128)S(1)}, f32[2,8,128]{2,1,0:T(8,128)S(1)}) custom-call(f32[3,25,40,128]{3,2,1,0:T(8,128)S(1)} %get-tuple-element.58.refs_0_, f32[3,24,40,128]{3,2,1,0:T(8,128)S(1)} %get-tuple-element.54.refs_1_, f32[24,40,128]{2,1,0:T(8,128)S(1)} %get-tuple-element.55.refs_2_, ...), custom_call_target="tpu_custom_call", output_to_operand_aliasing={{0}: (0, {})} | custom-call | flops 20000000 | bytes 1000000 | tf_op jit(solution)/shard_map/sweep2/pallas_call | solution.py:40
  52.6 0.0 collective-permute-done.11
  52.6 3.5 %collective-permute-start.12 = (f32[2,8,128]{2,1,0:T(8,128)S(1)}, f32[2,8,128]{2,1,0:T(8,128)S(1)}, u32[]{:S(2)}, u32[]{:S(2)}) collective-permute-start(f32[2,8,128]{2,1,0:T(8,128)S(1)} %pad_maximum_fusion.7.refs_4_), channel_id=1, source_target_pairs={{0,128},{32,160},{64,192},{96,224},{128,0},{160,32},{192,64},{224,... | collective-permute-start | bytes 24584 | tf_op jit(solution)/shard_map/ppermute | solution.py:560
  56.1 2.8 %sweep3.1 = (f32[3,25,40,128]{3,2,1,0:T(8,128)S(1)}, f32[2,8,128]{2,1,0:T(8,128)S(1)}) custom-call(f32[3,25,40,128]{3,2,1,0:T(8,128)S(1)} %get-tuple-element.60.refs_0_, f32[3,24,40,128]{3,2,1,0:T(8,128)S(1)} %get-tuple-element.54.refs_1_, f32[24,40,128]{2,1,0:T(8,128)S(1)} %get-tuple-element.55.refs_2_, ...), custom_call_target="tpu_custom_call", output_to_operand_aliasing={{0}: (0, {})} | custom-call | flops 20000000 | bytes 1000000 | tf_op jit(solution)/shard_map/sweep3/pallas_call | solution.py:40
  58.8 1.4 %collective-permute-done.12 = f32[2,8,128]{2,1,0:T(8,128)S(1)} collective-permute-done((f32[2,8,128]{2,1,0:T(8,128)S(1)}, f32[2,8,128]{2,1,0:T(8,128)S(1)}, u32[]{:S(2)}, u32[]{:S(2)}) %collective-permute-start.12) | collective-permute-done | bytes 8224 | tf_op jit(solution)/shard_map/ppermute | solution.py:560
  60.3 1.8 %collective-permute-start.13 = (f32[2,8,128]{2,1,0:T(8,128)S(1)}, f32[2,8,128]{2,1,0:T(8,128)S(1)}, u32[]{:S(2)}, u32[]{:S(2)}) collective-permute-start(f32[2,8,128]{2,1,0:T(8,128)S(1)} %pad_maximum_fusion.8.refs_4_), channel_id=1, source_target_pairs={{0,1},{1,0},{2,3},{3,2},{4,5},{5,4},{6,7},{7,6},{8,9},{9,8},{10,11... | collective-permute-start | bytes 24584 | tf_op jit(solution)/shard_map/ppermute | solution.py:560
  62.1 2.3 %sweep4.1 = (f32[3,25,40,128]{3,2,1,0:T(8,128)S(1)}, f32[2,8,128]{2,1,0:T(8,128)S(1)}) custom-call(f32[3,25,40,128]{3,2,1,0:T(8,128)S(1)} %get-tuple-element.62.refs_0_, f32[3,24,40,128]{3,2,1,0:T(8,128)S(1)} %get-tuple-element.54.refs_1_, f32[24,40,128]{2,1,0:T(8,128)S(1)} %get-tuple-element.55.refs_2_, ...), custom_call_target="tpu_custom_call", output_to_operand_aliasing={{0}: (0, {})} | custom-call | flops 20000000 | bytes 1000000 | tf_op jit(solution)/shard_map/sweep4/pallas_call | solution.py:40
  64.4 0.0 collective-permute-done.13
  64.4 2.9 %collective-permute-start.14 = (f32[2,8,128]{2,1,0:T(8,128)S(1)}, f32[2,8,128]{2,1,0:T(8,128)S(1)}, u32[]{:S(2)}, u32[]{:S(2)}) collective-permute-start(f32[2,8,128]{2,1,0:T(8,128)S(1)} %pad_maximum_fusion.9.refs_4_), channel_id=1, source_target_pairs={{0,2},{1,3},{2,0},{3,1},{4,6},{5,7},{6,4},{7,5},{8,10},{9,11},{10,... | collective-permute-start | bytes 24584 | tf_op jit(solution)/shard_map/ppermute | solution.py:560
  67.3 2.3 %sweep5.1 = (f32[3,25,40,128]{3,2,1,0:T(8,128)S(1)}, f32[2,8,128]{2,1,0:T(8,128)S(1)}) custom-call(f32[3,25,40,128]{3,2,1,0:T(8,128)S(1)} %get-tuple-element.64.refs_0_, f32[3,24,40,128]{3,2,1,0:T(8,128)S(1)} %get-tuple-element.54.refs_1_, f32[24,40,128]{2,1,0:T(8,128)S(1)} %get-tuple-element.55.refs_2_, ...), custom_call_target="tpu_custom_call", output_to_operand_aliasing={{0}: (0, {})} | custom-call | flops 20000000 | bytes 1000000 | tf_op jit(solution)/shard_map/sweep5/pallas_call | solution.py:40
  69.6 0.0 collective-permute-done.14
  69.7 2.5 %final.1 = (f32[3,8,16,128]{3,2,1,0:T(8,128)}, f32[8,16,128]{2,1,0:T(8,128)}, f32[1,1]{1,0:T(1,128)}) custom-call(f32[3,25,40,128]{3,2,1,0:T(8,128)S(1)} %get-tuple-element.66.field, f32[24,40,128]{2,1,0:T(8,128)S(1)} %get-tuple-element.67.explicit, f32[6,24,40,128]{3,2,1,0:T(8,128)S(1)} %get-tuple-element.49.refs_0_.base, ...), custom_call_target="tpu_custom_call" | custom-call | flops 1000000 | bytes 1000000 | tf_op jit(solution)/shard_map/final/pallas_call | solution.py:40
  (20 shorter events, 0.2 us)
Async XLA Ops:
  1.8 5.6 %collective-permute-start = (f32[16,8,128]{2,1,0:T(8,128)S(1)}, f32[16,8,128]{2,1,0:T(8,128)S(1)}, u32[]{:S(2)}, u32[]{:S(2)}) collective-permute-start(f32[16,8,128]{2,1,0:T(8,128)S(1)} %get-tuple-element.39), channel_id=1, source_target_pairs={{0,1},{1,2},{2,3},{3,0},{4,5},{5,6},{6,7},{7,4},{8,9},{9,10},{10,1... | collective-permute-start | bytes 196616 | tf_op jit(solution)/shard_map/ppermute | solution.py:525
  3.5 4.3 %collective-permute-start.1 = (f32[16,8,128]{2,1,0:T(8,128)S(1)}, f32[16,8,128]{2,1,0:T(8,128)S(1)}, u32[]{:S(2)}, u32[]{:S(2)}) collective-permute-start(f32[16,8,128]{2,1,0:T(8,128)S(1)} %get-tuple-element.40), channel_id=1, source_target_pairs={{0,3},{1,0},{2,1},{3,2},{4,7},{5,4},{6,5},{7,6},{8,11},{9,8},{10,9... | collective-permute-start | bytes 196616 | tf_op jit(solution)/shard_map/ppermute | solution.py:525
  7.8 13.1 %collective-permute-start.3 = (f32[80,8,128]{2,1,0:T(8,128)S(1)}, f32[80,8,128]{2,1,0:T(8,128)S(1)}, u32[]{:S(2)}, u32[]{:S(2)}) collective-permute-start(f32[80,8,128]{2,1,0:T(8,128)S(1)} %pad_maximum_fusion.mid.refs_0_), channel_id=1, source_target_pairs={{0,224},{32,0},{64,32},{96,64},{128,96},{160,128},{192,160},{224,1... | collective-permute-start | bytes 983048 | tf_op jit(solution)/shard_map/ppermute | solution.py:525
  13.7 9.0 %collective-permute-start.2 = (f32[80,8,128]{2,1,0:T(8,128)S(1)}, f32[80,8,128]{2,1,0:T(8,128)S(1)}, u32[]{:S(2)}, u32[]{:S(2)}) collective-permute-start(f32[80,8,128]{2,1,0:T(8,128)S(1)} %pad_maximum_fusion.mid.refs_0_), channel_id=1, source_target_pairs={{0,32},{32,64},{64,96},{96,128},{128,160},{160,192},{192,224},{224... | collective-permute-start | bytes 983048 | tf_op jit(solution)/shard_map/ppermute | solution.py:525
  13.7 7.1 %collective-permute-start.4 = (f32[9,8,128]{2,1,0:T(8,128)S(1)}, f32[9,8,128]{2,1,0:T(8,128)S(1)}, u32[]{:S(2)}, u32[]{:S(2)}) collective-permute-start(f32[9,8,128]{2,1,0:T(8,128)S(1)} %pad_maximum_fusion.2), channel_id=1, source_target_pairs={{0,192},{32,224},{64,0},{96,32},{128,64},{160,96},{192,128},{224,1... | collective-permute-start | bytes 110600 | tf_op jit(solution)/shard_map/ppermute | solution.py:525
  22.9 8.6 %collective-permute-start.6 = (f32[141,8,128]{2,1,0:T(8,128)S(1)}, f32[141,8,128]{2,1,0:T(8,128)S(1)}, u32[]{:S(2)}, u32[]{:S(2)}) collective-permute-start(f32[141,8,128]{2,1,0:T(8,128)S(1)} %get-tuple-element.43), channel_id=1, source_target_pairs={{0,28},{4,0},{8,4},{12,8},{16,12},{20,16},{24,20},{28,24},{1,29},{... | collective-permute-start | bytes 1732616 | tf_op jit(solution)/shard_map/ppermute | solution.py:525
  22.9 8.5 %collective-permute-start.5 = (f32[126,8,128]{2,1,0:T(8,128)S(1)}, f32[126,8,128]{2,1,0:T(8,128)S(1)}, u32[]{:S(2)}, u32[]{:S(2)}) collective-permute-start(f32[126,8,128]{2,1,0:T(8,128)S(1)} %get-tuple-element.42), channel_id=1, source_target_pairs={{0,4},{4,8},{8,12},{12,16},{16,20},{20,24},{24,28},{28,0},{1,5},{5... | collective-permute-start | bytes 1548296 | tf_op jit(solution)/shard_map/ppermute | solution.py:525
  32.0 1.4 %collective-permute-start.7 = (f32[2,8,128]{2,1,0:T(8,128)S(1)}, f32[2,8,128]{2,1,0:T(8,128)S(1)}, u32[]{:S(2)}, u32[]{:S(2)}) collective-permute-start(f32[2,8,128]{2,1,0:T(8,128)S(1)} %own.1.refs_6_), channel_id=1, source_target_pairs={{0,4},{4,0},{8,12},{12,8},{16,20},{20,16},{24,28},{28,24},{1,5},{5... | collective-permute-start | bytes 24584 | tf_op jit(solution)/shard_map/ppermute | solution.py:560
  33.4 5.0 %collective-permute-start.8 = (f32[2,8,128]{2,1,0:T(8,128)S(1)}, f32[2,8,128]{2,1,0:T(8,128)S(1)}, u32[]{:S(2)}, u32[]{:S(2)}) collective-permute-start(f32[2,8,128]{2,1,0:T(8,128)S(1)} %pad_maximum_fusion.3.refs_4_), channel_id=1, source_target_pairs={{0,8},{4,12},{8,0},{12,4},{16,24},{20,28},{24,16},{28,20},{1,9},{5... | collective-permute-start | bytes 24584 | tf_op jit(solution)/shard_map/ppermute | solution.py:560
  38.5 5.2 %collective-permute-start.9 = (f32[2,8,128]{2,1,0:T(8,128)S(1)}, f32[2,8,128]{2,1,0:T(8,128)S(1)}, u32[]{:S(2)}, u32[]{:S(2)}) collective-permute-start(f32[2,8,128]{2,1,0:T(8,128)S(1)} %pad_maximum_fusion.4.refs_4_), channel_id=1, source_target_pairs={{0,16},{4,20},{8,24},{12,28},{16,0},{20,4},{24,8},{28,12},{1,17},{... | collective-permute-start | bytes 24584 | tf_op jit(solution)/shard_map/ppermute | solution.py:560
  43.8 3.7 %collective-permute-start.10 = (f32[2,8,128]{2,1,0:T(8,128)S(1)}, f32[2,8,128]{2,1,0:T(8,128)S(1)}, u32[]{:S(2)}, u32[]{:S(2)}) collective-permute-start(f32[2,8,128]{2,1,0:T(8,128)S(1)} %pad_maximum_fusion.5.refs_4_), channel_id=1, source_target_pairs={{0,32},{32,0},{64,96},{96,64},{128,160},{160,128},{192,224},{224,1... | collective-permute-start | bytes 24584 | tf_op jit(solution)/shard_map/ppermute | solution.py:560
  47.5 5.0 %collective-permute-start.11 = (f32[2,8,128]{2,1,0:T(8,128)S(1)}, f32[2,8,128]{2,1,0:T(8,128)S(1)}, u32[]{:S(2)}, u32[]{:S(2)}) collective-permute-start(f32[2,8,128]{2,1,0:T(8,128)S(1)} %pad_maximum_fusion.6.refs_4_), channel_id=1, source_target_pairs={{0,64},{32,96},{64,0},{96,32},{128,192},{160,224},{192,128},{224,1... | collective-permute-start | bytes 24584 | tf_op jit(solution)/shard_map/ppermute | solution.py:560
  52.6 7.6 %collective-permute-start.12 = (f32[2,8,128]{2,1,0:T(8,128)S(1)}, f32[2,8,128]{2,1,0:T(8,128)S(1)}, u32[]{:S(2)}, u32[]{:S(2)}) collective-permute-start(f32[2,8,128]{2,1,0:T(8,128)S(1)} %pad_maximum_fusion.7.refs_4_), channel_id=1, source_target_pairs={{0,128},{32,160},{64,192},{96,224},{128,0},{160,32},{192,64},{224,... | collective-permute-start | bytes 24584 | tf_op jit(solution)/shard_map/ppermute | solution.py:560
  60.3 4.1 %collective-permute-start.13 = (f32[2,8,128]{2,1,0:T(8,128)S(1)}, f32[2,8,128]{2,1,0:T(8,128)S(1)}, u32[]{:S(2)}, u32[]{:S(2)}) collective-permute-start(f32[2,8,128]{2,1,0:T(8,128)S(1)} %pad_maximum_fusion.8.refs_4_), channel_id=1, source_target_pairs={{0,1},{1,0},{2,3},{3,2},{4,5},{5,4},{6,7},{7,6},{8,9},{9,8},{10,11... | collective-permute-start | bytes 24584 | tf_op jit(solution)/shard_map/ppermute | solution.py:560
  64.4 5.2 %collective-permute-start.14 = (f32[2,8,128]{2,1,0:T(8,128)S(1)}, f32[2,8,128]{2,1,0:T(8,128)S(1)}, u32[]{:S(2)}, u32[]{:S(2)}) collective-permute-start(f32[2,8,128]{2,1,0:T(8,128)S(1)} %pad_maximum_fusion.9.refs_4_), channel_id=1, source_target_pairs={{0,2},{1,3},{2,0},{3,1},{4,6},{5,7},{6,4},{7,5},{8,10},{9,11},{10,... | collective-permute-start | bytes 24584 | tf_op jit(solution)/shard_map/ppermute | solution.py:560

commit v7 on v6

--- a/solution.py
+++ b/solution.py
@@ -551,7 +551,7 @@
     up, down = kernel_call(pack_y, [(126, 8, 128), (141, 8, 128)], "pack_y")(mid, low, high, far)
     below, above = passed(up, "gy", 1), passed(down, "gy", -1)
     (known,) = kernel_call(own_kernel, [(2, 8, 128)], "own")(mid, high, above, below)
-    rounds = iter([("gy", 1), ("gy", 2), ("gy", 4), ("gx", 1), ("gx", 2), ("gx", 4), ("gz", 1), ("gz", 2)])
+    rounds = iter([("gy", 1), ("gx", 4), ("gx", 2), ("gx", 1), ("gy", 4), ("gy", 2), ("gz", 2), ("gz", 1)])
 
     def under(body, outs, name, scratch, aliases=None):
         def run(*args):

time: 72.3 us -> 71.4 us (0.988)
  starting transfers between devices: 25.8 us -> 24.9 us
    ppermute x8, starting transfers between devices: 13.6 us -> 12.7 us  [run(): lax.ppermute(known, axis, [(i, i ^ hop) for i in range(lax.axis_size(axis...]
  transfers between devices with their start and end apart: 15 -> 15, of which waited for: 9 -> 8; matrix products, arithmetic and copies ran while one was open for 0% -> 0% of each run, Pallas kernels for 28% -> 29%
where the time goes in v7:
time: 71.4 us; the launch traced here: 71.2 us
  starting transfers between devices  24.9 us (35%)
  Pallas kernels  23.9 us (33%)
  waiting for transfers between devices  20.4 us (29%)
  other arithmetic  1.14 us (2%)
  between operations  0.84 us (1%)
    pallas_call x12, Pallas kernels, run(): pl.pallas_call(body, out_shape=[tile(shape) for shape in outs], in_specs=...  23.9 us
    ppermute x7, waiting for transfers between devices, passed(): lax.ppermute(block, axis, [(i, (i + distance) % count) for i in range(cou...  17.1 us
    ppermute x8, starting transfers between devices, run(): lax.ppermute(known, axis, [(i, i ^ hop) for i in range(lax.axis_size(axis...  12.7 us
    ppermute x7, starting transfers between devices, passed(): lax.ppermute(block, axis, [(i, (i + distance) % count) for i in range(cou...  12.2 us
    ppermute x8, waiting for transfers between devices, run(): lax.ppermute(known, axis, [(i, i ^ hop) for i in range(lax.axis_size(axis...  3.27 us
  transfers between devices with their start and end apart: 15, of which 8 were waited for; matrix products, arithmetic and copies ran while one was open for 0% of the time, Pallas kernels for 29%

profile of v7, /device:TPU:2, one launch (start us, length us, event | category | flops | bytes accessed | tf_op | source)
XLA Modules:
  0.0 71.2 jit_solution(10105889023397476616)
XLA Ops:
  0.6 1.0 %pad_maximum_fusion.1.main = f32[64,8,128]{2,1,0:T(8,128)S(1)} fusion(f32[16,8,128]{2,1,0:T(8,128)} %bitcast.4, f32[48,8,128]{2,1,0:T(8,128)} %bitcast.3), kind=kLoop, calls=%fused_computation.1 | loop fusion | flops 65536 | bytes 524288 | tf_op jit(solution)/shard_map/concatenate | solution.py:543
  1.6 0.2 pack_z.1
  1.8 1.7 %collective-permute-start = (f32[16,8,128]{2,1,0:T(8,128)S(1)}, f32[16,8,128]{2,1,0:T(8,128)S(1)}, u32[]{:S(2)}, u32[]{:S(2)}) collective-permute-start(f32[16,8,128]{2,1,0:T(8,128)S(1)} %get-tuple-element.39), channel_id=1, source_target_pairs={{0,1},{1,2},{2,3},{3,0},{4,5},{5,6},{6,7},{7,4},{8,9},{9,10},{10,1... | collective-permute-start | bytes 196616 | tf_op jit(solution)/shard_map/ppermute | solution.py:525
  3.5 1.7 %collective-permute-start.1 = (f32[16,8,128]{2,1,0:T(8,128)S(1)}, f32[16,8,128]{2,1,0:T(8,128)S(1)}, u32[]{:S(2)}, u32[]{:S(2)}) collective-permute-start(f32[16,8,128]{2,1,0:T(8,128)S(1)} %get-tuple-element.40), channel_id=1, source_target_pairs={{0,3},{1,0},{2,1},{3,2},{4,7},{5,4},{6,5},{7,6},{8,11},{9,8},{10,9... | collective-permute-start | bytes 196616 | tf_op jit(solution)/shard_map/ppermute | solution.py:525
  5.1 2.2 %collective-permute-done = f32[16,8,128]{2,1,0:T(8,128)S(1)} collective-permute-done((f32[16,8,128]{2,1,0:T(8,128)S(1)}, f32[16,8,128]{2,1,0:T(8,128)S(1)}, u32[]{:S(2)}, u32[]{:S(2)}) %collective-permute-start) | collective-permute-done | bytes 65568 | tf_op jit(solution)/shard_map/ppermute | solution.py:525
  7.4 0.4 collective-permute-done.1
  7.8 5.9 %collective-permute-start.3 = (f32[80,8,128]{2,1,0:T(8,128)S(1)}, f32[80,8,128]{2,1,0:T(8,128)S(1)}, u32[]{:S(2)}, u32[]{:S(2)}) collective-permute-start(f32[80,8,128]{2,1,0:T(8,128)S(1)} %pad_maximum_fusion.mid.refs_0_), channel_id=1, source_target_pairs={{0,224},{32,0},{64,32},{96,64},{128,96},{160,128},{192,160},{224,1... | collective-permute-start | bytes 983048 | tf_op jit(solution)/shard_map/ppermute | solution.py:525
  13.7 0.0 collective-permute-start.2
  13.7 2.5 %collective-permute-start.4 = (f32[9,8,128]{2,1,0:T(8,128)S(1)}, f32[9,8,128]{2,1,0:T(8,128)S(1)}, u32[]{:S(2)}, u32[]{:S(2)}) collective-permute-start(f32[9,8,128]{2,1,0:T(8,128)S(1)} %pad_maximum_fusion.2), channel_id=1, source_target_pairs={{0,192},{32,224},{64,0},{96,32},{128,64},{160,96},{192,128},{224,1... | collective-permute-start | bytes 110600 | tf_op jit(solution)/shard_map/ppermute | solution.py:525
  16.2 4.6 %collective-permute-done.4.far.refs_3_ = f32[9,8,128]{2,1,0:T(8,128)S(1)} collective-permute-done((f32[9,8,128]{2,1,0:T(8,128)S(1)}, f32[9,8,128]{2,1,0:T(8,128)S(1)}, u32[]{:S(2)}, u32[]{:S(2)}) %collective-permute-start.4) | collective-permute-done | bytes 36896 | tf_op jit(solution)/shard_map/ppermute | solution.py:525
  20.8 0.0 collective-permute-done.3.high.refs_2_
  20.9 1.8 %collective-permute-done.2.low.refs_1_ = f32[80,8,128]{2,1,0:T(8,128)S(1)} collective-permute-done((f32[80,8,128]{2,1,0:T(8,128)S(1)}, f32[80,8,128]{2,1,0:T(8,128)S(1)}, u32[]{:S(2)}, u32[]{:S(2)}) %collective-permute-start.2) | collective-permute-done | bytes 327712 | tf_op jit(solution)/shard_map/ppermute | solution.py:525
  22.7 0.2 pack_y.1
  22.9 0.0 collective-permute-start.6
  22.9 0.5 collective-permute-start.5
  23.4 8.0 %collective-permute-done.5.below.refs_4_ = f32[126,8,128]{2,1,0:T(8,128)S(1)} collective-permute-done((f32[126,8,128]{2,1,0:T(8,128)S(1)}, f32[126,8,128]{2,1,0:T(8,128)S(1)}, u32[]{:S(2)}, u32[]{:S(2)}) %collective-permute-start.5) | collective-permute-done | bytes 516128 | tf_op jit(solution)/shard_map/ppermute | solution.py:525
  31.4 0.0 collective-permute-done.6.above.refs_5_
  31.4 0.6 own.1.refs_6_
  32.0 0.6 collective-permute-start.7
  32.6 0.4 widen.1
  33.0 0.4 collective-permute-done.7
  33.4 2.1 %collective-permute-start.8 = (f32[2,8,128]{2,1,0:T(8,128)S(1)}, f32[2,8,128]{2,1,0:T(8,128)S(1)}, u32[]{:S(2)}, u32[]{:S(2)}) collective-permute-start(f32[2,8,128]{2,1,0:T(8,128)S(1)} %pad_maximum_fusion.3.refs_4_), channel_id=1, source_target_pairs={{0,128},{32,160},{64,192},{96,224},{128,0},{160,32},{192,64},{224,... | collective-permute-start | bytes 24584 | tf_op jit(solution)/shard_map/ppermute | solution.py:560
  35.6 3.4 %stress.1 = (f32[6,24,40,128]{3,2,1,0:T(8,128)S(1)}, f32[24,40,128]{2,1,0:T(8,128)S(1)}, f32[40,128]{1,0:T(8,128)S(1)}, f32[2,8,128]{2,1,0:T(8,128)S(1)}) custom-call(f32[3,25,40,128]{3,2,1,0:T(8,128)S(1)} %get-tuple-element.44.refs_0_, f32[3,25,8,128]{3,2,1,0:T(8,128)S(1)} %get-tuple-element.45.refs_1_, f32[3,25,8,128]{3,2,1,0:T(8,128)S(1)} %get-tuple-element.46.refs_2_, ...), custom_call_target="tpu_custom_call" | custom-call | flops 20000000 | bytes 1000000 | tf_op jit(solution)/shard_map/stress/pallas_call | solution.py:40
  38.9 2.1 %collective-permute-done.8 = f32[2,8,128]{2,1,0:T(8,128)S(1)} collective-permute-done((f32[2,8,128]{2,1,0:T(8,128)S(1)}, f32[2,8,128]{2,1,0:T(8,128)S(1)}, u32[]{:S(2)}, u32[]{:S(2)}) %collective-permute-start.8) | collective-permute-done | bytes 8224 | tf_op jit(solution)/shard_map/ppermute | solution.py:560
  41.1 1.0 %collective-permute-start.9 = (f32[2,8,128]{2,1,0:T(8,128)S(1)}, f32[2,8,128]{2,1,0:T(8,128)S(1)}, u32[]{:S(2)}, u32[]{:S(2)}) collective-permute-start(f32[2,8,128]{2,1,0:T(8,128)S(1)} %pad_maximum_fusion.4.refs_4_), channel_id=1, source_target_pairs={{0,64},{32,96},{64,0},{96,32},{128,192},{160,224},{192,128},{224,1... | collective-permute-start | bytes 24584 | tf_op jit(solution)/shard_map/ppermute | solution.py:560
  42.1 2.9 %load.1 = (f32[3,24,40,128]{3,2,1,0:T(8,128)S(1)}, f32[24,40,128]{2,1,0:T(8,128)S(1)}, f32[24,40,128]{2,1,0:T(8,128)S(1)}, f32[24,40,128]{2,1,0:T(8,128)S(1)}, f...) custom-call(f32[6,24,40,128]{3,2,1,0:T(8,128)S(1)} %get-tuple-element.49.refs_0_.base, ...), custom_call_target="tpu_custom_call" | custom-call | flops 20000000 | bytes 1000000 | tf_op jit(solution)/shard_map/load/pallas_call | solution.py:40
  45.0 0.7 %collective-permute-done.9 = f32[2,8,128]{2,1,0:T(8,128)S(1)} collective-permute-done((f32[2,8,128]{2,1,0:T(8,128)S(1)}, f32[2,8,128]{2,1,0:T(8,128)S(1)}, u32[]{:S(2)}, u32[]{:S(2)}) %collective-permute-start.9) | collective-permute-done | bytes 8224 | tf_op jit(solution)/shard_map/ppermute | solution.py:560
  45.7 0.6 collective-permute-start.10
  46.3 3.2 %sweep1.1 = (f32[3,25,40,128]{3,2,1,0:T(8,128)S(1)}, f32[2,8,128]{2,1,0:T(8,128)S(1)}) custom-call(f32[3,25,40,128]{3,2,1,0:T(8,128)S(1)} %get-tuple-element.53.refs_0_, f32[3,24,40,128]{3,2,1,0:T(8,128)S(1)} %get-tuple-element.54.refs_1_, f32[24,40,128]{2,1,0:T(8,128)S(1)} %get-tuple-element.55.refs_2_, ...), custom_call_target="tpu_custom_call", output_to_operand_aliasing={{0}: (0, {})} | custom-call | flops 20000000 | bytes 1000000 | tf_op jit(solution)/shard_map/sweep1/pallas_call | solution.py:40
  49.5 0.0 collective-permute-done.10
  49.6 2.1 %collective-permute-start.11 = (f32[2,8,128]{2,1,0:T(8,128)S(1)}, f32[2,8,128]{2,1,0:T(8,128)S(1)}, u32[]{:S(2)}, u32[]{:S(2)}) collective-permute-start(f32[2,8,128]{2,1,0:T(8,128)S(1)} %pad_maximum_fusion.6.refs_4_), channel_id=1, source_target_pairs={{0,16},{4,20},{8,24},{12,28},{16,0},{20,4},{24,8},{28,12},{1,17},{... | collective-permute-start | bytes 24584 | tf_op jit(solution)/shard_map/ppermute | solution.py:560
  51.6 3.2 %sweep2.1 = (f32[3,25,40,128]{3,2,1,0:T(8,128)S(1)}, f32[2,8,128]{2,1,0:T(8,128)S(1)}) custom-call(f32[3,25,40,128]{3,2,1,0:T(8,128)S(1)} %get-tuple-element.58.refs_0_, f32[3,24,40,128]{3,2,1,0:T(8,128)S(1)} %get-tuple-element.54.refs_1_, f32[24,40,128]{2,1,0:T(8,128)S(1)} %get-tuple-element.55.refs_2_, ...), custom_call_target="tpu_custom_call", output_to_operand_aliasing={{0}: (0, {})} | custom-call | flops 20000000 | bytes 1000000 | tf_op jit(solution)/shard_map/sweep2/pallas_call | solution.py:40
  54.8 0.0 collective-permute-done.11
  54.9 1.6 %collective-permute-start.12 = (f32[2,8,128]{2,1,0:T(8,128)S(1)}, f32[2,8,128]{2,1,0:T(8,128)S(1)}, u32[]{:S(2)}, u32[]{:S(2)}) collective-permute-start(f32[2,8,128]{2,1,0:T(8,128)S(1)} %pad_maximum_fusion.7.refs_4_), channel_id=1, source_target_pairs={{0,8},{4,12},{8,0},{12,4},{16,24},{20,28},{24,16},{28,20},{1,9},{5... | collective-permute-start | bytes 24584 | tf_op jit(solution)/shard_map/ppermute | solution.py:560
  56.5 2.8 %sweep3.1 = (f32[3,25,40,128]{3,2,1,0:T(8,128)S(1)}, f32[2,8,128]{2,1,0:T(8,128)S(1)}) custom-call(f32[3,25,40,128]{3,2,1,0:T(8,128)S(1)} %get-tuple-element.60.refs_0_, f32[3,24,40,128]{3,2,1,0:T(8,128)S(1)} %get-tuple-element.54.refs_1_, f32[24,40,128]{2,1,0:T(8,128)S(1)} %get-tuple-element.55.refs_2_, ...), custom_call_target="tpu_custom_call", output_to_operand_aliasing={{0}: (0, {})} | custom-call | flops 20000000 | bytes 1000000 | tf_op jit(solution)/shard_map/sweep3/pallas_call | solution.py:40
  59.3 0.0 collective-permute-done.12
  59.3 3.3 %collective-permute-start.13 = (f32[2,8,128]{2,1,0:T(8,128)S(1)}, f32[2,8,128]{2,1,0:T(8,128)S(1)}, u32[]{:S(2)}, u32[]{:S(2)}) collective-permute-start(f32[2,8,128]{2,1,0:T(8,128)S(1)} %pad_maximum_fusion.8.refs_4_), channel_id=1, source_target_pairs={{0,2},{1,3},{2,0},{3,1},{4,6},{5,7},{6,4},{7,5},{8,10},{9,11},{10,... | collective-permute-start | bytes 24584 | tf_op jit(solution)/shard_map/ppermute | solution.py:560
  62.6 2.3 %sweep4.1 = (f32[3,25,40,128]{3,2,1,0:T(8,128)S(1)}, f32[2,8,128]{2,1,0:T(8,128)S(1)}) custom-call(f32[3,25,40,128]{3,2,1,0:T(8,128)S(1)} %get-tuple-element.62.refs_0_, f32[3,24,40,128]{3,2,1,0:T(8,128)S(1)} %get-tuple-element.54.refs_1_, f32[24,40,128]{2,1,0:T(8,128)S(1)} %get-tuple-element.55.refs_2_, ...), custom_call_target="tpu_custom_call", output_to_operand_aliasing={{0}: (0, {})} | custom-call | flops 20000000 | bytes 1000000 | tf_op jit(solution)/shard_map/sweep4/pallas_call | solution.py:40
  64.9 0.0 collective-permute-done.13
  65.0 1.4 %collective-permute-start.14 = (f32[2,8,128]{2,1,0:T(8,128)S(1)}, f32[2,8,128]{2,1,0:T(8,128)S(1)}, u32[]{:S(2)}, u32[]{:S(2)}) collective-permute-start(f32[2,8,128]{2,1,0:T(8,128)S(1)} %pad_maximum_fusion.9.refs_4_), channel_id=1, source_target_pairs={{0,1},{1,0},{2,3},{3,2},{4,5},{5,4},{6,7},{7,6},{8,9},{9,8},{10,11... | collective-permute-start | bytes 24584 | tf_op jit(solution)/shard_map/ppermute | solution.py:560
  66.3 2.3 %sweep5.1 = (f32[3,25,40,128]{3,2,1,0:T(8,128)S(1)}, f32[2,8,128]{2,1,0:T(8,128)S(1)}) custom-call(f32[3,25,40,128]{3,2,1,0:T(8,128)S(1)} %get-tuple-element.64.refs_0_, f32[3,24,40,128]{3,2,1,0:T(8,128)S(1)} %get-tuple-element.54.refs_1_, f32[24,40,128]{2,1,0:T(8,128)S(1)} %get-tuple-element.55.refs_2_, ...), custom_call_target="tpu_custom_call", output_to_operand_aliasing={{0}: (0, {})} | custom-call | flops 20000000 | bytes 1000000 | tf_op jit(solution)/shard_map/sweep5/pallas_call | solution.py:40
  68.7 0.0 collective-permute-done.14
  68.7 2.5 %final.1 = (f32[3,8,16,128]{3,2,1,0:T(8,128)}, f32[8,16,128]{2,1,0:T(8,128)}, f32[1,1]{1,0:T(1,128)}) custom-call(f32[3,25,40,128]{3,2,1,0:T(8,128)S(1)} %get-tuple-element.66.field, f32[24,40,128]{2,1,0:T(8,128)S(1)} %get-tuple-element.67.explicit, f32[6,24,40,128]{3,2,1,0:T(8,128)S(1)} %get-tuple-element.49.refs_0_.base, ...), custom_call_target="tpu_custom_call" | custom-call | flops 1000000 | bytes 1000000 | tf_op jit(solution)/shard_map/final/pallas_call | solution.py:40
  (20 shorter events, 0.2 us)
Async XLA Ops:
  1.8 5.6 %collective-permute-start = (f32[16,8,128]{2,1,0:T(8,128)S(1)}, f32[16,8,128]{2,1,0:T(8,128)S(1)}, u32[]{:S(2)}, u32[]{:S(2)}) collective-permute-start(f32[16,8,128]{2,1,0:T(8,128)S(1)} %get-tuple-element.39), channel_id=1, source_target_pairs={{0,1},{1,2},{2,3},{3,0},{4,5},{5,6},{6,7},{7,4},{8,9},{9,10},{10,1... | collective-permute-start | bytes 196616 | tf_op jit(solution)/shard_map/ppermute | solution.py:525
  3.5 4.3 %collective-permute-start.1 = (f32[16,8,128]{2,1,0:T(8,128)S(1)}, f32[16,8,128]{2,1,0:T(8,128)S(1)}, u32[]{:S(2)}, u32[]{:S(2)}) collective-permute-start(f32[16,8,128]{2,1,0:T(8,128)S(1)} %get-tuple-element.40), channel_id=1, source_target_pairs={{0,3},{1,0},{2,1},{3,2},{4,7},{5,4},{6,5},{7,6},{8,11},{9,8},{10,9... | collective-permute-start | bytes 196616 | tf_op jit(solution)/shard_map/ppermute | solution.py:525
  7.8 13.1 %collective-permute-start.3 = (f32[80,8,128]{2,1,0:T(8,128)S(1)}, f32[80,8,128]{2,1,0:T(8,128)S(1)}, u32[]{:S(2)}, u32[]{:S(2)}) collective-permute-start(f32[80,8,128]{2,1,0:T(8,128)S(1)} %pad_maximum_fusion.mid.refs_0_), channel_id=1, source_target_pairs={{0,224},{32,0},{64,32},{96,64},{128,96},{160,128},{192,160},{224,1... | collective-permute-start | bytes 983048 | tf_op jit(solution)/shard_map/ppermute | solution.py:525
  13.7 9.0 %collective-permute-start.2 = (f32[80,8,128]{2,1,0:T(8,128)S(1)}, f32[80,8,128]{2,1,0:T(8,128)S(1)}, u32[]{:S(2)}, u32[]{:S(2)}) collective-permute-start(f32[80,8,128]{2,1,0:T(8,128)S(1)} %pad_maximum_fusion.mid.refs_0_), channel_id=1, source_target_pairs={{0,32},{32,64},{64,96},{96,128},{128,160},{160,192},{192,224},{224... | collective-permute-start | bytes 983048 | tf_op jit(solution)/shard_map/ppermute | solution.py:525
  13.7 7.1 %collective-permute-start.4 = (f32[9,8,128]{2,1,0:T(8,128)S(1)}, f32[9,8,128]{2,1,0:T(8,128)S(1)}, u32[]{:S(2)}, u32[]{:S(2)}) collective-permute-start(f32[9,8,128]{2,1,0:T(8,128)S(1)} %pad_maximum_fusion.2), channel_id=1, source_target_pairs={{0,192},{32,224},{64,0},{96,32},{128,64},{160,96},{192,128},{224,1... | collective-permute-start | bytes 110600 | tf_op jit(solution)/shard_map/ppermute | solution.py:525
  22.9 8.6 %collective-permute-start.6 = (f32[141,8,128]{2,1,0:T(8,128)S(1)}, f32[141,8,128]{2,1,0:T(8,128)S(1)}, u32[]{:S(2)}, u32[]{:S(2)}) collective-permute-start(f32[141,8,128]{2,1,0:T(8,128)S(1)} %get-tuple-element.43), channel_id=1, source_target_pairs={{0,28},{4,0},{8,4},{12,8},{16,12},{20,16},{24,20},{28,24},{1,29},{... | collective-permute-start | bytes 1732616 | tf_op jit(solution)/shard_map/ppermute | solution.py:525
  22.9 8.5 %collective-permute-start.5 = (f32[126,8,128]{2,1,0:T(8,128)S(1)}, f32[126,8,128]{2,1,0:T(8,128)S(1)}, u32[]{:S(2)}, u32[]{:S(2)}) collective-permute-start(f32[126,8,128]{2,1,0:T(8,128)S(1)} %get-tuple-element.42), channel_id=1, source_target_pairs={{0,4},{4,8},{8,12},{12,16},{16,20},{20,24},{24,28},{28,0},{1,5},{5... | collective-permute-start | bytes 1548296 | tf_op jit(solution)/shard_map/ppermute | solution.py:525
  32.0 1.4 %collective-permute-start.7 = (f32[2,8,128]{2,1,0:T(8,128)S(1)}, f32[2,8,128]{2,1,0:T(8,128)S(1)}, u32[]{:S(2)}, u32[]{:S(2)}) collective-permute-start(f32[2,8,128]{2,1,0:T(8,128)S(1)} %own.1.refs_6_), channel_id=1, source_target_pairs={{0,4},{4,0},{8,12},{12,8},{16,20},{20,16},{24,28},{28,24},{1,5},{5... | collective-permute-start | bytes 24584 | tf_op jit(solution)/shard_map/ppermute | solution.py:560
  33.4 7.6 %collective-permute-start.8 = (f32[2,8,128]{2,1,0:T(8,128)S(1)}, f32[2,8,128]{2,1,0:T(8,128)S(1)}, u32[]{:S(2)}, u32[]{:S(2)}) collective-permute-start(f32[2,8,128]{2,1,0:T(8,128)S(1)} %pad_maximum_fusion.3.refs_4_), channel_id=1, source_target_pairs={{0,128},{32,160},{64,192},{96,224},{128,0},{160,32},{192,64},{224,... | collective-permute-start | bytes 24584 | tf_op jit(solution)/shard_map/ppermute | solution.py:560
  41.1 4.6 %collective-permute-start.9 = (f32[2,8,128]{2,1,0:T(8,128)S(1)}, f32[2,8,128]{2,1,0:T(8,128)S(1)}, u32[]{:S(2)}, u32[]{:S(2)}) collective-permute-start(f32[2,8,128]{2,1,0:T(8,128)S(1)} %pad_maximum_fusion.4.refs_4_), channel_id=1, source_target_pairs={{0,64},{32,96},{64,0},{96,32},{128,192},{160,224},{192,128},{224,1... | collective-permute-start | bytes 24584 | tf_op jit(solution)/shard_map/ppermute | solution.py:560
  45.7 3.8 %collective-permute-start.10 = (f32[2,8,128]{2,1,0:T(8,128)S(1)}, f32[2,8,128]{2,1,0:T(8,128)S(1)}, u32[]{:S(2)}, u32[]{:S(2)}) collective-permute-start(f32[2,8,128]{2,1,0:T(8,128)S(1)} %pad_maximum_fusion.5.refs_4_), channel_id=1, source_target_pairs={{0,32},{32,0},{64,96},{96,64},{128,160},{160,128},{192,224},{224,1... | collective-permute-start | bytes 24584 | tf_op jit(solution)/shard_map/ppermute | solution.py:560
  49.6 5.3 %collective-permute-start.11 = (f32[2,8,128]{2,1,0:T(8,128)S(1)}, f32[2,8,128]{2,1,0:T(8,128)S(1)}, u32[]{:S(2)}, u32[]{:S(2)}) collective-permute-start(f32[2,8,128]{2,1,0:T(8,128)S(1)} %pad_maximum_fusion.6.refs_4_), channel_id=1, source_target_pairs={{0,16},{4,20},{8,24},{12,28},{16,0},{20,4},{24,8},{28,12},{1,17},{... | collective-permute-start | bytes 24584 | tf_op jit(solution)/shard_map/ppermute | solution.py:560
  54.9 4.4 %collective-permute-start.12 = (f32[2,8,128]{2,1,0:T(8,128)S(1)}, f32[2,8,128]{2,1,0:T(8,128)S(1)}, u32[]{:S(2)}, u32[]{:S(2)}) collective-permute-start(f32[2,8,128]{2,1,0:T(8,128)S(1)} %pad_maximum_fusion.7.refs_4_), channel_id=1, source_target_pairs={{0,8},{4,12},{8,0},{12,4},{16,24},{20,28},{24,16},{28,20},{1,9},{5... | collective-permute-start | bytes 24584 | tf_op jit(solution)/shard_map/ppermute | solution.py:560
  59.3 5.6 %collective-permute-start.13 = (f32[2,8,128]{2,1,0:T(8,128)S(1)}, f32[2,8,128]{2,1,0:T(8,128)S(1)}, u32[]{:S(2)}, u32[]{:S(2)}) collective-permute-start(f32[2,8,128]{2,1,0:T(8,128)S(1)} %pad_maximum_fusion.8.refs_4_), channel_id=1, source_target_pairs={{0,2},{1,3},{2,0},{3,1},{4,6},{5,7},{6,4},{7,5},{8,10},{9,11},{10,... | collective-permute-start | bytes 24584 | tf_op jit(solution)/shard_map/ppermute | solution.py:560
  65.0 3.7 %collective-permute-start.14 = (f32[2,8,128]{2,1,0:T(8,128)S(1)}, f32[2,8,128]{2,1,0:T(8,128)S(1)}, u32[]{:S(2)}, u32[]{:S(2)}) collective-permute-start(f32[2,8,128]{2,1,0:T(8,128)S(1)} %pad_maximum_fusion.9.refs_4_), channel_id=1, source_target_pairs={{0,1},{1,0},{2,3},{3,2},{4,5},{5,4},{6,7},{7,6},{8,9},{9,8},{10,11... | collective-permute-start | bytes 24584 | tf_op jit(solution)/shard_map/ppermute | solution.py:560
